TPU v7x, 128 devices: a whole 4x4x4 slice. The times are simulated.
128 devices in a mesh: dom: 32 (over x, y, core), grp: 4 (over z).
Axes of the slice: x: 4, y: 4, z: 4, core: 2. Of those that a mesh axis runs over, the one named last changes fastest.
Arguments:
- features: bfloat16 [262144, 256], P(('dom', 'grp')), may hold values from -6 to 6
- edge_src: int32 [2097152], P(('dom', 'grp')), may hold values from 0 to 3071, as said below
- edge_dst: int32 [2097152], P(('dom', 'grp')), may hold values from 0 to 2047, as said below
- edge_count: int32 [128], P(('dom', 'grp')), may hold values from 4096 to 16384, as said below
- halo_index: int32 [128, 128, 8], P(('dom', 'grp')), may hold values from 0 to 2047
- request_rows: int32 [128, 128, 16], P(('dom', 'grp')), may hold values from 0 to 2047, as said below
- pair_ends: int32 [262144, 2], P(('dom', 'grp')), may hold values from 0 to 2047
- labels: int32 [262144], P(('dom', 'grp')), may hold values 0 or 1
- pair_weight: float32 [262144], P(('dom', 'grp')), may hold values from 0.25 to 4
- w_self: bfloat16 [256, 256], replicated, may hold values from -0.375 to 0.375
- w_neigh: bfloat16 [256, 256], replicated, may hold values from -0.375 to 0.375
- w_hidden: bfloat16 [512, 256], replicated, may hold values from -0.25 to 0.25
- b_hidden: float32 [256], replicated, may hold values from -3 to 3
- w_out: float32 [256], replicated, may hold values from -0.375 to 0.375
Outputs:
- logits: float32 [262144], P(('dom', 'grp'))
- grad_features: float32 [262144, 256], P(('dom', 'grp'))
- grad_w_self: float32 [256, 256], replicated
- grad_w_neigh: float32 [256, 256], replicated
- grad_w_hidden: float32 [512, 256], replicated
- grad_b_hidden: float32 [256], replicated
- grad_w_out: float32 [256], replicated
Inputs may be any that keep to these rules, and one draw needn't show every extreme that they name: `edge_src`: a row of the partition's own table. `edge_dst`: a local node of the partition; slots at or past edge_count are not live and hold arbitrary values. `edge_count`: some partition has exactly 16384 live slots. `halo_index`: local rows of the sending partition; 8 to every partition, itself included. `request_rows`: local rows of the owning partition, distinct and increasing within each list of 16. `pair_ends`: rows of the shard's own received rows.
All inputs are finite; a program needn't handle non-finite values. No bound on the sum of `labels` on one device may be relied on, other than what follows from the above.
Results may differ from a plain program's by a relative error of at most 0.02.
The roundings to bfloat16 on the way count: a program that leaves them out, or rounds other values in their place, can miss the bound.
Values may be sent and summed in bfloat16 or wider, within the bound.
A program may use at most 192 MiB of HBM per device.

v0:
```python
import jax
import jax.numpy as jnp
from jax import lax
from jax.sharding import PartitionSpec as P


def in_one(arrays, axis):
    vector, at, outs = (jnp.concatenate([a.reshape(-1) for a in arrays]), 0, [])
    total = lax.psum(vector, axis)
    for a in arrays:
        outs.append(total[at : at + a.size].reshape(a.shape))
        at += a.size
    return tuple(outs)


def contract_rows(left, right):
    return lax.dot_general(
        left, right, (((0,), (0,)), ((), ())), preferred_element_type=jnp.float32
    )


def per_device(
    features,
    edge_src,
    edge_dst,
    edge_count,
    halo_index,
    request_rows,
    pair_ends,
    labels,
    pair_weight,
    w_self,
    w_neigh,
    w_hidden,
    b_hidden,
    w_out,
):
    node_rows, feat_width = features.shape
    dom_count = lax.axis_size("dom")
    grp_count = lax.axis_size("grp")
    peer_count = dom_count * grp_count
    halo_len = halo_index.shape[2]
    outgoing = features[halo_index[0]]
    arrived = lax.all_to_all(outgoing, ("dom", "grp"), split_axis=0, concat_axis=0, tiled=True)
    row_table = jnp.concatenate(
        [features, arrived.reshape(peer_count * halo_len, feat_width)], axis=0
    )
    table_rows = row_table.shape[0]
    slot_total = edge_src.shape[0]
    alive_slot = jnp.arange(slot_total, dtype=jnp.int32) < edge_count[0]
    dst_index = jnp.where(alive_slot, edge_dst, node_rows)
    adjacency = (
        jnp.zeros((node_rows + 1, table_rows), jnp.float32)
        .at[dst_index, edge_src]
        .add(1.0)[:node_rows]
    )
    degree = jnp.sum(adjacency, axis=1)
    floor_deg = jnp.maximum(degree, 1.0)[:, None]
    agg_sums = jnp.dot(adjacency, row_table.astype(jnp.float32))
    aggregate = (agg_sums / floor_deg).astype(jnp.bfloat16)
    embedding = (
        jnp.dot(features, w_self, preferred_element_type=jnp.float32)
        + jnp.dot(aggregate, w_neigh, preferred_element_type=jnp.float32)
    ).astype(jnp.bfloat16)
    wanted = lax.all_to_all(
        request_rows[0], ("dom", "grp"), split_axis=0, concat_axis=0, tiled=True
    )
    req_len = wanted.shape[1]
    served = embedding[wanted]
    received = lax.all_to_all(served, ("dom", "grp"), split_axis=0, concat_axis=0, tiled=True)
    recv_rows = peer_count * req_len
    received = received.reshape(recv_rows, feat_width)
    slot_ids = jnp.arange(recv_rows, dtype=jnp.int32)[None, :]
    select_left = (pair_ends[:, 0][:, None] == slot_ids).astype(jnp.float32)
    select_right = (pair_ends[:, 1][:, None] == slot_ids).astype(jnp.float32)
    left_rows = jnp.dot(
        select_left.astype(jnp.bfloat16), received, preferred_element_type=jnp.float32
    ).astype(jnp.bfloat16)
    right_rows = jnp.dot(
        select_right.astype(jnp.bfloat16), received, preferred_element_type=jnp.float32
    ).astype(jnp.bfloat16)
    pair_input = jnp.concatenate([left_rows, right_rows], axis=1)
    pre_act = jnp.dot(pair_input, w_hidden, preferred_element_type=jnp.float32) + b_hidden
    hidden = jnp.maximum(pre_act, 0.0)
    logits = jnp.dot(hidden, w_out)
    slope_term = pair_weight * (jax.nn.sigmoid(logits) - labels.astype(jnp.float32))
    grad_out = jnp.dot(slope_term, hidden)
    delta_act = jnp.where(pre_act > 0, slope_term[:, None] * w_out[None, :], 0.0)
    grad_bias = jnp.sum(delta_act, axis=0)
    delta_b = delta_act.astype(jnp.bfloat16)
    grad_hidden = jnp.dot(pair_input.T, delta_b, preferred_element_type=jnp.float32)
    pair_grad = jnp.dot(delta_b, w_hidden.T, preferred_element_type=jnp.float32)
    received_grad = contract_rows(select_left, pair_grad[:, :feat_width]) + contract_rows(
        select_right, pair_grad[:, feat_width:]
    )
    received_grad_b = received_grad.astype(jnp.bfloat16)
    back_rows = lax.all_to_all(
        received_grad_b.reshape(peer_count, req_len, feat_width),
        ("dom", "grp"),
        split_axis=0,
        concat_axis=0,
        tiled=True,
    )
    embedding_grad = (
        jnp.zeros((node_rows, feat_width), jnp.float32)
        .at[wanted.reshape(recv_rows)]
        .add(back_rows.reshape(recv_rows, feat_width).astype(jnp.float32))
    )
    grad_b = embedding_grad.astype(jnp.bfloat16)
    grad_self = jnp.dot(features.T, grad_b, preferred_element_type=jnp.float32)
    grad_neigh = jnp.dot(aggregate.T, grad_b, preferred_element_type=jnp.float32)
    direct = jnp.dot(grad_b, w_self.T, preferred_element_type=jnp.float32)
    agg_grad = jnp.dot(grad_b, w_neigh.T, preferred_element_type=jnp.float32) / floor_deg
    table_grad = contract_rows(adjacency, agg_grad)
    returned = table_grad[node_rows:].reshape(peer_count, halo_len, feat_width)
    halo_back = lax.all_to_all(
        returned.astype(jnp.bfloat16), ("dom", "grp"), split_axis=0, concat_axis=0, tiled=True
    ).astype(returned.dtype)
    grad_features = (
        (direct + table_grad[:node_rows])
        .at[halo_index[0].reshape(peer_count * halo_len)]
        .add(halo_back.reshape(peer_count * halo_len, feat_width))
    )
    summed = in_one((grad_self, grad_neigh, grad_hidden, grad_bias, grad_out), ("dom", "grp"))
    return (logits, grad_features, summed[0], summed[1], summed[2], summed[3], summed[4])


def solution(mesh):
    in_specs = (
        P(("dom", "grp"), None),
        P(("dom", "grp")),
        P(("dom", "grp")),
        P(("dom", "grp")),
        P(("dom", "grp"), None, None),
        P(("dom", "grp"), None, None),
        P(("dom", "grp"), None),
        P(("dom", "grp")),
        P(("dom", "grp")),
        P(),
        P(),
        P(),
        P(),
        P(),
    )
    out_specs = (P(("dom", "grp")), P(("dom", "grp"), None), P(), P(), P(), P(), P())
    return jax.shard_map(
        per_device, mesh=mesh, in_specs=in_specs, out_specs=out_specs, check_vma=False
    )
```

profile of v0, /device:TPU:1, one launch (start us, length us, event | category | flops | bytes accessed | tf_op | source)
XLA Modules:
  0.0 484.6 jit_solution(14658335759810923802)
XLA Ops:
  7.2 1.5 copy.31
  8.7 11.5 %all-to-all-start.1 = ((s32[128,1,16]{2,1,0:T(1,128)}), s32[128,1,16]{2,1,0:T(1,128)S(1)}, u32[]{:S(2)}, u32[]{:S(2)}) async-start(s32[128,1,16]{2,1,0:T(1,128)} %bitcast.7), calls=%async_computation.1 | async-start | bytes 131072 | tf_op jit(solution)/shard_map/all_to_all | solution.py:65
  20.8 0.9 compare_select_fusion.1
  21.6 0.9 compare_select_fusion.2
  22.5 0.9 multiply_reduce_fusion
  23.4 1.0 and_reduce_fusion
  24.4 0.7 compare_select_fusion.5
  25.3 3.0 fusion.59
  28.3 95.7 %scatter_custom_fusion.2 = f32[6294528]{0:T(1024)} fusion(s32[16384]{0:T(1024)S(1)} %broadcast_select_fusion, f32[16384]{0:T(1024)S(1)} %broadcast.84, f32[]{:T(128)} %constant.6.clone.1), kind=kCustom, calls=%fused_computation.11 | custom fusion | flops 16384 | bytes 25178116
  124.0 16.7 %slice.87 = f32[6291456]{0:T(1024)} slice(f32[6294528]{0:T(1024)} %scatter_custom_fusion.2), slice={[0:6291456]} | slice | bytes 50331648 | tf_op jit(solution)/shard_map/slice | solution.py:53
  140.8 27.1 %reshape.208 = f32[2048,3072]{1,0:T(8,128)} reshape(f32[6291456]{0:T(1024)} %slice.87) | data formatting | bytes 50331648 | tf_op jit(solution)/shard_map/slice | solution.py:53
  167.9 9.2 %reduce_sum.18 = f32[2048]{0:T(1024)S(1)} reduce(f32[2048,3072]{1,0:T(8,128)} %reshape.208, f32[]{:T(128)} %constant.6.clone.1), dimensions={1}, to_apply=%region_1.2 | reduce | flops 6289408 | bytes 25174020 | tf_op jit(solution)/shard_map/reduce_sum | solution.py:57
  177.1 5.0 %gather_fusion = bf16[1024,256]{1,0:T(8,128)(2,1)} fusion(bf16[2048,256]{1,0:T(8,128)(2,1)S(1)} %copy-done.1, s32[1024]{0:T(1024)S(1)} %broadcast_clamp_fusion.1), kind=kCustom, calls=%fused_computation | custom fusion | bytes 1052672 | tf_op jit(solution)/shard_map/gather | solution.py:43
  182.1 10.1 %all-to-all-start = ((bf16[128,8,256]{2,1,0:T(8,128)(2,1)}), bf16[128,8,256]{2,1,0:T(8,128)(2,1)S(1)}, u32[]{:S(2)}, u32[]{:S(2)}) async-start(bf16[128,8,256]{2,1,0:T(8,128)(2,1)} %bitcast.5), calls=%async_computation | async-start | bytes 1048576 | tf_op jit(solution)/shard_map/all_to_all | solution.py:44
  192.3 13.7 %all-to-all-done = bf16[128,8,256]{2,1,0:T(8,128)(2,1)S(1)} async-done(((bf16[128,8,256]{2,1,0:T(8,128)(2,1)}), bf16[128,8,256]{2,1,0:T(8,128)(2,1)S(1)}, u32[]{:S(2)}, u32[]{:S(2)}) %all-to-all-start) | async-done | bytes 524320 | tf_op jit(solution)/shard_map/all_to_all | solution.py:44
  205.9 11.9 %fusion.15 = bf16[2048,256]{1,0:T(8,128)(2,1)S(1)} fusion(f32[2048,3072]{1,0:T(8,128)} %reshape.208, bf16[1024,256]{1,0:T(8,128)(2,1)S(1)} %bitcast.67, bf16[2048,256]{1,0:T(8,128)(2,1)S(1)} %copy-done.1, f32[2048]{0:T(1024)S(1)} %broadcast_maximum_fusion), kind=kOutput, calls=%fused_computation.29 | convolution fusion | flops 3225419776 | bytes 27795456 | tf_op jit(solution)/shard_map/dot_general | solution.py:59
  218.3 9.1 %gather_fusion.1 = bf16[2048,256]{1,0:T(8,128)(2,1)} fusion(bf16[2048,256]{1,0:T(8,128)(2,1)S(1)} %fusion.12, s32[2048]{0:T(1024)S(1)} %broadcast_clamp_fusion), kind=kCustom, calls=%fused_computation.1 | custom fusion | bytes 2105344 | tf_op jit(solution)/shard_map/gather | solution.py:69
  227.3 4.1 all-to-all-start.2
  231.5 19.5 %all-to-all-done.2 = bf16[128,16,256]{2,1,0:T(8,128)(2,1)S(1)} async-done(((bf16[128,16,256]{2,1,0:T(8,128)(2,1)}), bf16[128,16,256]{2,1,0:T(8,128)(2,1)S(1)}, u32[]{:S(2)}, u32[]{:S(2)}) %all-to-all-start.2) | async-done | bytes 1048608 | tf_op jit(solution)/shard_map/all_to_all | solution.py:70
  251.0 2.9 fusion.13
  253.9 3.1 fusion.14
  257.1 0.7 convolution_add_fusion
  258.8 1.1 fusion.21
  259.9 0.7 fusion.33
  260.7 4.9 %fusion = f32[2048,256]{1,0:T(8,128)S(1)} fusion(s32[2048]{0:T(1024)S(1)} %bitcast.87, bf16[2048,512]{1,0:T(8,128)(2,1)S(1)} %fusion.33), kind=kOutput, calls=%fused_computation.7 | convolution fusion | flops 2151677952 | bytes 3153920 | tf_op jit(solution)/shard_map/dot_general | solution.py:17
  265.6 6.3 %fusion.11 = bf16[2048,256]{1,0:T(8,128)(2,1)} fusion(f32[2048,256]{1,0:T(8,128)S(1)} %fusion, s32[2048]{0:T(1024)S(1)} %bitcast.85, bf16[2048,512]{1,0:T(8,128)(2,1)S(1)} %fusion.33), kind=kOutput, calls=%fused_computation.24 | convolution fusion | flops 2152726528 | bytes 4202496 | tf_op jit(solution)/shard_map/dot_general | solution.py:17
  271.9 3.9 all-to-all-start.3
  275.9 0.8 copy.32
  276.7 0.7 reshape_squeeze.3
  277.9 0.8 reduce.7
  278.8 2.7 fusion.31
  281.5 1.1 copy.36
  282.9 12.5 %all-to-all-done.3 = bf16[128,16,256]{2,1,0:T(8,128)(2,1)S(1)} async-done(((bf16[128,16,256]{2,1,0:T(8,128)(2,1)}), bf16[128,16,256]{2,1,0:T(8,128)(2,1)S(1)}, u32[]{:S(2)}, u32[]{:S(2)}) %all-to-all-start.3) | async-done | bytes 1048608 | tf_op jit(solution)/shard_map/all_to_all | solution.py:97
  295.4 13.0 %scatter_custom_fusion = f32[2048,256]{1,0:T(8,128)} fusion(s32[2048]{0:T(1024)S(1)} %bitcast.83, bf16[2048,256]{1,0:T(8,128)(2,1)S(1)} %bitcast.66, f32[]{:T(128)} %constant.6.clone.1), kind=kCustom, calls=%fused_computation.34 | custom fusion | flops 1048576 | bytes 3145732 | tf_op jit(solution)/shard_map/scatter-add | solution.py:107
  308.4 1.7 convert_element_type.61
  310.1 1.2 convolution_bitcast_fusion
  311.8 12.3 %fusion.16 = f32[3072,256]{1,0:T(8,128)} fusion(f32[2048,3072]{1,0:T(8,128)} %reshape.208, bf16[2048,256]{1,0:T(8,128)(2,1)S(1)} %convert_element_type.61, bf16[256,256]{1,0:T(8,128)(2,1)S(1)} %copy-done.10, f32[2048]{0:T(1024)S(1)} %broadcast_maximum_fusion), kind=kOutput, calls=%fused_computation.30 | convolution fusion | flops 3490185216 | bytes 29499392 | tf_op jit(solution)/shard_map/dot_general | solution.py:17
  325.2 1.0 copy-done.6
  326.2 2.1 fusion.47
  328.3 4.3 all-to-all-start.4
  332.7 3.4 convolution_add_fusion.1
  336.0 10.8 %all-to-all-done.4 = bf16[128,8,256]{2,1,0:T(8,128)(2,1)S(1)} async-done(((bf16[128,8,256]{2,1,0:T(8,128)(2,1)}), bf16[128,8,256]{2,1,0:T(8,128)(2,1)S(1)}, u32[]{:S(2)}, u32[]{:S(2)}) %all-to-all-start.4) | async-done | bytes 524320 | tf_op jit(solution)/shard_map/all_to_all | solution.py:116
  346.9 9.0 %scatter_custom_fusion.1 = f32[2048,256]{1,0:T(8,128)} fusion(f32[2048,256]{1,0:T(8,128)} %convolution_add_fusion.1, s32[1024]{0:T(1024)S(1)} %bitcast.90, bf16[128,8,256]{2,1,0:T(8,128)(2,1)S(1)} %all-to-all-done.4), kind=kCustom, calls=%fused_computation.52 | custom fusion | flops 524288 | bytes 2621440 | tf_op jit(solution)/shard_map/scatter-add | solution.py:122
  355.8 117.2 %all-reduce.2.cloned.1.call-done = f32[262656]{0:T(1024)} async-done(((f32[262656]{0:T(1024)}), f32[262656]{0:T(1024)}) %all-reduce.2.cloned.1.call-update) | async-done | bytes 1050640 | tf_op jit(solution)/shard_map/psum | solution.py:9
  473.0 1.2 slice.94
  474.2 0.9 slice.79
  475.2 0.8 slice.75
  476.0 0.8 slice.77
  (77 shorter events, 4.9 us)
Async XLA Ops:
  7.2 249.9 %copy-start = (bf16[512,256]{1,0:T(8,128)(2,1)S(1)}, bf16[512,256]{1,0:T(8,128)(2,1)}, u32[]{:S(2)}) copy-start(bf16[512,256]{1,0:T(8,128)(2,1)} %param.25) | copy-start | bytes 786436
  8.7 173.4 %all-to-all-start.1 = ((s32[128,1,16]{2,1,0:T(1,128)}), s32[128,1,16]{2,1,0:T(1,128)S(1)}, u32[]{:S(2)}, u32[]{:S(2)}) async-start(s32[128,1,16]{2,1,0:T(1,128)} %bitcast.7), calls=%async_computation.1 | async-start | bytes 131072 | tf_op jit(solution)/shard_map/all_to_all | solution.py:65
  167.9 9.2 %copy-start.1 = (bf16[2048,256]{1,0:T(8,128)(2,1)S(1)}, bf16[2048,256]{1,0:T(8,128)(2,1)}, u32[]{:S(2)}) copy-start(bf16[2048,256]{1,0:T(8,128)(2,1)} %param.14) | copy-start | bytes 3145732
  182.1 23.8 %all-to-all-start = ((bf16[128,8,256]{2,1,0:T(8,128)(2,1)}), bf16[128,8,256]{2,1,0:T(8,128)(2,1)S(1)}, u32[]{:S(2)}, u32[]{:S(2)}) async-start(bf16[128,8,256]{2,1,0:T(8,128)(2,1)} %bitcast.5), calls=%async_computation | async-start | bytes 1048576 | tf_op jit(solution)/shard_map/all_to_all | solution.py:44
  205.9 11.9 %copy-start.4 = (f32[2048,256]{1,0:T(8,128)S(1)}, f32[2048,256]{1,0:T(8,128)}, u32[]{:S(2)}) copy-start(f32[2048,256]{1,0:T(8,128)} %fusion.59) | copy-start | bytes 6291460
  205.9 11.9 %copy-start.9 = (bf16[256,256]{1,0:T(8,128)(2,1)S(1)}, bf16[256,256]{1,0:T(8,128)(2,1)}, u32[]{:S(2)}) copy-start(bf16[256,256]{1,0:T(8,128)(2,1)} %param.24) | copy-start | bytes 393220
  227.3 4.1 copy-start.15
  227.3 23.7 %all-to-all-start.2 = ((bf16[128,16,256]{2,1,0:T(8,128)(2,1)}), bf16[128,16,256]{2,1,0:T(8,128)(2,1)S(1)}, u32[]{:S(2)}, u32[]{:S(2)}) async-start(bf16[128,16,256]{2,1,0:T(8,128)(2,1)} %bitcast.65), calls=%async_computation.2 | async-start | bytes 2097152 | tf_op jit(solution)/shard_map/all_to_all | solution.py:70
  253.9 3.2 copy-start.21
  253.9 3.2 copy-start.20
  257.1 1.0 copy-start.22
  257.1 1.0 copy-start.18
  258.1 1.9 copy-start.2
  258.1 0.7 copy-start.16
  258.1 0.8 copy-start.17
  258.5 2.2 copy-start.13
  259.9 5.7 %copy-start.11 = (pred[2048,256]{1,0:T(32,128)(4,1)}, pred[2048,256]{1,0:T(32,128)(4,1)S(1)}, u32[]{:S(2)}) copy-start(pred[2048,256]{1,0:T(32,128)(4,1)S(1)} %get-tuple-element.8) | copy-start | bytes 1572868
  271.9 23.4 %all-to-all-start.3 = ((bf16[128,16,256]{2,1,0:T(8,128)(2,1)}), bf16[128,16,256]{2,1,0:T(8,128)(2,1)S(1)}, u32[]{:S(2)}, u32[]{:S(2)}) async-start(bf16[128,16,256]{2,1,0:T(8,128)(2,1)} %bitcast.69), calls=%async_computation.3 | async-start | bytes 2097152 | tf_op jit(solution)/shard_map/all_to_all | solution.py:97
  275.8 197.2 %all-reduce.2.cloned.1.call-start = ((), (), s32[]{:S(2)}) async-start(), calls=%async_computation.5 | async-start | bytes 2105344 | tf_op jit(solution)/shard_map/psum | solution.py:9
  278.8 3.8 copy-start.3
  310.1 1.7 copy-start.10
  311.8 12.3 %copy-start.8 = (f32[32,2,8,128]{3,2,1,0:T(8,128)S(1)}, f32[32,2,8,128]{3,2,1,0:T(8,128)}, u32[]{:S(2)}) copy-start(f32[32,2,8,128]{3,2,1,0:T(8,128)} %convolution_bitcast_fusion) | copy-start | bytes 786436
  324.1 1.0 copy-start.5
  324.1 1.1 copy-start.19
  325.1 7.5 %copy-start.14 = (s32[1024,1]{0,1:T(1,128)S(1)}, s32[1024,1]{0,1:T(1,128)}, u32[]{:S(2)}) copy-start(s32[1024,1]{0,1:T(1,128)} %reshape_squeeze.3) | copy-start | bytes 12292
  325.1 7.5 %copy-start.12 = (bf16[256,256]{1,0:T(8,128)(2,1)S(1)}, bf16[256,256]{1,0:T(8,128)(2,1)}, u32[]{:S(2)}) copy-start(bf16[256,256]{1,0:T(8,128)(2,1)} %param.23) | copy-start | bytes 393220
  325.2 1.0 copy-start.6
  328.3 18.5 %all-to-all-start.4 = ((bf16[128,8,256]{2,1,0:T(8,128)(2,1)}), bf16[128,8,256]{2,1,0:T(8,128)(2,1)S(1)}, u32[]{:S(2)}, u32[]{:S(2)}) async-start(bf16[128,8,256]{2,1,0:T(8,128)(2,1)} %fusion.47), calls=%async_computation.4 | async-start | bytes 1048576 | tf_op jit(solution)/shard_map/all_to_all | solution.py:116
  473.0 2.1 copy-start.7
Sparse Core Ops, SparseCore 0:
  326.4 146.6 all-reduce.1
where the time goes:
time: 492 us; the launch traced here: 485 us
  waiting for transfers between devices  174 us (35%)
  other arithmetic  135 us (27%)
  local copies, waits for them, and re-layouts  71.9 us (15%)
  matrix products  54.7 us (11%)
  starting transfers between devices  33.9 us (7%)
  between operations  15.6 us (3%)
    psum x1, waiting for transfers between devices, in_one(): total = lax.psum(vector, axis)  117 us
    unnamed x4, other arithmetic  97.6 us
    slice x2, local copies, waits for them, and re-layouts, per_device(): jnp.zeros((node_rows + 1, table_rows), jnp.float32).at[dst_index, edge_src]  43.9 us
    dot_general x3, matrix products, contract_rows(): lax.dot_general(left, right, (((0,), (0,)), ((), ())), preferred_element_...  23.5 us
    all_to_all x1, waiting for transfers between devices, per_device(): lax.all_to_all(served, ('dom', 'grp'), split_axis=0, concat_axis=0, tiled...  19.5 us
    all_to_all x1, waiting for transfers between devices, per_device(): lax.all_to_all(outgoing, ('dom', 'grp'), split_axis=0, concat_axis=0, til...  13.7 us
    scatter-add x1, other arithmetic, per_device(): embedding_grad = jnp.zeros((node_rows, feat_width), jnp.float32).at[wante...  13 us
    all_to_all x1, waiting for transfers between devices, per_device(): lax.all_to_all(received_grad_b.reshape(peer_count, req_len, feat_width),...  12.5 us
  transfers between devices with their start and end apart: 6, of which 5 were waited for; matrix products, arithmetic and copies ran while one was open for 38% of the time, Pallas kernels for 0%

commit v1 on v0

v1 whole, which is shorter than its diff:
```python
import jax
import jax.numpy as jnp
from jax import lax
from jax.experimental import pallas as pl
from jax.experimental.pallas import tpu as pltpu
from jax.sharding import PartitionSpec as P

AXES = ("dom", "grp")
GROUP = 32
LANES = 128
TILE = 256


def exchange(x):
    return lax.all_to_all(x, AXES, split_axis=0, concat_axis=0, tiled=True)


def dot32(a, b):
    return jnp.dot(a, b, preferred_element_type=jnp.float32)


def contract_rows(left, right):
    return lax.dot_general(
        left, right, (((0,), (0,)), ((), ())), preferred_element_type=jnp.float32
    )


def adjacency_kernel(half, panels, row_ref, inc_ref, flag_ref, unit_ref, adj_ref, deg_ref, words):
    step = pl.program_id(0)
    blocks = flag_ref.shape[0]

    @pl.when(step == 0)
    def _():
        rows = half * panels

        def zero(i, carry):
            words[pl.ds(pl.multiple_of(i * TILE, TILE), TILE), :] = jnp.zeros(
                (TILE, LANES), jnp.int32
            )
            return carry

        lax.fori_loop(0, rows // TILE, zero, 0)

        def block(b, carry):
            @pl.when(flag_ref[b] == 0)
            def _():
                at = [row_ref[j * blocks + b] for j in range(GROUP)]
                unit = [inc_ref[j * blocks + b] for j in range(GROUP)]
                new = [
                    words[pl.ds(at[j], 1), :] + unit_ref[pl.ds(unit[j], 1), :]
                    for j in range(GROUP)
                ]
                for j in range(GROUP):
                    words[pl.ds(at[j], 1), :] = new[j]

            @pl.when(flag_ref[b] != 0)
            def _():
                for j in range(GROUP):
                    at = row_ref[j * blocks + b]
                    unit = inc_ref[j * blocks + b]
                    words[pl.ds(at, 1), :] = (
                        words[pl.ds(at, 1), :] + unit_ref[pl.ds(unit, 1), :]
                    )

            return carry

        lax.fori_loop(0, blocks, block, 0)

    per_half = half // TILE
    shift = jnp.where(step >= per_half, 16, 0)
    first = lax.rem(step, per_half) * TILE
    total = jnp.zeros((TILE, LANES), jnp.int32)
    for p in range(panels):
        word = words[pl.ds(pl.multiple_of(p * half + first, TILE), TILE), :]
        count = jnp.bitwise_and(jnp.right_shift(word, shift), 0xFFFF)
        total = total + count
        adj_ref[:, p * LANES : (p + 1) * LANES] = count.astype(jnp.float32).astype(jnp.bfloat16)
    degree = jnp.sum(total.astype(jnp.float32), axis=1, keepdims=True)
    deg_ref[...] = jnp.broadcast_to(jnp.maximum(degree, 1.0), (TILE, LANES))


def adjacency(edge_src, edge_dst, live_count, node_rows, table_rows):
    half = node_rows // 2
    panels = table_rows // LANES
    slots = edge_src.shape[0]
    blocks = slots // GROUP
    slot = lax.iota(jnp.int32, slots)
    live = slot < live_count
    hi = edge_dst // half
    row = (edge_src // LANES) * half + (edge_dst - hi * half)
    spare = half * panels + slot // blocks
    row = jnp.where(live, row, spare)
    unit = jnp.where(live, edge_src % LANES + hi * LANES, 2 * LANES)
    key = row.reshape(GROUP, blocks)
    clash = jnp.zeros((GROUP, blocks), jnp.bool_)
    for s in range(1, GROUP // 2 + 1):
        clash = clash | (key == jnp.roll(key, s, axis=0))
    flag = jnp.any(clash, axis=0).astype(jnp.int32)
    lane = lax.broadcasted_iota(jnp.int32, (2 * LANES + 8, LANES), 1)
    which = lax.broadcasted_iota(jnp.int32, (2 * LANES + 8, LANES), 0)
    units = jnp.where(which == lane, 1, 0) + jnp.where(which - LANES == lane, 65536, 0)
    smem = pl.BlockSpec(memory_space=pltpu.SMEM)
    steps = node_rows // TILE
    return pl.pallas_call(
        lambda *refs: adjacency_kernel(half, panels, *refs),
        grid=(steps,),
        out_shape=(
            jax.ShapeDtypeStruct((node_rows, table_rows), jnp.bfloat16),
            jax.ShapeDtypeStruct((node_rows, LANES), jnp.float32),
        ),
        in_specs=[smem, smem, smem, pl.BlockSpec((2 * LANES + 8, LANES), lambda i: (0, 0))],
        out_specs=(
            pl.BlockSpec((TILE, table_rows), lambda i: (i, 0)),
            pl.BlockSpec((TILE, LANES), lambda i: (i, 0)),
        ),
        scratch_shapes=[pltpu.VMEM((half * panels + GROUP, LANES), jnp.int32)],
        compiler_params=pltpu.CompilerParams(vmem_limit_bytes=24 * 2**20),
        cost_estimate=pl.CostEstimate(
            flops=60_000_000, bytes_accessed=16 * 2**20, transcendentals=0
        ),
        name="adjacency",
    )(row, unit, flag, units)


def per_device(
    features,
    edge_src,
    edge_dst,
    edge_count,
    halo_index,
    request_rows,
    pair_ends,
    labels,
    pair_weight,
    w_self,
    w_neigh,
    w_hidden,
    b_hidden,
    w_out,
):
    node_rows, width = features.shape
    peers = lax.axis_size(AXES)
    halo_len = halo_index.shape[2]
    halo_rows = peers * halo_len
    req_len = request_rows.shape[2]
    recv_rows = peers * req_len
    nodes = lax.iota(jnp.int32, node_rows)

    wanted = exchange(request_rows[0]).reshape(recv_rows)
    halo_rows_of = halo_index[0].reshape(halo_rows)
    halo_pick = (halo_rows_of[:, None] == nodes[None, :]).astype(jnp.bfloat16)
    outgoing = dot32(halo_pick, features).astype(jnp.bfloat16)
    arrived = exchange(outgoing.reshape(peers, halo_len, width)).reshape(halo_rows, width)

    adj, floor_deg = adjacency(
        edge_src, edge_dst, edge_count[0], node_rows, node_rows + halo_rows
    )
    floor_deg = floor_deg[:, :1]
    agg_sums = dot32(adj[:, :node_rows], features) + dot32(adj[:, node_rows:], arrived)
    aggregate = (agg_sums / floor_deg).astype(jnp.bfloat16)
    embedding = (dot32(features, w_self) + dot32(aggregate, w_neigh)).astype(jnp.bfloat16)

    want_pick = (wanted[:, None] == nodes[None, :]).astype(jnp.bfloat16)
    served = dot32(want_pick, embedding).astype(jnp.bfloat16)
    received = exchange(served.reshape(peers, req_len, width)).reshape(recv_rows, width)

    slot_ids = lax.iota(jnp.int32, recv_rows)[None, :]
    select_left = (pair_ends[:, 0][:, None] == slot_ids).astype(jnp.bfloat16)
    select_right = (pair_ends[:, 1][:, None] == slot_ids).astype(jnp.bfloat16)
    left_rows = dot32(select_left, received).astype(jnp.bfloat16)
    right_rows = dot32(select_right, received).astype(jnp.bfloat16)
    pre_act = dot32(left_rows, w_hidden[:width]) + dot32(right_rows, w_hidden[width:]) + b_hidden
    hidden = jnp.maximum(pre_act, 0.0)
    logits = jnp.sum(hidden * w_out, axis=1)
    slope = pair_weight * (jax.nn.sigmoid(logits) - labels.astype(jnp.float32))
    grad_out = jnp.sum(slope[:, None] * hidden, axis=0)
    delta = jnp.where(pre_act > 0, slope[:, None] * w_out[None, :], 0.0)
    grad_bias = jnp.sum(delta, axis=0)
    delta_b = delta.astype(jnp.bfloat16)
    pair_grad = lax.dot_general(
        delta_b, w_hidden, (((1,), (1,)), ((), ())), preferred_element_type=jnp.float32
    ).astype(jnp.bfloat16)
    received_grad = contract_rows(select_left, pair_grad[:, :width]) + contract_rows(
        select_right, pair_grad[:, width:]
    )
    grad_hidden = jnp.concatenate(
        [contract_rows(left_rows, delta_b), contract_rows(right_rows, delta_b)], axis=0
    )
    small = jnp.concatenate([grad_bias, grad_out]).reshape(peers, -1)
    small_hi = small.astype(jnp.bfloat16)
    small_lo = (small - small_hi.astype(jnp.float32)).astype(jnp.bfloat16)
    small_len = small.shape[1]
    small_row = jnp.concatenate(
        [small_hi, small_lo, jnp.zeros((peers, width - 2 * small_len), jnp.bfloat16)], axis=1
    ).reshape(peers, 1, width)
    part_hidden = grad_hidden.shape[0] // peers
    back = exchange(
        jnp.concatenate(
            [
                received_grad.astype(jnp.bfloat16).reshape(peers, req_len, width),
                grad_hidden.astype(jnp.bfloat16).reshape(peers, part_hidden, width),
                small_row,
                jnp.zeros((peers, 7 - part_hidden, width), jnp.bfloat16),
            ],
            axis=1,
        )
    )
    back_rows = back[:, :req_len].reshape(recv_rows, width)
    own_hidden = jnp.sum(back[:, req_len : req_len + part_hidden].astype(jnp.float32), axis=0)
    small_sum = jnp.sum(
        back[:, req_len + part_hidden, : 2 * small_len].astype(jnp.float32), axis=0
    )
    own_small = small_sum[:small_len] + small_sum[small_len:]

    want_put = (nodes[:, None] == wanted[None, :]).astype(jnp.bfloat16)
    grad_b = dot32(want_put, back_rows).astype(jnp.bfloat16)
    grad_self = contract_rows(features, grad_b)
    grad_neigh = contract_rows(aggregate, grad_b)
    agg_grad = (
        lax.dot_general(
            grad_b, w_neigh, (((1,), (1,)), ((), ())), preferred_element_type=jnp.float32
        )
        / floor_deg
    ).astype(jnp.bfloat16)
    table_grad = contract_rows(adj, agg_grad)
    part_node = 2 * width // peers
    weight_terms = jnp.concatenate([grad_self, grad_neigh], axis=0).astype(jnp.bfloat16)
    last = exchange(
        jnp.concatenate(
            [
                table_grad[node_rows:].astype(jnp.bfloat16).reshape(peers, halo_len, width),
                weight_terms.reshape(peers, part_node, width),
                jnp.broadcast_to(
                    own_hidden.astype(jnp.bfloat16)[None], (peers, part_hidden, width)
                ),
            ],
            axis=1,
        )
    )
    own_node = jnp.sum(last[:, halo_len : halo_len + part_node].astype(jnp.float32), axis=0)
    small_own = jnp.concatenate([own_small, jnp.zeros((width - small_len,), jnp.float32)])
    finals = jnp.concatenate(
        [own_node, small_own[None], jnp.zeros((7 - part_node, width), jnp.float32)], axis=0
    ).astype(jnp.bfloat16)
    gathered = exchange(jnp.broadcast_to(finals[None], (peers, 8, width)))
    halo_put = (nodes[:, None] == halo_rows_of[None, :]).astype(jnp.bfloat16)
    grad_features = (
        lax.dot_general(
            grad_b, w_self, (((1,), (1,)), ((), ())), preferred_element_type=jnp.float32
        )
        + table_grad[:node_rows]
        + dot32(halo_put, last[:, :halo_len].reshape(halo_rows, width))
    )
    all_hidden = last[:, halo_len + part_node :].reshape(2 * width, width).astype(jnp.float32)
    all_node = gathered[:, :part_node].reshape(2 * width, width).astype(jnp.float32)
    all_small = gathered[:, part_node, :small_len].reshape(2 * width).astype(jnp.float32)
    return (
        logits,
        grad_features,
        all_node[:width],
        all_node[width:],
        all_hidden,
        all_small[:width],
        all_small[width:],
    )


def solution(mesh):
    split = P(AXES)
    in_specs = (
        P(AXES, None),
        split,
        split,
        split,
        P(AXES, None, None),
        P(AXES, None, None),
        P(AXES, None),
        split,
        split,
        P(),
        P(),
        P(),
        P(),
        P(),
    )
    out_specs = (split, P(AXES, None), P(), P(), P(), P(), P())
    return jax.shard_map(
        per_device, mesh=mesh, in_specs=in_specs, out_specs=out_specs, check_vma=False
    )
```

time: 492 us -> 290 us (0.59)
  waiting for transfers between devices: 174 us -> 46 us
  other arithmetic: 135 us -> 11.2 us
  Pallas kernels: 0 us -> 67.1 us
  local copies, waits for them, and re-layouts: 71.9 us -> 22.3 us
  blocking collectives: 0 us -> 28.9 us
  matrix products: 54.7 us -> 69.5 us
  between operations: 15.6 us -> 2.62 us
    psum x1 -> x0, waiting for transfers between devices: 117 us -> none  [in_one(): total = lax.psum(vector, axis)]
    unnamed x4 -> x0, other arithmetic: 97.6 us -> none
    pallas_call x0 -> x1, Pallas kernels: none -> 67.1 us  [adjacency(): pl.pallas_call(lambda *refs: adjacency_kernel(half, panels, *refs), grid=...]
    slice x9 -> x70, local copies, waits for them, and re-layouts: 48.1 us -> 3.95 us  [the longest x2 0.84 us: per_device(): all_small[width:]]
    all_to_all x0 -> x1, blocking collectives: none -> 28.9 us  [exchange(): return lax.all_to_all(x, AXES, split_axis=0, concat_axis=0, tiled=True)]
    scatter-add x2 -> x0, other arithmetic: 22 us -> none  [the longest x1 13 us: per_device(): embedding_grad = jnp.zeros((node_rows, feat_width), jnp.float32).at[wante...]
    gather x2 -> x0, local copies, waits for them, and re-layouts: 14 us -> none  [the longest x1 9.06 us: per_device(): served = embedding[wanted]]
    dot_general x13, matrix products: 31.2 us -> 43.1 us  [the longest x11 37 us: dot32(): return jnp.dot(a, b, preferred_element_type=jnp.float32)]
  transfers between devices with their start and end apart: 6 -> 5, of which waited for: 5 -> 4; matrix products, arithmetic and copies ran while one was open for 38% -> 8% of each run, Pallas kernels for 0% -> 24%
where the time goes in v1:
time: 290 us; the launch traced here: 285 us
  matrix products  69.5 us (24%)
  Pallas kernels  67.1 us (23%)
  waiting for transfers between devices  46 us (16%)
  starting transfers between devices  37.6 us (13%)
  blocking collectives  28.9 us (10%)
  local copies, waits for them, and re-layouts  22.3 us (8%)
  other arithmetic  11.2 us (4%)
    pallas_call x1, Pallas kernels, adjacency(): pl.pallas_call(lambda *refs: adjacency_kernel(half, panels, *refs), grid=...  67.1 us
    all_to_all x5, waiting for transfers between devices, exchange(): return lax.all_to_all(x, AXES, split_axis=0, concat_axis=0, tiled=True)  46 us
    all_to_all x5, starting transfers between devices, exchange(): return lax.all_to_all(x, AXES, split_axis=0, concat_axis=0, tiled=True)  37.6 us
    dot_general x11, matrix products, dot32(): return jnp.dot(a, b, preferred_element_type=jnp.float32)  37 us
    all_to_all x1, blocking collectives, exchange(): return lax.all_to_all(x, AXES, split_axis=0, concat_axis=0, tiled=True)  28.9 us
    dot_general x7, matrix products, contract_rows(): lax.dot_general(left, right, (((0,), (0,)), ((), ())), preferred_element_...  26.4 us
    unnamed x76, local copies, waits for them, and re-layouts  7.06 us
  transfers between devices with their start and end apart: 5, of which 4 were waited for; matrix products, arithmetic and copies ran while one was open for 8% of the time, Pallas kernels for 24%

profile of v1, /device:TPU:1, one launch (start us, length us, event | category | flops | bytes accessed | tf_op | source)
XLA Modules:
  0.0 285.1 jit_solution(5287524982536675921)
XLA Ops:
  0.6 1.5 copy.33
  2.2 11.5 %all-to-all-start = ((s32[128,1,16]{2,1,0:T(1,128)}), s32[128,1,16]{2,1,0:T(1,128)S(1)}, u32[]{:S(2)}, u32[]{:S(2)}) async-start(s32[128,1,16]{2,1,0:T(1,128)} %bitcast.1), calls=%async_computation | async-start | bytes 131072 | tf_op jit(solution)/shard_map/all_to_all | solution.py:15
  14.3 1.0 fusion.67
  16.5 2.3 fusion.39
  19.0 67.1 %adjacency.1 = (bf16[2048,3072]{1,0:T(8,128)(2,1)S(1)}, f32[2048,128]{1,0:T(8,128)S(1)}) custom-call(s32[16384]{0:T(1024)S(1)} %get-tuple-element.21.refs_0_, s32[16384]{0:T(1024)S(1)} %get-tuple-element.20.refs_1_, s32[512]{0:T(512)S(1)} %convert_element_type.93.refs_2_, s32[264,128]{1,0:T(8,128)S(1)} %select_add_fusion.refs_3_), custom_call_target="tpu_custom_call" | custom-call | flops 60000000 | bytes 16777216 | tf_op jit(solution)/shard_map/adjacency/pallas_call | solution.py:104
  86.1 4.5 %copy-done.1 = bf16[2048,3072]{1,0:T(8,128)(2,1)} copy-done((bf16[2048,3072]{1,0:T(8,128)(2,1)}, bf16[2048,3072]{1,0:T(8,128)(2,1)S(1)}, u32[]{:S(2)}) %copy-start.1) | copy-done | bytes 12582936
  90.6 11.1 %all-to-all-start.1 = ((bf16[128,8,256]{2,1,0:T(8,128)(2,1)}), bf16[128,8,256]{2,1,0:T(8,128)(2,1)}, u32[]{:S(2)}, u32[]{:S(2)}) async-start(bf16[128,8,256]{2,1,0:T(8,128)(2,1)} %fusion.39), calls=%async_computation.1 | async-start | bytes 1048576 | tf_op jit(solution)/shard_map/all_to_all | solution.py:15
  101.8 7.1 %fusion.9 = f32[2048,256]{1,0:T(8,128)} fusion(bf16[2048,256]{1,0:T(8,128)(2,1)S(1)} %copy-done, bf16[2048,3072]{1,0:T(8,128)(2,1)} %copy-done.1), kind=kOutput, calls=%fused_computation.15 | convolution fusion | flops 2147483648 | bytes 11534336 | tf_op jit(solution)/shard_map/dot_general | solution.py:19
  110.2 0.8 reduce.17
  111.1 4.0 %all-to-all-done.1 = bf16[128,8,256]{2,1,0:T(8,128)(2,1)} async-done(((bf16[128,8,256]{2,1,0:T(8,128)(2,1)}), bf16[128,8,256]{2,1,0:T(8,128)(2,1)}, u32[]{:S(2)}, u32[]{:S(2)}) %all-to-all-start.1) | async-done | bytes 524320 | tf_op jit(solution)/shard_map/all_to_all | solution.py:15
  115.1 5.3 %divide_convert_fusion = bf16[2048,256]{1,0:T(8,128)(2,1)} fusion(f32[2048,256]{1,0:T(8,128)} %fusion.9, bf16[2048,3072]{1,0:T(8,128)(2,1)} %copy-done.1, f32[2048]{0:T(1024)S(1)} %slice_reduce_fusion, bf16[128,8,256]{2,1,0:T(8,128)(2,1)} %all-to-all-done.1), kind=kOutput, calls=%fused_computation.47 | convolution fusion | flops 1075314688 | bytes 7872512 | tf_op jit(solution)/shard_map/dot_general | solution.py:19
  120.5 5.8 %fusion.30 = bf16[2048,256]{1,0:T(8,128)(2,1)} fusion(s32[2048]{0:T(1024)S(1)} %eq.146, f32[2048,256]{1,0:T(8,128)S(1)} %fusion.98, bf16[2048,256]{1,0:T(8,128)(2,1)} %divide_convert_fusion, bf16[256,256]{1,0:T(8,128)(2,1)S(1)} %copy-done.32), kind=kOutput, calls=%fused_computation.39 | convolution fusion | flops 2421686272 | bytes 4333568 | tf_op jit(solution)/shard_map/dot_general | solution.py:19
  126.3 5.8 %all-to-all-start.2 = ((bf16[128,16,256]{2,1,0:T(8,128)(2,1)}), bf16[128,16,256]{2,1,0:T(8,128)(2,1)S(1)}, u32[]{:S(2)}, u32[]{:S(2)}) async-start(bf16[128,16,256]{2,1,0:T(8,128)(2,1)} %bitcast.52), calls=%async_computation.2 | async-start | bytes 2097152 | tf_op jit(solution)/shard_map/all_to_all | solution.py:15
  133.3 18.3 %all-to-all-done.2 = bf16[128,16,256]{2,1,0:T(8,128)(2,1)S(1)} async-done(((bf16[128,16,256]{2,1,0:T(8,128)(2,1)}), bf16[128,16,256]{2,1,0:T(8,128)(2,1)S(1)}, u32[]{:S(2)}, u32[]{:S(2)}) %all-to-all-start.2) | async-done | bytes 1048608 | tf_op jit(solution)/shard_map/all_to_all | solution.py:15
  151.6 3.0 %fusion.31 = bf16[2048,256]{1,0:T(8,128)(2,1)S(1)} fusion(bf16[2048,256]{1,0:T(8,128)(2,1)S(1)} %bitcast.50, s32[2048]{0:T(1024)S(1)} %bitcast.55), kind=kOutput, calls=%fused_computation.40 | convolution fusion | flops 2152202240 | bytes 2105344 | tf_op jit(solution)/shard_map/dot_general | solution.py:19
  154.7 4.7 %fusion.32 = bf16[2048,256]{1,0:T(8,128)(2,1)S(1)} fusion(bf16[2048,256]{1,0:T(8,128)(2,1)} %bitcast.51, s32[2048]{0:T(1024)S(1)} %bitcast.57), kind=kOutput, calls=%fused_computation.41 | convolution fusion | flops 2152202240 | bytes 2105344 | tf_op jit(solution)/shard_map/dot_general | solution.py:19
  160.1 0.6 multiply_reduce_fusion.1
  160.8 2.1 fusion.33
  162.9 1.4 concatenate.120
  164.3 1.4 copy.36
  165.7 1.4 concatenate.119
  167.1 1.4 copy.35
  168.5 1.4 subtract_convert_fusion
  169.9 1.3 fusion.91
  171.2 2.5 convolution_convert_fusion.3
  173.7 0.8 convolution_convert_fusion.4
  174.6 2.1 convolution_convert_fusion
  177.3 6.3 %fusion = f32[2048,256]{1,0:T(8,128)S(1)} fusion(s32[2048]{0:T(1024)S(1)} %bitcast.58, bf16[2048,512]{1,0:T(8,128)(2,1)} %convolution_convert_fusion), kind=kOutput, calls=%fused_computation.2 | convolution fusion | flops 2151677952 | bytes 3153920 | tf_op jit(solution)/shard_map/dot_general | solution.py:23
  183.6 5.1 %fusion.26 = bf16[2048,256]{1,0:T(8,128)(2,1)S(1)} fusion(f32[2048,256]{1,0:T(8,128)S(1)} %fusion, s32[2048]{0:T(1024)S(1)} %bitcast.56, bf16[2048,512]{1,0:T(8,128)(2,1)S(1)} %copy-done.36), kind=kOutput, calls=%fused_computation.35 | convolution fusion | flops 2152726528 | bytes 4202496 | tf_op jit(solution)/shard_map/dot_general | solution.py:23
  188.8 0.8 maximum_maximum_fusion
  189.6 28.9 %all_to_all.34 = bf16[128,24,256]{2,1,0:T(8,128)(2,1)S(1)} all-to-all(bf16[128,24,256]{2,1,0:T(8,128)(2,1)S(1)} %maximum_maximum_fusion), channel_id=1, replica_groups=mesh['dom'=32,'grp'=4] {'dom','grp'}, dimensions={0} | all-to-all | bytes 3145728 | tf_op jit(solution)/shard_map/all_to_all | solution.py:15
  218.5 3.2 %fusion.29 = bf16[2048,256]{1,0:T(8,128)(2,1)S(1)} fusion(bf16[2048,256]{1,0:T(8,128)(2,1)S(1)} %bitcast.53, s32[2048]{0:T(1024)S(1)} %copy-done.15), kind=kOutput, calls=%fused_computation.38 | convolution fusion | flops 2152202240 | bytes 2105344 | tf_op jit(solution)/shard_map/dot_general | solution.py:19
  223.3 10.7 %fusion.37 = f32[3072,256]{1,0:T(8,128)} fusion(bf16[2048,3072]{1,0:T(8,128)(2,1)} %copy-done.1, bf16[2048,256]{1,0:T(8,128)(2,1)} %copy-done.2, bf16[256,256]{1,0:T(8,128)(2,1)S(1)} %copy-done.33, f32[2048]{0:T(1024)S(1)} %copy-done.13), kind=kOutput, calls=%fused_computation.48 | convolution fusion | flops 3490709504 | bytes 16916480 | tf_op jit(solution)/shard_map/dot_general | solution.py:23
  234.0 1.3 fusion.56
  235.5 1.3 pad_maximum_fusion
  236.9 5.0 %all-to-all-start.4 = ((bf16[128,16,256]{2,1,0:T(8,128)(2,1)}), bf16[128,16,256]{2,1,0:T(8,128)(2,1)}, u32[]{:S(2)}, u32[]{:S(2)}) async-start(bf16[128,16,256]{2,1,0:T(8,128)(2,1)} %pad_maximum_fusion), calls=%async_computation.4 | async-start | bytes 2097152 | tf_op jit(solution)/shard_map/all_to_all | solution.py:15
  242.2 19.0 %all-to-all-done.4 = bf16[128,16,256]{2,1,0:T(8,128)(2,1)} async-done(((bf16[128,16,256]{2,1,0:T(8,128)(2,1)}), bf16[128,16,256]{2,1,0:T(8,128)(2,1)}, u32[]{:S(2)}, u32[]{:S(2)}) %all-to-all-start.4) | async-done | bytes 1048608 | tf_op jit(solution)/shard_map/all_to_all | solution.py:15
  261.2 1.5 slice_convert_fusion.1
  262.7 0.8 broadcast_in_dim.59
  263.6 4.2 %all-to-all-start.5 = ((bf16[128,8,256]{2,1,0:T(8,128)(2,1)}), bf16[128,8,256]{2,1,0:T(8,128)(2,1)S(1)}, u32[]{:S(2)}, u32[]{:S(2)}) async-start(bf16[128,8,256]{2,1,0:T(8,128)(2,1)} %broadcast_in_dim.59), calls=%async_computation.5 | async-start | bytes 1048576 | tf_op jit(solution)/shard_map/all_to_all | solution.py:15
  267.8 4.0 %fusion.15 = f32[2048,256]{1,0:T(8,128)} fusion(s32[1024]{0:T(1024)S(1)} %copy-done.26, bf16[128,16,256]{2,1,0:T(8,128)(2,1)} %all-to-all-done.4), kind=kOutput, calls=%fused_computation.21 | convolution fusion | flops 1075838976 | bytes 2625536 | tf_op jit(solution)/shard_map/dot_general | solution.py:19
  271.8 1.0 reshape.388
  272.8 4.0 %fusion.20 = f32[2048,256]{1,0:T(8,128)} fusion(f32[2048,256]{1,0:T(8,128)} %fusion.15, bf16[2048,256]{1,0:T(8,128)(2,1)S(1)} %copy-done.3, bf16[256,256]{1,0:T(8,128)(2,1)S(1)} %copy-done.6, f32[3072,256]{1,0:T(8,128)} %fusion.37), kind=kOutput, calls=%fused_computation.28 | convolution fusion | flops 269484032 | bytes 7471104 | tf_op jit(solution)/shard_map/dot_general | solution.py:248
  276.8 4.7 %all-to-all-done.5 = bf16[128,8,256]{2,1,0:T(8,128)(2,1)S(1)} async-done(((bf16[128,8,256]{2,1,0:T(8,128)(2,1)}), bf16[128,8,256]{2,1,0:T(8,128)(2,1)S(1)}, u32[]{:S(2)}, u32[]{:S(2)}) %all-to-all-start.5) | async-done | bytes 524320 | tf_op jit(solution)/shard_map/all_to_all | solution.py:15
  281.7 0.8 slice.644
  282.5 0.8 slice.646
  283.5 0.7 slice.650
  284.2 0.7 slice.652
  (176 shorter events, 7.5 us)
Async XLA Ops:
  0.6 15.9 %copy-start = (bf16[2048,256]{1,0:T(8,128)(2,1)S(1)}, bf16[2048,256]{1,0:T(8,128)(2,1)}, u32[]{:S(2)}) copy-start(bf16[2048,256]{1,0:T(8,128)(2,1)} %param.14) | copy-start | bytes 3145732
  2.2 88.5 %all-to-all-start = ((s32[128,1,16]{2,1,0:T(1,128)}), s32[128,1,16]{2,1,0:T(1,128)S(1)}, u32[]{:S(2)}, u32[]{:S(2)}) async-start(s32[128,1,16]{2,1,0:T(1,128)} %bitcast.1), calls=%async_computation | async-start | bytes 131072 | tf_op jit(solution)/shard_map/all_to_all | solution.py:15
  15.4 0.9 copy-start.24
  16.5 2.3 copy-start.25
  86.1 4.5 %copy-start.1 = (bf16[2048,3072]{1,0:T(8,128)(2,1)}, bf16[2048,3072]{1,0:T(8,128)(2,1)S(1)}, u32[]{:S(2)}) copy-start(bf16[2048,3072]{1,0:T(8,128)(2,1)S(1)} %get-tuple-element.9) | copy-start | bytes 37748740
  90.6 24.5 %all-to-all-start.1 = ((bf16[128,8,256]{2,1,0:T(8,128)(2,1)}), bf16[128,8,256]{2,1,0:T(8,128)(2,1)}, u32[]{:S(2)}, u32[]{:S(2)}) async-start(bf16[128,8,256]{2,1,0:T(8,128)(2,1)} %fusion.39), calls=%async_computation.1 | async-start | bytes 1048576 | tf_op jit(solution)/shard_map/all_to_all | solution.py:15
  101.8 7.5 %copy-start.6 = (bf16[256,256]{1,0:T(8,128)(2,1)S(1)}, bf16[256,256]{1,0:T(8,128)(2,1)}, u32[]{:S(2)}) copy-start(bf16[256,256]{1,0:T(8,128)(2,1)} %param.23) | copy-start | bytes 393220
  109.2 11.2 %copy-start.12 = (f32[2048]{0:T(1024)}, f32[2048]{0:T(1024)S(1)}, u32[]{:S(2)}) copy-start(f32[2048]{0:T(1024)S(1)} %slice_reduce_fusion) | copy-start | bytes 24580
  111.1 9.4 %copy-start.14 = (s32[2048]{0:T(1024)}, s32[2048]{0:T(1024)S(1)}, u32[]{:S(2)}) copy-start(s32[2048]{0:T(1024)S(1)} %eq.146) | copy-start | bytes 24580
  111.1 9.4 %copy-start.32 = (bf16[256,256]{1,0:T(8,128)(2,1)S(1)}, bf16[256,256]{1,0:T(8,128)(2,1)}, u32[]{:S(2)}) copy-start(bf16[256,256]{1,0:T(8,128)(2,1)} %param.24) | copy-start | bytes 393220
  126.3 7.0 %copy-start.11 = (s32[2048,2]{0,1:T(2,128)S(1)}, s32[2048,2]{0,1:T(2,128)}, u32[]{:S(2)}) copy-start(s32[2048,2]{0,1:T(2,128)} %param.20) | copy-start | bytes 49156
  126.3 25.3 %all-to-all-start.2 = ((bf16[128,16,256]{2,1,0:T(8,128)(2,1)}), bf16[128,16,256]{2,1,0:T(8,128)(2,1)S(1)}, u32[]{:S(2)}, u32[]{:S(2)}) async-start(bf16[128,16,256]{2,1,0:T(8,128)(2,1)} %bitcast.52), calls=%async_computation.2 | async-start | bytes 2097152 | tf_op jit(solution)/shard_map/all_to_all | solution.py:15
  132.7 18.9 %copy-start.34 = (bf16[3]{0:T(256)(128)(2,1)}, bf16[3]{0:T(256)(128)(2,1)S(1)}, u32[]{:S(2)}) copy-start(bf16[3]{0:T(256)(128)(2,1)S(1)} %broadcast_in_dim.56) | copy-start | bytes 22
  133.3 21.3 %copy-start.18 = (s32[2048,1]{0,1:T(1,128)}, s32[2048,1]{0,1:T(1,128)S(1)}, u32[]{:S(2)}) copy-start(s32[2048,1]{0,1:T(1,128)S(1)} %get-tuple-element.25) | copy-start | bytes 24580
  133.3 21.3 %copy-start.20 = (s32[2048,1]{0,1:T(1,128)}, s32[2048,1]{0,1:T(1,128)S(1)}, u32[]{:S(2)}) copy-start(s32[2048,1]{0,1:T(1,128)S(1)} %get-tuple-element.24) | copy-start | bytes 24580
  151.6 3.0 %copy-start.5 = (bf16[128,16,256]{2,1,0:T(8,128)(2,1)}, bf16[128,16,256]{2,1,0:T(8,128)(2,1)S(1)}, u32[]{:S(2)}) copy-start(bf16[128,16,256]{2,1,0:T(8,128)(2,1)S(1)} %all-to-all-done.2) | copy-start | bytes 3145732
  154.7 4.7 %copy-start.8 = (bf16[512,256]{1,0:T(8,128)(2,1)S(1)}, bf16[512,256]{1,0:T(8,128)(2,1)}, u32[]{:S(2)}) copy-start(bf16[512,256]{1,0:T(8,128)(2,1)} %param.25) | copy-start | bytes 786436
  159.4 0.7 copy-start.22
  159.4 0.7 copy-start.29
  160.1 0.7 copy-start.16
  160.1 0.7 copy-start.17
  160.7 13.0 %copy-start.10 = (f32[2048]{0:T(1024)}, f32[2048]{0:T(1024)S(1)}, u32[]{:S(2)}) copy-start(f32[2048]{0:T(1024)S(1)} %get-tuple-element.26) | copy-start | bytes 24580
  168.5 5.2 %copy-start.7 = (pred[2048,256]{1,0:T(32,128)(4,1)S(1)}, pred[2048,256]{1,0:T(32,128)(4,1)}, u32[]{:S(2)}) copy-start(pred[2048,256]{1,0:T(32,128)(4,1)} %get-tuple-element.15) | copy-start | bytes 1572868
  168.5 5.2 %copy-start.23 = (f32[256]{0:T(256)S(1)}, f32[256]{0:T(256)}, u32[]{:S(2)}) copy-start(f32[256]{0:T(256)} %param.27) | copy-start | bytes 3076
  174.5 2.1 copy-start.28
  174.5 2.3 copy-start.27
  174.5 2.4 copy-start.31
  174.6 2.6 copy-start.9
  174.6 2.7 copy-start.21
  177.3 6.3 %copy-start.19 = (s32[2048,1]{0,1:T(1,128)S(1)}, s32[2048,1]{0,1:T(1,128)}, u32[]{:S(2)}) copy-start(s32[2048,1]{0,1:T(1,128)} %copy-done.18) | copy-start | bytes 24580
  177.3 6.3 %copy-start.36 = (bf16[2048,512]{1,0:T(8,128)(2,1)S(1)}, bf16[2048,512]{1,0:T(8,128)(2,1)}, u32[]{:S(2)}) copy-start(bf16[2048,512]{1,0:T(8,128)(2,1)} %convolution_convert_fusion) | copy-start | bytes 6291460
  183.6 5.2 %copy-start.30 = (bf16[24]{0:T(256)(128)(2,1)S(1)}, bf16[24]{0:T(256)(128)(2,1)}, u32[]{:S(2)}) copy-start(bf16[24]{0:T(256)(128)(2,1)} %pad.13.clone) | copy-start | bytes 148
  189.6 29.0 %copy-start.15 = (s32[2048]{0:T(1024)S(1)}, s32[2048]{0:T(1024)}, u32[]{:S(2)}) copy-start(s32[2048]{0:T(1024)} %copy-done.14) | copy-start | bytes 24580
  218.5 3.2 %copy-start.4 = (bf16[2048,256]{1,0:T(8,128)(2,1)S(1)}, bf16[2048,256]{1,0:T(8,128)(2,1)}, u32[]{:S(2)}) copy-start(bf16[2048,256]{1,0:T(8,128)(2,1)} %divide_convert_fusion) | copy-start | bytes 3145732
  221.7 1.0 copy-start.2
  221.7 1.5 copy-start.13
  221.8 1.5 copy-start.33
  235.5 6.3 %copy-start.35 = (bf16[3]{0:T(256)(128)(2,1)S(1)}, bf16[3]{0:T(256)(128)(2,1)}, u32[]{:S(2)}) copy-start(bf16[3]{0:T(256)(128)(2,1)} %copy-done.34) | copy-start | bytes 22
  236.9 30.9 %copy-start.26 = (s32[1024]{0:T(1024)S(1)}, s32[1024]{0:T(1024)}, u32[]{:S(2)}) copy-start(s32[1024]{0:T(1024)} %copy-done.25) | copy-start | bytes 12292
  236.9 24.3 %all-to-all-start.4 = ((bf16[128,16,256]{2,1,0:T(8,128)(2,1)}), bf16[128,16,256]{2,1,0:T(8,128)(2,1)}, u32[]{:S(2)}, u32[]{:S(2)}) async-start(bf16[128,16,256]{2,1,0:T(8,128)(2,1)} %pad_maximum_fusion), calls=%async_computation.4 | async-start | bytes 2097152 | tf_op jit(solution)/shard_map/all_to_all | solution.py:15
  263.6 18.0 %all-to-all-start.5 = ((bf16[128,8,256]{2,1,0:T(8,128)(2,1)}), bf16[128,8,256]{2,1,0:T(8,128)(2,1)S(1)}, u32[]{:S(2)}, u32[]{:S(2)}) async-start(bf16[128,8,256]{2,1,0:T(8,128)(2,1)} %broadcast_in_dim.59), calls=%async_computation.5 | async-start | bytes 1048576 | tf_op jit(solution)/shard_map/all_to_all | solution.py:15
  267.8 5.0 %copy-start.3 = (bf16[2048,256]{1,0:T(8,128)(2,1)S(1)}, bf16[2048,256]{1,0:T(8,128)(2,1)}, u32[]{:S(2)}) copy-start(bf16[2048,256]{1,0:T(8,128)(2,1)} %copy-done.2) | copy-start | bytes 3145732

commit v2 on v1

v2 whole, which is shorter than its diff:
```python
import jax
import jax.numpy as jnp
from jax import lax
from jax.experimental import pallas as pl
from jax.experimental.pallas import tpu as pltpu
from jax.sharding import PartitionSpec as P

AXES = ("dom", "grp")
LANES = 128
STRIDE = 8
GROUP = LANES // STRIDE
TILE = 256
CLASH = 1 << 20
VMEM = pl.BlockSpec(memory_space=pltpu.VMEM)
SMEM = pl.BlockSpec(memory_space=pltpu.SMEM)


def exchange(x):
    return lax.all_to_all(x, AXES, split_axis=0, concat_axis=0, tiled=True)


def dot32(a, b):
    return jnp.dot(a, b, preferred_element_type=jnp.float32)


def dot_nt(a, b):
    return lax.dot_general(a, b, (((1,), (1,)), ((), ())), preferred_element_type=jnp.float32)


def dot_tn(a, b):
    return lax.dot_general(a, b, (((0,), (0,)), ((), ())), preferred_element_type=jnp.float32)


def params(mib):
    return pltpu.CompilerParams(vmem_limit_bytes=mib * 2**20)


def cost(flops, size):
    return pl.CostEstimate(flops=flops, bytes_accessed=size, transcendentals=0)


def tile_of(i):
    return pl.ds(pl.multiple_of(i * TILE, TILE), TILE)


def pick(index, first, count, axis):
    shape = (index.shape[0], count) if axis == 1 else (count, index.shape[1])
    ids = lax.broadcasted_iota(jnp.int32, shape, axis) + first
    return jnp.where(index == ids, 1.0, 0.0).astype(jnp.bfloat16)


def slots_kernel(half, panels, count_ref, src_ref, dst_ref, row_ref, unit_ref):
    chunks = src_ref.shape[0]
    lane = lax.broadcasted_iota(jnp.int32, (chunks, LANES), 1)
    slot = lax.broadcasted_iota(jnp.int32, (chunks, LANES), 0) * LANES + lane
    live = slot < count_ref[0]
    src = src_ref[...]
    dst = dst_ref[...]
    upper = jnp.where(dst >= half, 1, 0)
    row = jnp.right_shift(src, 7) * half + dst - upper * half
    row = jnp.where(live, row, half * panels + jnp.right_shift(lane, 3))
    unit_ref[...] = jnp.where(live, jnp.bitwise_and(src, LANES - 1) + upper * LANES, 2 * LANES)
    clash = jnp.zeros((chunks, LANES), jnp.int32)
    for k in range(1, GROUP // 2 + 1):
        clash = clash + jnp.where(row == pltpu.roll(row, k * STRIDE, 1), 1, 0)
    any_clash = jnp.max(clash.astype(jnp.float32), axis=1, keepdims=True) > 0.0
    row_ref[...] = row + jnp.where(any_clash & (lane == 0), CLASH, 0)


def counts_kernel(half, panels, row_ref, unit_ref, adj_ref, deg_ref, degt_ref, words, units):
    step = pl.program_id(0)
    chunks = unit_ref.shape[0]

    @pl.when(step == 0)
    def _():
        def zero(i, carry):
            words[tile_of(i), :] = jnp.zeros((TILE, LANES), jnp.int32)
            return carry

        lax.fori_loop(0, half * panels // TILE, zero, 0)
        lane = lax.broadcasted_iota(jnp.int32, (LANES, LANES), 1)

        def fill(c):
            wide = jnp.transpose(
                jnp.broadcast_to(unit_ref[pl.ds(c, 1), :], (LANES, LANES))
            )
            return jnp.where(wide == lane, 1, jnp.where(wide == lane + LANES, 65536, 0))

        units[0:LANES, :] = fill(0)

        def chunk(c, carry):
            now = pl.multiple_of(lax.rem(c, 2) * LANES, LANES)
            later = pl.multiple_of(lax.rem(c + 1, 2) * LANES, LANES)
            base = c * LANES
            head = row_ref[base]
            nxt = fill(jnp.minimum(c + 1, chunks - 1))

            @pl.when(head < CLASH)
            def _():
                for s in range(STRIDE):
                    places = [s + STRIDE * t for t in range(GROUP)]
                    at = [row_ref[base + j] for j in places]
                    new = [
                        words[pl.ds(a, 1), :] + units[pl.ds(now + j, 1), :]
                        for a, j in zip(at, places)
                    ]
                    for a, n in zip(at, new):
                        words[pl.ds(a, 1), :] = n

            @pl.when(head >= CLASH)
            def _():
                def one(j, carry):
                    a = jnp.bitwise_and(row_ref[base + j], CLASH - 1)
                    words[pl.ds(a, 1), :] = words[pl.ds(a, 1), :] + units[pl.ds(now + j, 1), :]
                    return carry

                lax.fori_loop(0, LANES, one, 0)

            units[pl.ds(later, LANES), :] = nxt
            return carry

        lax.fori_loop(0, chunks, chunk, 0)

    per_half = half // TILE
    shift = jnp.where(step >= per_half, 16, 0)
    first = lax.rem(step, per_half) * TILE
    total = jnp.zeros((TILE, LANES), jnp.int32)
    for p in range(panels):
        word = words[pl.ds(pl.multiple_of(p * half + first, TILE), TILE), :]
        count = jnp.bitwise_and(jnp.right_shift(word, shift), 0xFFFF)
        total = total + count
        adj_ref[:, p * LANES : (p + 1) * LANES] = count.astype(jnp.float32).astype(jnp.bfloat16)
    degree = jnp.sum(total.astype(jnp.float32), axis=1, keepdims=True)
    wide = jnp.broadcast_to(jnp.maximum(degree, 1.0), (TILE, LANES))
    deg_ref[...] = wide
    degt_ref[...] = jnp.transpose(wide)[:8]


def adjacency(edge_src, edge_dst, edge_count, node_rows, table_rows):
    half = node_rows // 2
    panels = table_rows // LANES
    chunks = edge_src.shape[0] // LANES
    grid_shape = (chunks, LANES)
    row, unit = pl.pallas_call(
        lambda *refs: slots_kernel(half, panels, *refs),
        out_shape=(
            jax.ShapeDtypeStruct(grid_shape, jnp.int32),
            jax.ShapeDtypeStruct(grid_shape, jnp.int32),
        ),
        in_specs=[SMEM, VMEM, VMEM],
        out_specs=(VMEM, VMEM),
        compiler_params=params(8),
        name="slots",
    )(edge_count, edge_src.reshape(grid_shape), edge_dst.reshape(grid_shape))
    return pl.pallas_call(
        lambda *refs: counts_kernel(half, panels, *refs),
        grid=(node_rows // TILE,),
        out_shape=(
            jax.ShapeDtypeStruct((node_rows, table_rows), jnp.bfloat16),
            jax.ShapeDtypeStruct((node_rows, LANES), jnp.float32),
            jax.ShapeDtypeStruct((8, node_rows), jnp.float32),
        ),
        in_specs=[SMEM, pl.BlockSpec(grid_shape, lambda i: (0, 0))],
        out_specs=(
            pl.BlockSpec((TILE, table_rows), lambda i: (i, 0)),
            pl.BlockSpec((TILE, LANES), lambda i: (i, 0)),
            pl.BlockSpec((8, TILE), lambda i: (0, i)),
        ),
        scratch_shapes=[
            pltpu.VMEM((half * panels + GROUP, LANES), jnp.int32),
            pltpu.VMEM((2 * LANES, LANES), jnp.int32),
        ],
        compiler_params=params(24),
        cost_estimate=cost(60_000_000, 16 * 2**20),
        name="counts",
    )(row.reshape(-1), unit)


def encode_kernel(
    adj_ref, feat_ref, arr_ref, deg_ref, ws_ref, wn_ref, want_ref, agg_ref, served_ref, emb
):
    step = pl.program_id(0)
    node_rows = feat_ref.shape[0]
    sums = dot32(adj_ref[:, :node_rows], feat_ref[...]) + dot32(
        adj_ref[:, node_rows:], arr_ref[...]
    )
    mean = (sums / deg_ref[:, :1]).astype(jnp.bfloat16)
    agg_ref[...] = mean
    own = feat_ref[tile_of(step), :]
    emb[tile_of(step), :] = (dot32(own, ws_ref[...]) + dot32(mean, wn_ref[...])).astype(
        jnp.bfloat16
    )

    @pl.when(step == pl.num_programs(0) - 1)
    def _():
        def serve(j, carry):
            hot = pick(want_ref[tile_of(j), :], 0, node_rows, 1)
            served_ref[tile_of(j), :] = dot32(hot, emb[...]).astype(jnp.bfloat16)
            return carry

        lax.fori_loop(0, served_ref.shape[0] // TILE, serve, 0)


def encode(adj, features, arrived, deg, w_self, w_neigh, want_col):
    node_rows, width = features.shape
    table_rows = adj.shape[1]
    recv_rows = want_col.shape[0]
    whole = lambda a: pl.BlockSpec(a.shape, lambda i: (0, 0))
    return pl.pallas_call(
        encode_kernel,
        grid=(node_rows // TILE,),
        out_shape=(
            jax.ShapeDtypeStruct((node_rows, width), jnp.bfloat16),
            jax.ShapeDtypeStruct((recv_rows, width), jnp.bfloat16),
        ),
        in_specs=[
            pl.BlockSpec((TILE, table_rows), lambda i: (i, 0)),
            whole(features),
            whole(arrived),
            pl.BlockSpec((TILE, LANES), lambda i: (i, 0)),
            whole(w_self),
            whole(w_neigh),
            whole(want_col),
        ],
        out_specs=(
            pl.BlockSpec((TILE, width), lambda i: (i, 0)),
            pl.BlockSpec((recv_rows, width), lambda i: (0, 0)),
        ),
        scratch_shapes=[pltpu.VMEM((node_rows, width), jnp.bfloat16)],
        compiler_params=params(24),
        cost_estimate=cost(8_000_000_000, 16 * 2**20),
        name="encode",
    )(adj, features, arrived, deg, w_self, w_neigh, want_col)


def decode_kernel(
    recv_ref,
    endc_ref,
    endr_ref,
    wl_ref,
    wh_ref,
    bias_ref,
    wo_ref,
    logit_ref,
    rgrad_ref,
    ghid_ref,
    gsmall_ref,
    left_s,
    right_s,
    delta_s,
    pgl_s,
    pgr_s,
):
    pairs = endc_ref.shape[0]
    recv_rows, width = recv_ref.shape
    gsmall_ref[...] = jnp.zeros(gsmall_ref.shape, jnp.float32)

    def forward(i, carry):
        at = tile_of(i)
        ends = endc_ref[at, :]
        left = dot32(pick(ends[:, 0:1], 0, recv_rows, 1), recv_ref[...]).astype(jnp.bfloat16)
        right = dot32(pick(ends[:, 1:2], 0, recv_rows, 1), recv_ref[...]).astype(jnp.bfloat16)
        pre = dot32(left, wh_ref[:width, :]) + dot32(right, wh_ref[width:, :]) + bias_ref[...]
        hidden = jnp.maximum(pre, 0.0)
        logit = jnp.sum(hidden * wo_ref[...], axis=1, keepdims=True)
        logit_ref[at, :] = logit
        wl = wl_ref[at, :]
        slope = wl[:, 0:1] * (jax.nn.sigmoid(logit) - wl[:, 1:2])
        delta = jnp.where(pre > 0, slope * wo_ref[...], 0.0)
        gsmall_ref[0:1, :] += jnp.sum(delta, axis=0, keepdims=True)
        gsmall_ref[1:2, :] += jnp.sum(slope * hidden, axis=0, keepdims=True)
        delta_b = delta.astype(jnp.bfloat16)
        left_s[at, :] = left
        right_s[at, :] = right
        delta_s[at, :] = delta_b
        pgl_s[at, :] = dot_nt(delta_b, wh_ref[:width, :]).astype(jnp.bfloat16)
        pgr_s[at, :] = dot_nt(delta_b, wh_ref[width:, :]).astype(jnp.bfloat16)
        return carry

    lax.fori_loop(0, pairs // TILE, forward, 0)

    def backward(i, carry):
        total = dot32(pick(endr_ref[0:1, :], i * TILE, TILE, 0), pgl_s[...]) + dot32(
            pick(endr_ref[1:2, :], i * TILE, TILE, 0), pgr_s[...]
        )
        rgrad_ref[tile_of(i), :] = total.astype(jnp.bfloat16)
        return carry

    lax.fori_loop(0, recv_rows // TILE, backward, 0)
    ghid_ref[:width, :] = dot_tn(left_s[...], delta_s[...]).astype(jnp.bfloat16)
    ghid_ref[width:, :] = dot_tn(right_s[...], delta_s[...]).astype(jnp.bfloat16)


def decode(received, end_cols, end_rows, wl_cols, w_hidden, bias, w_out):
    recv_rows, width = received.shape
    pairs = end_cols.shape[0]
    scratch = pltpu.VMEM((pairs, width), jnp.bfloat16)
    return pl.pallas_call(
        decode_kernel,
        out_shape=(
            jax.ShapeDtypeStruct((pairs, 1), jnp.float32),
            jax.ShapeDtypeStruct((recv_rows, width), jnp.bfloat16),
            jax.ShapeDtypeStruct((2 * width, width), jnp.bfloat16),
            jax.ShapeDtypeStruct((8, width), jnp.float32),
        ),
        in_specs=[VMEM] * 7,
        out_specs=(VMEM,) * 4,
        scratch_shapes=[scratch] * 5,
        compiler_params=params(32),
        cost_estimate=cost(12_000_000_000, 4 * 2**20),
        name="decode",
    )(received, end_cols, end_rows, wl_cols, w_hidden, bias, w_out)


def node_grads_kernel(
    back_ref, want_ref, feat_ref, agg_ref, wn_ref, degt_ref, adj_ref,
    gradb_ref, gt_ref, gw_ref, halo_ref
):
    step = pl.program_id(0)
    node_rows, width = feat_ref.shape

    @pl.when(step == 0)
    def _():
        def put(i, carry):
            hot = pick(want_ref[...], i * TILE, TILE, 0)
            gradb_ref[tile_of(i), :] = dot32(hot, back_ref[...]).astype(jnp.bfloat16)
            return carry

        lax.fori_loop(0, node_rows // TILE, put, 0)
        gw_ref[:width, :] = dot_tn(feat_ref[...], gradb_ref[...]).astype(jnp.bfloat16)
        gw_ref[width:, :] = dot_tn(agg_ref[...], gradb_ref[...]).astype(jnp.bfloat16)
        gt_ref[...] = (dot_nt(wn_ref[...], gradb_ref[...]) / degt_ref[0:1, :]).astype(
            jnp.bfloat16
        )

    halo_ref[...] = jnp.transpose(dot32(gt_ref[...], adj_ref[...])).astype(jnp.bfloat16)


def node_grads(back, want_row, features, aggregate, w_neigh, degt, adj):
    node_rows, width = features.shape
    halo_rows = adj.shape[1] - node_rows
    whole = lambda a: pl.BlockSpec(a.shape, lambda i: (0, 0))
    skip = node_rows // TILE
    fixed = lambda i: (0, 0)
    return pl.pallas_call(
        node_grads_kernel,
        grid=(halo_rows // TILE,),
        out_shape=(
            jax.ShapeDtypeStruct((node_rows, width), jnp.bfloat16),
            jax.ShapeDtypeStruct((width, node_rows), jnp.bfloat16),
            jax.ShapeDtypeStruct((2 * width, width), jnp.bfloat16),
            jax.ShapeDtypeStruct((halo_rows, width), jnp.bfloat16),
        ),
        in_specs=[
            whole(back),
            whole(want_row),
            whole(features),
            whole(aggregate),
            whole(w_neigh),
            whole(degt),
            pl.BlockSpec((node_rows, TILE), lambda i: (0, i + skip)),
        ],
        out_specs=(
            pl.BlockSpec((node_rows, width), fixed),
            pl.BlockSpec((width, node_rows), fixed),
            pl.BlockSpec((2 * width, width), fixed),
            pl.BlockSpec((TILE, width), lambda i: (i, 0)),
        ),
        compiler_params=params(24),
        cost_estimate=cost(6_000_000_000, 8 * 2**20),
        name="node_grads",
    )(back, want_row, features, aggregate, w_neigh, degt, adj)


def own_grads_kernel(gradb_ref, gt_ref, ws_ref, adj_ref, out_ref):
    out_ref[...] = dot_nt(gradb_ref[...], ws_ref[...]) + jnp.transpose(
        dot32(gt_ref[...], adj_ref[...])
    )


def own_grads(grad_b, grad_t, w_self, adj):
    node_rows, width = grad_b.shape
    whole = lambda a: pl.BlockSpec(a.shape, lambda i: (0, 0))
    return pl.pallas_call(
        own_grads_kernel,
        grid=(node_rows // TILE,),
        out_shape=jax.ShapeDtypeStruct((node_rows, width), jnp.float32),
        in_specs=[
            pl.BlockSpec((TILE, width), lambda i: (i, 0)),
            whole(grad_t),
            whole(w_self),
            pl.BlockSpec((node_rows, TILE), lambda i: (0, i)),
        ],
        out_specs=pl.BlockSpec((TILE, width), lambda i: (i, 0)),
        compiler_params=params(24),
        cost_estimate=cost(6_000_000_000, 8 * 2**20),
        name="own_grads",
    )(grad_b, grad_t, w_self, adj)


def per_device(
    features,
    edge_src,
    edge_dst,
    edge_count,
    halo_index,
    request_rows,
    pair_ends,
    labels,
    pair_weight,
    w_self,
    w_neigh,
    w_hidden,
    b_hidden,
    w_out,
):
    node_rows, width = features.shape
    peers = lax.axis_size(AXES)
    halo_len = halo_index.shape[2]
    halo_rows = peers * halo_len
    req_len = request_rows.shape[2]
    recv_rows = peers * req_len
    nodes = lax.iota(jnp.int32, node_rows)

    halo_pad = jnp.pad(halo_index[0], ((0, 0), (0, req_len - halo_len)), constant_values=-1)
    halo_pick = (halo_pad.reshape(-1)[:, None] == nodes[None, :]).astype(jnp.bfloat16)
    asked = jnp.concatenate([request_rows[0] // 64, request_rows[0] % 64], axis=1)
    asked = jnp.pad(
        asked.astype(jnp.float32)[:, None, :],
        ((0, 0), (halo_len, req_len - halo_len - 1), (0, width - 2 * req_len)),
    ).reshape(peers * req_len, width)
    outgoing = (dot32(halo_pick, features) + asked).astype(jnp.bfloat16)
    outgoing = outgoing.reshape(peers, req_len, width)
    first = exchange(outgoing)
    edge_src, edge_dst, _ = lax.optimization_barrier((edge_src, edge_dst, outgoing))

    adj, deg, degt = adjacency(edge_src, edge_dst, edge_count, node_rows, node_rows + halo_rows)
    arrived = first[:, :halo_len].reshape(halo_rows, width)
    codes = first[:, halo_len, : 2 * req_len].astype(jnp.int32)
    wanted = (codes[:, :req_len] * 64 + codes[:, req_len:]).reshape(recv_rows)
    want_col = wanted.reshape(recv_rows, 1)
    want_row = wanted.reshape(1, recv_rows)
    aggregate, served = encode(adj, features, arrived, deg, w_self, w_neigh, want_col)
    received = exchange(served.reshape(peers, req_len, width)).reshape(recv_rows, width)

    wl_cols = jnp.stack([pair_weight, labels.astype(jnp.float32)], axis=1)
    logits, received_grad, grad_hidden, small = decode(
        received, pair_ends, pair_ends.T, wl_cols, w_hidden, b_hidden[None], w_out[None]
    )
    small = small[:2]
    small_hi = small.astype(jnp.bfloat16)
    small_lo = (small - small_hi.astype(jnp.float32)).astype(jnp.bfloat16)
    part = 2 * width // peers
    back = exchange(
        jnp.concatenate(
            [
                received_grad.reshape(peers, req_len, width),
                grad_hidden.reshape(peers, part, width),
                jnp.broadcast_to(small_hi[None], (peers, 2, width)),
                jnp.broadcast_to(small_lo[None], (peers, 2, width)),
            ],
            axis=1,
        )
    )
    back_rows = back[:, :req_len].reshape(recv_rows, width)
    sums = jnp.sum(back[:, req_len:].astype(jnp.float32), axis=0)
    own_hidden = sums[:part].astype(jnp.bfloat16)
    all_small = sums[part : part + 2] + sums[part + 2 : part + 4]

    grad_b, grad_t, weight_terms, halo_grad = node_grads(
        back_rows, want_row, features, aggregate, w_neigh, degt, adj
    )
    last = exchange(
        jnp.concatenate(
            [
                halo_grad.reshape(peers, halo_len, width),
                weight_terms.reshape(peers, part, width),
                jnp.broadcast_to(own_hidden[None], (peers, part, width)),
            ],
            axis=1,
        )
    )
    own = own_grads(grad_b, grad_t, w_self, adj)
    own_node = jnp.sum(last[:, halo_len : halo_len + part].astype(jnp.float32), axis=0)
    finals = own_node.astype(jnp.bfloat16).reshape(1, part * width // LANES, LANES)
    gathered = exchange(jnp.broadcast_to(finals, (peers, part * width // LANES, LANES)))
    halo_put = (nodes[:, None] == halo_index[0].reshape(halo_rows)[None, :]).astype(jnp.bfloat16)
    grad_features = own + dot32(halo_put, last[:, :halo_len].reshape(halo_rows, width))
    all_hidden = last[:, halo_len + part :].reshape(2 * width, width).astype(jnp.float32)
    all_node = gathered.reshape(2 * width, width).astype(jnp.float32)
    return (
        logits.reshape(-1),
        grad_features,
        all_node[:width],
        all_node[width:],
        all_hidden,
        all_small[0],
        all_small[1],
    )


def solution(mesh):
    split = P(AXES)
    in_specs = (
        P(AXES, None),
        split,
        split,
        split,
        P(AXES, None, None),
        P(AXES, None, None),
        P(AXES, None),
        split,
        split,
        P(),
        P(),
        P(),
        P(),
        P(),
    )
    out_specs = (split, P(AXES, None), P(), P(), P(), P(), P())
    return jax.shard_map(
        per_device, mesh=mesh, in_specs=in_specs, out_specs=out_specs, check_vma=False
    )
```

time: 290 us -> 242 us (0.83); the launches traced: 285 us -> 240 us
  matrix products: 69.5 us -> 7.91 us
  blocking collectives: 28.9 us -> 0 us
  local copies, waits for them, and re-layouts: 22.3 us -> 41.9 us
  Pallas kernels: 67.1 us -> 86.3 us
  waiting for transfers between devices: 46 us -> 53.6 us
  other arithmetic: 11.2 us -> 7.14 us
  starting transfers between devices: 37.6 us -> 41.6 us
    dot_general x9 -> x0, matrix products: 32.5 us -> none  [the longest x7 26.4 us: contract_rows(): lax.dot_general(left, right, (((0,), (0,)), ((), ())), preferred_element_...]
    dot_general x11 -> x2, matrix products: 37 us -> 7.91 us  [dot32(): return jnp.dot(a, b, preferred_element_type=jnp.float32)]
    all_to_all x1 -> x0, blocking collectives: 28.9 us -> none  [exchange(): return lax.all_to_all(x, AXES, split_axis=0, concat_axis=0, tiled=True)]
    unnamed x76 -> x67, local copies, waits for them, and re-layouts: 7.06 us -> 32.7 us
    pallas_call x1 -> x6, Pallas kernels: 67.1 us -> 86.3 us  [the longest x1 43.8 us: adjacency(): pl.pallas_call(lambda *refs: counts_kernel(half, panels, *refs), grid=(no...]
    all_to_all x5, waiting for transfers between devices: 46 us -> 53.6 us  [exchange(): return lax.all_to_all(x, AXES, split_axis=0, concat_axis=0, tiled=True)]
    concatenate x9 -> x2, local copies, waits for them, and re-layouts: 6.91 us -> 0.12 us  [per_device(): jnp.concatenate([request_rows[0] // 64, request_rows[0] % 64], axis=1)]
    all_to_all x5, starting transfers between devices: 37.6 us -> 41.6 us  [exchange(): return lax.all_to_all(x, AXES, split_axis=0, concat_axis=0, tiled=True)]
  transfers between devices with their start and end apart: 5 -> 5, of which waited for: 4 -> 4; matrix products, arithmetic and copies ran while one was open for 8% -> 4% of each run, Pallas kernels for 24% -> 21%
where the time goes in v2:
time: 242 us; the launch traced here: 240 us
  Pallas kernels  86.3 us (36%)
  waiting for transfers between devices  53.6 us (22%)
  local copies, waits for them, and re-layouts  41.9 us (17%)
  starting transfers between devices  41.6 us (17%)
  matrix products  7.91 us (3%)
  other arithmetic  7.14 us (3%)
    all_to_all x5, waiting for transfers between devices, exchange(): return lax.all_to_all(x, AXES, split_axis=0, concat_axis=0, tiled=True)  53.6 us
    pallas_call x1, Pallas kernels, adjacency(): pl.pallas_call(lambda *refs: counts_kernel(half, panels, *refs), grid=(no...  43.8 us
    all_to_all x5, starting transfers between devices, exchange(): return lax.all_to_all(x, AXES, split_axis=0, concat_axis=0, tiled=True)  41.6 us
    unnamed x67, local copies, waits for them, and re-layouts  32.7 us
    pallas_call x1, Pallas kernels, decode(): pl.pallas_call(decode_kernel, out_shape=(jax.ShapeDtypeStruct((pairs, 1),...  17.6 us
    pallas_call x1, Pallas kernels, encode(): pl.pallas_call(encode_kernel, grid=(node_rows // TILE,), out_shape=(jax.S...  11.5 us
    dot_general x2, matrix products, dot32(): return jnp.dot(a, b, preferred_element_type=jnp.float32)  7.91 us
    pallas_call x1, Pallas kernels, node_grads(): pl.pallas_call(node_grads_kernel, grid=(halo_rows // TILE,), out_shape=(j...  7.2 us
  transfers between devices with their start and end apart: 5, of which 4 were waited for; matrix products, arithmetic and copies ran while one was open for 4% of the time, Pallas kernels for 21%

profile of v2, /device:TPU:1, one launch (start us, length us, event | category | flops | bytes accessed | tf_op | source)
XLA Modules:
  0.0 240.2 jit_solution(9643576739054737718)
XLA Ops:
  0.6 0.9 copy.46
  1.8 0.8 copy.54
  3.0 3.9 %fusion.6 = bf16[2048,256]{1,0:T(8,128)(2,1)} fusion(f32[2048,256]{1,0:T(8,128)S(1)} %bitcast.65, bf16[2048,256]{1,0:T(8,128)(2,1)S(1)} %copy-done.5, s32[2048]{0:T(1024)S(1)} %eq.32), kind=kOutput, calls=%fused_computation.8 | convolution fusion | flops 2152726528 | bytes 4202496 | tf_op jit(solution)/shard_map/dot_general | solution.py:23
  6.9 11.5 %all-to-all-start = ((bf16[128,16,256]{2,1,0:T(8,128)(2,1)}), bf16[128,16,256]{2,1,0:T(8,128)(2,1)S(1)}, u32[]{:S(2)}, u32[]{:S(2)}) async-start(bf16[128,16,256]{2,1,0:T(8,128)(2,1)} %bitcast.5), calls=%async_computation | async-start | bytes 2097152 | tf_op jit(solution)/shard_map/all_to_all | solution.py:19
  19.4 43.8 %counts.1 = (bf16[2048,3072]{1,0:T(8,128)(2,1)S(1)}, f32[2048,128]{1,0:T(8,128)S(1)}, f32[8,2048]{1,0:T(8,128)S(1)}) custom-call(s32[16384]{0:T(1024)S(1)} %bitcast.62, s32[128,128]{1,0:T(8,128)S(1)} %get-tuple-element.27.refs_1_), custom_call_target="tpu_custom_call" | custom-call | flops 60000000 | bytes 16777216 | tf_op jit(solution)/shard_map/counts/pallas_call | solution.py:155
  63.2 4.6 %copy-done.13 = bf16[2048,3072]{1,0:T(8,128)(2,1)} copy-done((bf16[2048,3072]{1,0:T(8,128)(2,1)}, bf16[2048,3072]{1,0:T(8,128)(2,1)S(1)}, u32[]{:S(2)}) %copy-start.13) | copy-done | bytes 12582936
  67.9 0.9 copy-done.25
  68.9 0.6 reshape_reshape.8.want_ref
  69.5 1.1 slice_bitcast_fusion.2.arr_ref
  70.6 4.6 %copy-done.14 = bf16[2048,3072]{1,0:T(8,128)(2,1)S(1)} copy-done((bf16[2048,3072]{1,0:T(8,128)(2,1)S(1)}, bf16[2048,3072]{1,0:T(8,128)(2,1)}, u32[]{:S(2)}) %copy-start.14) | copy-done | bytes 12582936
  75.1 11.5 %encode.1 = (bf16[2048,256]{1,0:T(8,128)(2,1)S(1)}, bf16[2048,256]{1,0:T(8,128)(2,1)}) custom-call(bf16[2048,3072]{1,0:T(8,128)(2,1)S(1)} %copy-done.14, bf16[2048,256]{1,0:T(8,128)(2,1)S(1)} %copy-done.5, bf16[1024,256]{1,0:T(8,128)(2,1)S(1)} %slice_bitcast_fusion.2.arr_ref, f32[2048,128]{1,0:T(8,128)S(1)} %get-tuple-element.29.deg_ref, ...), custom_call_target="tpu_custom_call" | custom-call | flops 8000000000 | bytes 16777216 | tf_op jit(solution)/shard_map/encode/pallas_call | solution.py:209
  86.7 1.0 copy-done.23
  87.6 16.2 %all-to-all-start.1 = ((bf16[128,16,256]{2,1,0:T(8,128)(2,1)}), bf16[128,16,256]{2,1,0:T(8,128)(2,1)S(1)}, u32[]{:S(2)}, u32[]{:S(2)}) async-start(bf16[128,16,256]{2,1,0:T(8,128)(2,1)} %bitcast.11), calls=%async_computation.1 | async-start | bytes 2097152 | tf_op jit(solution)/shard_map/all_to_all | solution.py:19
  103.9 1.4 copy.51.endc_ref
  105.3 1.4 copy.52.wl_ref
  106.7 16.7 %all-to-all-done.1 = bf16[128,16,256]{2,1,0:T(8,128)(2,1)S(1)} async-done(((bf16[128,16,256]{2,1,0:T(8,128)(2,1)}), bf16[128,16,256]{2,1,0:T(8,128)(2,1)S(1)}, u32[]{:S(2)}, u32[]{:S(2)}) %all-to-all-start.1) | async-done | bytes 1048608 | tf_op jit(solution)/shard_map/all_to_all | solution.py:19
  123.4 1.2 copy-done
  124.6 1.2 copy-done.1
  125.9 0.9 copy-done.7
  126.8 0.7 copy-done.11
  127.5 0.7 copy-done.12
  128.2 17.6 %decode.1 = (f32[2048,1]{1,0:T(8,128)S(1)}, bf16[2048,256]{1,0:T(8,128)(2,1)S(1)}, bf16[512,256]{1,0:T(8,128)(2,1)S(1)}, f32[8,256]{1,0:T(8,128)S(1)}) custom-call(bf16[2048,256]{1,0:T(8,128)(2,1)S(1)} %bitcast.56, s32[2048,2]{1,0:T(8,128)S(1)} %copy-done, s32[2,2048]{1,0:T(2,128)S(1)} %bitcast.61, f32[2048,2]{1,0:T(8,128)S(1)} %copy-done.1, ...), custom_call_target="tpu_custom_call" | custom-call | flops 12000000000 | bytes 4194304 | tf_op jit(solution)/shard_map/decode/pallas_call | solution.py:298
  146.1 1.9 pad_maximum_fusion
  148.0 4.9 %all-to-all-start.2 = ((bf16[128,24,256]{2,1,0:T(8,128)(2,1)}), bf16[128,24,256]{2,1,0:T(8,128)(2,1)}, u32[]{:S(2)}, u32[]{:S(2)}) async-start(bf16[128,24,256]{2,1,0:T(8,128)(2,1)} %pad_maximum_fusion), calls=%async_computation.2 | async-start | bytes 3145728 | tf_op jit(solution)/shard_map/all_to_all | solution.py:19
  153.0 24.8 %all-to-all-done.2 = bf16[128,24,256]{2,1,0:T(8,128)(2,1)} async-done(((bf16[128,24,256]{2,1,0:T(8,128)(2,1)}), bf16[128,24,256]{2,1,0:T(8,128)(2,1)}, u32[]{:S(2)}, u32[]{:S(2)}) %all-to-all-start.2) | async-done | bytes 1572896 | tf_op jit(solution)/shard_map/all_to_all | solution.py:19
  177.9 1.2 convert_reduce_fusion
  179.1 1.3 slice.81
  180.4 4.6 %copy-done.15 = bf16[2048,3072]{1,0:T(8,128)(2,1)S(1)} copy-done((bf16[2048,3072]{1,0:T(8,128)(2,1)S(1)}, bf16[2048,3072]{1,0:T(8,128)(2,1)}, u32[]{:S(2)}) %copy-start.15) | copy-done | bytes 12582936
  185.0 1.2 copy-done.24
  186.2 7.2 %node_grads.1 = (bf16[2048,256]{1,0:T(8,128)(2,1)S(1)}, bf16[256,2048]{1,0:T(8,128)(2,1)S(1)}, bf16[512,256]{1,0:T(8,128)(2,1)S(1)}, bf16[1024,256]{1,0:T(8,128)(2,1)S(1)}) custom-call(bf16[2048,256]{1,0:T(8,128)(2,1)S(1)} %bitcast.57, s32[1,2048]{1,0:T(1,128)S(1)} %reshape_reshape.7.want_ref, bf16[2048,256]{1,0:T(8,128)(2,1)S(1)} %copy-done.6, ...), custom_call_target="tpu_custom_call" | custom-call | flops 6000000000 | bytes 8388608 | tf_op jit(solution)/shard_map/node_grads/pallas_call | solution.py:345
  193.4 1.0 copy-done.19
  194.4 1.0 copy-done.21
  195.5 1.4 pad_maximum_fusion.1
  196.9 5.0 %all-to-all-start.3 = ((bf16[128,16,256]{2,1,0:T(8,128)(2,1)}), bf16[128,16,256]{2,1,0:T(8,128)(2,1)}, u32[]{:S(2)}, u32[]{:S(2)}) async-start(bf16[128,16,256]{2,1,0:T(8,128)(2,1)} %pad_maximum_fusion.1), calls=%async_computation.3 | async-start | bytes 2097152 | tf_op jit(solution)/shard_map/all_to_all | solution.py:19
  202.1 0.9 reduce.1
  203.0 0.6 fusion.13
  203.6 4.6 %copy-done.16 = bf16[2048,3072]{1,0:T(8,128)(2,1)S(1)} copy-done((bf16[2048,3072]{1,0:T(8,128)(2,1)S(1)}, bf16[2048,3072]{1,0:T(8,128)(2,1)}, u32[]{:S(2)}) %copy-start.16) | copy-done | bytes 12582936
  208.2 1.2 copy-done.22
  209.4 5.9 %own_grads.1 = f32[2048,256]{1,0:T(8,128)S(1)} custom-call(bf16[2048,256]{1,0:T(8,128)(2,1)S(1)} %copy-done.20, bf16[256,2048]{1,0:T(8,128)(2,1)S(1)} %copy-done.22, bf16[256,256]{1,0:T(8,128)(2,1)S(1)} %copy-done.10, bf16[2048,3072]{1,0:T(8,128)(2,1)S(1)} %copy-done.16), custom_call_target="tpu_custom_call" | custom-call | flops 6000000000 | bytes 8388608 | tf_op jit(solution)/shard_map/own_grads/pallas_call | solution.py:384
  215.3 5.9 %all-to-all-done.3 = bf16[128,16,256]{2,1,0:T(8,128)(2,1)} async-done(((bf16[128,16,256]{2,1,0:T(8,128)(2,1)}), bf16[128,16,256]{2,1,0:T(8,128)(2,1)}, u32[]{:S(2)}, u32[]{:S(2)}) %all-to-all-start.3) | async-done | bytes 1048608 | tf_op jit(solution)/shard_map/all_to_all | solution.py:19
  221.2 1.5 slice_convert_fusion
  222.7 0.7 broadcast_in_dim.40
  223.4 4.0 %all-to-all-start.4 = ((bf16[128,8,128]{2,1,0:T(8,128)(2,1)}), bf16[128,8,128]{2,1,0:T(8,128)(2,1)S(1)}, u32[]{:S(2)}, u32[]{:S(2)}) async-start(bf16[128,8,128]{2,1,0:T(8,128)(2,1)} %broadcast_in_dim.40), calls=%async_computation.4 | async-start | bytes 524288 | tf_op jit(solution)/shard_map/all_to_all | solution.py:19
  227.5 1.0 reshape.120
  228.4 4.0 %fusion.5 = f32[2048,256]{1,0:T(8,128)} fusion(f32[2048,256]{1,0:T(8,128)S(1)} %own_grads.1, s32[1024]{0:T(1024)S(1)} %eq.37, bf16[128,16,256]{2,1,0:T(8,128)(2,1)} %all-to-all-done.3), kind=kOutput, calls=%fused_computation.7 | convolution fusion | flops 1076363264 | bytes 4722688 | tf_op jit(solution)/shard_map/dot_general | solution.py:23
  232.4 6.1 %all-to-all-done.4 = bf16[128,8,128]{2,1,0:T(8,128)(2,1)S(1)} async-done(((bf16[128,8,128]{2,1,0:T(8,128)(2,1)}), bf16[128,8,128]{2,1,0:T(8,128)(2,1)S(1)}, u32[]{:S(2)}, u32[]{:S(2)}) %all-to-all-start.4) | async-done | bytes 262176 | tf_op jit(solution)/shard_map/all_to_all | solution.py:19
  238.6 0.8 slice.69
  239.4 0.8 slice.71
  (74 shorter events, 1.9 us)
Async XLA Ops:
  0.6 2.4 copy-start.5
  6.9 12.2 %copy-start.2 = (s32[16384]{0:T(1024)S(1)}, s32[16384]{0:T(1024)}, u32[]{:S(2)}) copy-start(s32[16384]{0:T(1024)} %param.15) | copy-start | bytes 196612
  6.9 12.2 %copy-start.3 = (s32[16384]{0:T(1024)S(1)}, s32[16384]{0:T(1024)}, u32[]{:S(2)}) copy-start(s32[16384]{0:T(1024)} %param.16) | copy-start | bytes 196612
  6.9 63.6 %copy-start.8 = (bf16[256,256]{1,0:T(8,128)(2,1)S(1)}, bf16[256,256]{1,0:T(8,128)(2,1)}, u32[]{:S(2)}) copy-start(bf16[256,256]{1,0:T(8,128)(2,1)} %wn_ref.3) | copy-start | bytes 393220
  6.9 63.6 %copy-start.9 = (bf16[256,256]{1,0:T(8,128)(2,1)S(1)}, bf16[256,256]{1,0:T(8,128)(2,1)}, u32[]{:S(2)}) copy-start(bf16[256,256]{1,0:T(8,128)(2,1)} %ws_ref.3) | copy-start | bytes 393220
  6.9 60.9 %all-to-all-start = ((bf16[128,16,256]{2,1,0:T(8,128)(2,1)}), bf16[128,16,256]{2,1,0:T(8,128)(2,1)S(1)}, u32[]{:S(2)}, u32[]{:S(2)}) async-start(bf16[128,16,256]{2,1,0:T(8,128)(2,1)} %bitcast.5), calls=%async_computation | async-start | bytes 2097152 | tf_op jit(solution)/shard_map/all_to_all | solution.py:19
  63.2 4.6 %copy-start.13 = (bf16[2048,3072]{1,0:T(8,128)(2,1)}, bf16[2048,3072]{1,0:T(8,128)(2,1)S(1)}, u32[]{:S(2)}) copy-start(bf16[2048,3072]{1,0:T(8,128)(2,1)S(1)} %get-tuple-element.28.adj_ref) | copy-start | bytes 37748740
  67.8 18.9 %copy-start.17 = (f32[8,2048]{1,0:T(8,128)}, f32[8,2048]{1,0:T(8,128)S(1)}, u32[]{:S(2)}) copy-start(f32[8,2048]{1,0:T(8,128)S(1)} %get-tuple-element.36.degt_ref) | copy-start | bytes 196612
  67.8 1.0 copy-start.25
  68.9 17.8 %copy-start.26 = (s32[128,16]{1,0:T(8,128)}, s32[128,16]{1,0:T(8,128)S(1)}, u32[]{:S(2)}) copy-start(s32[128,16]{1,0:T(8,128)S(1)} %slice_add_fusion) | copy-start | bytes 24580
  70.6 4.6 %copy-start.14 = (bf16[2048,3072]{1,0:T(8,128)(2,1)S(1)}, bf16[2048,3072]{1,0:T(8,128)(2,1)}, u32[]{:S(2)}) copy-start(bf16[2048,3072]{1,0:T(8,128)(2,1)} %copy-done.13) | copy-start | bytes 37748740
  86.7 1.0 copy-start.23
  87.6 16.3 %copy-start.4 = (s32[2048,2]{0,1:T(2,128)S(1)}, s32[2048,2]{0,1:T(2,128)}, u32[]{:S(2)}) copy-start(s32[2048,2]{0,1:T(2,128)} %param.20) | copy-start | bytes 49156
  87.6 17.6 %copy-start.29 = (s32[2048]{0:T(1024)S(1)}, s32[2048]{0:T(1024)}, u32[]{:S(2)}) copy-start(s32[2048]{0:T(1024)} %param.21) | copy-start | bytes 24580
  87.6 17.6 %copy-start.30 = (f32[2048]{0:T(1024)S(1)}, f32[2048]{0:T(1024)}, u32[]{:S(2)}) copy-start(f32[2048]{0:T(1024)} %param.22) | copy-start | bytes 24580
  87.6 35.8 %all-to-all-start.1 = ((bf16[128,16,256]{2,1,0:T(8,128)(2,1)}), bf16[128,16,256]{2,1,0:T(8,128)(2,1)S(1)}, u32[]{:S(2)}, u32[]{:S(2)}) async-start(bf16[128,16,256]{2,1,0:T(8,128)(2,1)} %bitcast.11), calls=%async_computation.1 | async-start | bytes 2097152 | tf_op jit(solution)/shard_map/all_to_all | solution.py:19
  123.4 1.2 copy-start
  124.6 1.2 copy-start.1
  125.9 0.9 copy-start.7
  126.8 0.7 copy-start.11
  127.5 0.7 copy-start.12
  148.0 5.0 %copy-start.27 = (s32[128,16]{1,0:T(8,128)S(1)}, s32[128,16]{1,0:T(8,128)}, u32[]{:S(2)}) copy-start(s32[128,16]{1,0:T(8,128)} %copy-done.26) | copy-start | bytes 24580
  148.0 29.9 %all-to-all-start.2 = ((bf16[128,24,256]{2,1,0:T(8,128)(2,1)}), bf16[128,24,256]{2,1,0:T(8,128)(2,1)}, u32[]{:S(2)}, u32[]{:S(2)}) async-start(bf16[128,24,256]{2,1,0:T(8,128)(2,1)} %pad_maximum_fusion), calls=%async_computation.2 | async-start | bytes 3145728 | tf_op jit(solution)/shard_map/all_to_all | solution.py:19
  152.9 27.5 %copy-start.6 = (bf16[2048,256]{1,0:T(8,128)(2,1)S(1)}, bf16[2048,256]{1,0:T(8,128)(2,1)}, u32[]{:S(2)}) copy-start(bf16[2048,256]{1,0:T(8,128)(2,1)} %feat_ref.3) | copy-start | bytes 3145732
  152.9 27.5 %copy-start.18 = (f32[8,2048]{1,0:T(8,128)S(1)}, f32[8,2048]{1,0:T(8,128)}, u32[]{:S(2)}) copy-start(f32[8,2048]{1,0:T(8,128)} %copy-done.17) | copy-start | bytes 196612
  180.4 4.6 %copy-start.15 = (bf16[2048,3072]{1,0:T(8,128)(2,1)S(1)}, bf16[2048,3072]{1,0:T(8,128)(2,1)}, u32[]{:S(2)}) copy-start(bf16[2048,3072]{1,0:T(8,128)(2,1)} %copy-done.13) | copy-start | bytes 37748740
  185.0 1.2 copy-start.24
  193.4 1.0 copy-start.19
  194.4 1.0 copy-start.21
  195.5 6.4 %copy-start.28 = (s32[1,128,8]{1,2,0:T(8,128)S(1)}, s32[1,128,8]{1,2,0:T(8,128)}, u32[]{:S(2)}) copy-start(s32[1,128,8]{1,2,0:T(8,128)} %param.18) | copy-start | bytes 12292
  196.9 6.7 %copy-start.10 = (bf16[256,256]{1,0:T(8,128)(2,1)S(1)}, bf16[256,256]{1,0:T(8,128)(2,1)}, u32[]{:S(2)}) copy-start(bf16[256,256]{1,0:T(8,128)(2,1)} %ws_ref.3) | copy-start | bytes 393220
  196.9 6.7 %copy-start.20 = (bf16[2048,256]{1,0:T(8,128)(2,1)S(1)}, bf16[2048,256]{1,0:T(8,128)(2,1)}, u32[]{:S(2)}) copy-start(bf16[2048,256]{1,0:T(8,128)(2,1)} %copy-done.19) | copy-start | bytes 3145732
  196.9 24.3 %all-to-all-start.3 = ((bf16[128,16,256]{2,1,0:T(8,128)(2,1)}), bf16[128,16,256]{2,1,0:T(8,128)(2,1)}, u32[]{:S(2)}, u32[]{:S(2)}) async-start(bf16[128,16,256]{2,1,0:T(8,128)(2,1)} %pad_maximum_fusion.1), calls=%async_computation.3 | async-start | bytes 2097152 | tf_op jit(solution)/shard_map/all_to_all | solution.py:19
  203.6 4.6 %copy-start.16 = (bf16[2048,3072]{1,0:T(8,128)(2,1)S(1)}, bf16[2048,3072]{1,0:T(8,128)(2,1)}, u32[]{:S(2)}) copy-start(bf16[2048,3072]{1,0:T(8,128)(2,1)} %copy-done.13) | copy-start | bytes 37748740
  208.2 1.2 copy-start.22
  223.4 15.1 %all-to-all-start.4 = ((bf16[128,8,128]{2,1,0:T(8,128)(2,1)}), bf16[128,8,128]{2,1,0:T(8,128)(2,1)S(1)}, u32[]{:S(2)}, u32[]{:S(2)}) async-start(bf16[128,8,128]{2,1,0:T(8,128)(2,1)} %broadcast_in_dim.40), calls=%async_computation.4 | async-start | bytes 524288 | tf_op jit(solution)/shard_map/all_to_all | solution.py:19

commit v3 on v2

--- a/solution.py
+++ b/solution.py
@@ -7,8 +7,9 @@
 
 AXES = ("dom", "grp")
 LANES = 128
-STRIDE = 8
-GROUP = LANES // STRIDE
+GROUP = 8
+STRIDE = LANES // GROUP
+BATCH = 8
 TILE = 256
 CLASH = 1 << 20
 VMEM = pl.BlockSpec(memory_space=pltpu.VMEM)
@@ -47,6 +48,11 @@
     shape = (index.shape[0], count) if axis == 1 else (count, index.shape[1])
     ids = lax.broadcasted_iota(jnp.int32, shape, axis) + first
     return jnp.where(index == ids, 1.0, 0.0).astype(jnp.bfloat16)
+
+
+def column(ref, i):
+    rows = ref[:, tile_of(i)]
+    return jnp.transpose(jnp.broadcast_to(rows, (8, TILE)) if ref.shape[0] == 1 else rows)
 
 
 def slots_kernel(half, panels, count_ref, src_ref, dst_ref, row_ref, unit_ref):
@@ -58,7 +64,7 @@
     dst = dst_ref[...]
     upper = jnp.where(dst >= half, 1, 0)
     row = jnp.right_shift(src, 7) * half + dst - upper * half
-    row = jnp.where(live, row, half * panels + jnp.right_shift(lane, 3))
+    row = jnp.where(live, row, half * panels + lane // STRIDE)
     unit_ref[...] = jnp.where(live, jnp.bitwise_and(src, LANES - 1) + upper * LANES, 2 * LANES)
     clash = jnp.zeros((chunks, LANES), jnp.int32)
     for k in range(1, GROUP // 2 + 1):
@@ -67,73 +73,85 @@
     row_ref[...] = row + jnp.where(any_clash & (lane == 0), CLASH, 0)
 
 
-def counts_kernel(half, panels, row_ref, unit_ref, adj_ref, deg_ref, degt_ref, words, units):
+def counts_kernel(half, panels, row_ref, unit_ref, adj_ref, deg_ref, degt_ref, even, odd, units):
     step = pl.program_id(0)
     chunks = unit_ref.shape[0]
 
     @pl.when(step == 0)
     def _():
-        def zero(i, carry):
-            words[tile_of(i), :] = jnp.zeros((TILE, LANES), jnp.int32)
+        lane = lax.broadcasted_iota(jnp.int32, (LANES, LANES), 1)
+        share = half * panels // (chunks // BATCH)
+
+        def prepare(i, carry):
+            part = pl.ds(pl.multiple_of(i * share, share), share)
+            for k in range(BATCH):
+                c = i * BATCH + k
+                wide = jnp.transpose(
+                    jnp.broadcast_to(unit_ref[pl.ds(c, 1), :], (LANES, LANES))
+                )
+                units[pl.ds(pl.multiple_of(c * LANES, LANES), LANES), :] = jnp.where(
+                    wide == lane, 1, jnp.where(wide == lane + LANES, 65536, 0)
+                )
+            even[part, :] = jnp.zeros((share, LANES), jnp.int32)
+            odd[part, :] = jnp.zeros((share, LANES), jnp.int32)
             return carry
 
-        lax.fori_loop(0, half * panels // TILE, zero, 0)
-        lane = lax.broadcasted_iota(jnp.int32, (LANES, LANES), 1)
-
-        def fill(c):
-            wide = jnp.transpose(
-                jnp.broadcast_to(unit_ref[pl.ds(c, 1), :], (LANES, LANES))
-            )
-            return jnp.where(wide == lane, 1, jnp.where(wide == lane + LANES, 65536, 0))
-
-        units[0:LANES, :] = fill(0)
+        lax.fori_loop(0, chunks // BATCH, prepare, 0)
 
         def chunk(c, carry):
-            now = pl.multiple_of(lax.rem(c, 2) * LANES, LANES)
-            later = pl.multiple_of(lax.rem(c + 1, 2) * LANES, LANES)
-            base = c * LANES
-            head = row_ref[base]
-            nxt = fill(jnp.minimum(c + 1, chunks - 1))
+            base = pl.multiple_of(c * LANES, LANES)
+            places = row_ref.at[pl.ds(base, LANES)]
+            head = places[0]
+
+            def load(s):
+                words = odd if s % 2 else even
+                at = [places[s + STRIDE * t] for t in range(GROUP)]
+                new = [
+                    words[pl.ds(a, 1), :] + units[pl.ds(base + (s + STRIDE * t), 1), :]
+                    for t, a in enumerate(at)
+                ]
+                return words, at, new
+
+            def store(words, at, new):
+                for a, n in zip(at, new):
+                    words[pl.ds(a, 1), :] = n
 
             @pl.when(head < CLASH)
             def _():
-                for s in range(STRIDE):
-                    places = [s + STRIDE * t for t in range(GROUP)]
-                    at = [row_ref[base + j] for j in places]
-                    new = [
-                        words[pl.ds(a, 1), :] + units[pl.ds(now + j, 1), :]
-                        for a, j in zip(at, places)
-                    ]
-                    for a, n in zip(at, new):
-                        words[pl.ds(a, 1), :] = n
+                held = load(0)
+                for s in range(1, STRIDE):
+                    following = load(s)
+                    store(*held)
+                    held = following
+                store(*held)
 
             @pl.when(head >= CLASH)
             def _():
-                def one(j, carry):
-                    a = jnp.bitwise_and(row_ref[base + j], CLASH - 1)
-                    words[pl.ds(a, 1), :] = words[pl.ds(a, 1), :] + units[pl.ds(now + j, 1), :]
-                    return carry
-
-                lax.fori_loop(0, LANES, one, 0)
-
-            units[pl.ds(later, LANES), :] = nxt
+                for j in range(LANES):
+                    words = odd if j % 2 else even
+                    a = places[j]
+                    if j == 0:
+                        a = a - CLASH
+                    words[pl.ds(a, 1), :] = words[pl.ds(a, 1), :] + units[pl.ds(base + j, 1), :]
+
             return carry
 
         lax.fori_loop(0, chunks, chunk, 0)
 
-    per_half = half // TILE
-    shift = jnp.where(step >= per_half, 16, 0)
-    first = lax.rem(step, per_half) * TILE
+    first = step * TILE
     total = jnp.zeros((TILE, LANES), jnp.int32)
     for p in range(panels):
-        word = words[pl.ds(pl.multiple_of(p * half + first, TILE), TILE), :]
-        count = jnp.bitwise_and(jnp.right_shift(word, shift), 0xFFFF)
-        total = total + count
-        adj_ref[:, p * LANES : (p + 1) * LANES] = count.astype(jnp.float32).astype(jnp.bfloat16)
-    degree = jnp.sum(total.astype(jnp.float32), axis=1, keepdims=True)
-    wide = jnp.broadcast_to(jnp.maximum(degree, 1.0), (TILE, LANES))
-    deg_ref[...] = wide
-    degt_ref[...] = jnp.transpose(wide)[:8]
+        part = pl.ds(pl.multiple_of(p * half + first, TILE), TILE)
+        word = even[part, :] + odd[part, :]
+        total = total + word
+        cols = slice(p * LANES, (p + 1) * LANES)
+        for h, count in enumerate((jnp.bitwise_and(word, 0xFFFF), jnp.right_shift(word, 16))):
+            adj_ref[h, :, cols] = count.astype(jnp.float32).astype(jnp.bfloat16)
+    for h, count in enumerate((jnp.bitwise_and(total, 0xFFFF), jnp.right_shift(total, 16))):
+        degree = jnp.sum(count.astype(jnp.float32), axis=1, keepdims=True)
+        wide = jnp.broadcast_to(jnp.maximum(degree, 1.0), (TILE, LANES))
+        deg_ref[h] = wide
+        degt_ref[h] = jnp.transpose(wide)[:8]
 
 
 def adjacency(edge_src, edge_dst, edge_count, node_rows, table_rows):
@@ -149,31 +167,33 @@
         ),
         in_specs=[SMEM, VMEM, VMEM],
         out_specs=(VMEM, VMEM),
-        compiler_params=params(8),
+        compiler_params=params(60),
         name="slots",
     )(edge_count, edge_src.reshape(grid_shape), edge_dst.reshape(grid_shape))
-    return pl.pallas_call(
+    adj, deg, degt = pl.pallas_call(
         lambda *refs: counts_kernel(half, panels, *refs),
-        grid=(node_rows // TILE,),
+        grid=(half // TILE,),
         out_shape=(
-            jax.ShapeDtypeStruct((node_rows, table_rows), jnp.bfloat16),
-            jax.ShapeDtypeStruct((node_rows, LANES), jnp.float32),
-            jax.ShapeDtypeStruct((8, node_rows), jnp.float32),
+            jax.ShapeDtypeStruct((2, half, table_rows), jnp.bfloat16),
+            jax.ShapeDtypeStruct((2, half, LANES), jnp.float32),
+            jax.ShapeDtypeStruct((2, 8, half), jnp.float32),
         ),
         in_specs=[SMEM, pl.BlockSpec(grid_shape, lambda i: (0, 0))],
         out_specs=(
-            pl.BlockSpec((TILE, table_rows), lambda i: (i, 0)),
-            pl.BlockSpec((TILE, LANES), lambda i: (i, 0)),
-            pl.BlockSpec((8, TILE), lambda i: (0, i)),
+            pl.BlockSpec((2, TILE, table_rows), lambda i: (0, i, 0)),
+            pl.BlockSpec((2, TILE, LANES), lambda i: (0, i, 0)),
+            pl.BlockSpec((2, 8, TILE), lambda i: (0, 0, i)),
         ),
         scratch_shapes=[
             pltpu.VMEM((half * panels + GROUP, LANES), jnp.int32),
-            pltpu.VMEM((2 * LANES, LANES), jnp.int32),
+            pltpu.VMEM((half * panels + GROUP, LANES), jnp.int32),
+            pltpu.VMEM((edge_src.shape[0], LANES), jnp.int32),
         ],
-        compiler_params=params(24),
+        compiler_params=params(60),
         cost_estimate=cost(60_000_000, 16 * 2**20),
         name="counts",
     )(row.reshape(-1), unit)
+    return adj.reshape(node_rows, table_rows), deg.reshape(node_rows, LANES), degt
 
 
 def encode_kernel(
@@ -194,17 +214,17 @@
     @pl.when(step == pl.num_programs(0) - 1)
     def _():
         def serve(j, carry):
-            hot = pick(want_ref[tile_of(j), :], 0, node_rows, 1)
+            hot = pick(column(want_ref, j)[:, :1], 0, node_rows, 1)
             served_ref[tile_of(j), :] = dot32(hot, emb[...]).astype(jnp.bfloat16)
             return carry
 
-        lax.fori_loop(0, served_ref.shape[0] // TILE, serve, 0)
-
-
-def encode(adj, features, arrived, deg, w_self, w_neigh, want_col):
+        lax.fori_loop(0, served_ref.shape[0] // TILE, serve, 0, unroll=2)
+
+
+def encode(adj, features, arrived, deg, w_self, w_neigh, want_row):
     node_rows, width = features.shape
     table_rows = adj.shape[1]
-    recv_rows = want_col.shape[0]
+    recv_rows = want_row.shape[1]
     whole = lambda a: pl.BlockSpec(a.shape, lambda i: (0, 0))
     return pl.pallas_call(
         encode_kernel,
@@ -220,24 +240,22 @@
             pl.BlockSpec((TILE, LANES), lambda i: (i, 0)),
             whole(w_self),
             whole(w_neigh),
-            whole(want_col),
+            whole(want_row),
         ],
         out_specs=(
             pl.BlockSpec((TILE, width), lambda i: (i, 0)),
             pl.BlockSpec((recv_rows, width), lambda i: (0, 0)),
         ),
         scratch_shapes=[pltpu.VMEM((node_rows, width), jnp.bfloat16)],
-        compiler_params=params(24),
+        compiler_params=params(60),
         cost_estimate=cost(8_000_000_000, 16 * 2**20),
         name="encode",
-    )(adj, features, arrived, deg, w_self, w_neigh, want_col)
+    )(adj, features, arrived, deg, w_self, w_neigh, want_row)
 
 
 def decode_kernel(
     recv_ref,
-    endc_ref,
-    endr_ref,
-    wl_ref,
+    pair_ref,
     wh_ref,
     bias_ref,
     wo_ref,
@@ -251,21 +269,21 @@
     pgl_s,
     pgr_s,
 ):
-    pairs = endc_ref.shape[0]
+    pairs = pair_ref.shape[1]
     recv_rows, width = recv_ref.shape
     gsmall_ref[...] = jnp.zeros(gsmall_ref.shape, jnp.float32)
 
     def forward(i, carry):
         at = tile_of(i)
-        ends = endc_ref[at, :]
+        cols = column(pair_ref, i)
+        ends = cols[:, 0:2].astype(jnp.int32)
         left = dot32(pick(ends[:, 0:1], 0, recv_rows, 1), recv_ref[...]).astype(jnp.bfloat16)
         right = dot32(pick(ends[:, 1:2], 0, recv_rows, 1), recv_ref[...]).astype(jnp.bfloat16)
         pre = dot32(left, wh_ref[:width, :]) + dot32(right, wh_ref[width:, :]) + bias_ref[...]
         hidden = jnp.maximum(pre, 0.0)
         logit = jnp.sum(hidden * wo_ref[...], axis=1, keepdims=True)
         logit_ref[at, :] = logit
-        wl = wl_ref[at, :]
-        slope = wl[:, 0:1] * (jax.nn.sigmoid(logit) - wl[:, 1:2])
+        slope = cols[:, 2:3] * (jax.nn.sigmoid(logit) - cols[:, 3:4])
         delta = jnp.where(pre > 0, slope * wo_ref[...], 0.0)
         gsmall_ref[0:1, :] += jnp.sum(delta, axis=0, keepdims=True)
         gsmall_ref[1:2, :] += jnp.sum(slope * hidden, axis=0, keepdims=True)
@@ -277,23 +295,25 @@
         pgr_s[at, :] = dot_nt(delta_b, wh_ref[width:, :]).astype(jnp.bfloat16)
         return carry
 
-    lax.fori_loop(0, pairs // TILE, forward, 0)
+    lax.fori_loop(0, pairs // TILE, forward, 0, unroll=2)
+
+    ends = pair_ref[0:2, :].astype(jnp.int32)
 
     def backward(i, carry):
-        total = dot32(pick(endr_ref[0:1, :], i * TILE, TILE, 0), pgl_s[...]) + dot32(
-            pick(endr_ref[1:2, :], i * TILE, TILE, 0), pgr_s[...]
+        total = dot32(pick(ends[0:1, :], i * TILE, TILE, 0), pgl_s[...]) + dot32(
+            pick(ends[1:2, :], i * TILE, TILE, 0), pgr_s[...]
         )
         rgrad_ref[tile_of(i), :] = total.astype(jnp.bfloat16)
         return carry
 
-    lax.fori_loop(0, recv_rows // TILE, backward, 0)
+    lax.fori_loop(0, recv_rows // TILE, backward, 0, unroll=2)
     ghid_ref[:width, :] = dot_tn(left_s[...], delta_s[...]).astype(jnp.bfloat16)
     ghid_ref[width:, :] = dot_tn(right_s[...], delta_s[...]).astype(jnp.bfloat16)
 
 
-def decode(received, end_cols, end_rows, wl_cols, w_hidden, bias, w_out):
+def decode(received, pair_rows, w_hidden, bias, w_out):
     recv_rows, width = received.shape
-    pairs = end_cols.shape[0]
+    pairs = pair_rows.shape[1]
     scratch = pltpu.VMEM((pairs, width), jnp.bfloat16)
     return pl.pallas_call(
         decode_kernel,
@@ -303,13 +323,13 @@
             jax.ShapeDtypeStruct((2 * width, width), jnp.bfloat16),
             jax.ShapeDtypeStruct((8, width), jnp.float32),
         ),
-        in_specs=[VMEM] * 7,
+        in_specs=[VMEM] * 5,
         out_specs=(VMEM,) * 4,
         scratch_shapes=[scratch] * 5,
-        compiler_params=params(32),
+        compiler_params=params(60),
         cost_estimate=cost(12_000_000_000, 4 * 2**20),
         name="decode",
-    )(received, end_cols, end_rows, wl_cols, w_hidden, bias, w_out)
+    )(received, pair_rows, w_hidden, bias, w_out)
 
 
 def node_grads_kernel(
@@ -326,12 +346,13 @@
             gradb_ref[tile_of(i), :] = dot32(hot, back_ref[...]).astype(jnp.bfloat16)
             return carry
 
-        lax.fori_loop(0, node_rows // TILE, put, 0)
+        lax.fori_loop(0, node_rows // TILE, put, 0, unroll=2)
         gw_ref[:width, :] = dot_tn(feat_ref[...], gradb_ref[...]).astype(jnp.bfloat16)
         gw_ref[width:, :] = dot_tn(agg_ref[...], gradb_ref[...]).astype(jnp.bfloat16)
-        gt_ref[...] = (dot_nt(wn_ref[...], gradb_ref[...]) / degt_ref[0:1, :]).astype(
-            jnp.bfloat16
-        )
+        gt_ref[...] = (
+            dot_nt(wn_ref[...], gradb_ref[...])
+            / jnp.concatenate([degt_ref[0, 0:1, :], degt_ref[1, 0:1, :]], axis=1)
+        ).astype(jnp.bfloat16)
 
     halo_ref[...] = jnp.transpose(dot32(gt_ref[...], adj_ref[...])).astype(jnp.bfloat16)
 
@@ -357,7 +378,7 @@
             whole(features),
             whole(aggregate),
             whole(w_neigh),
-            whole(degt),
+            pl.BlockSpec(degt.shape, lambda i: (0, 0, 0)),
             pl.BlockSpec((node_rows, TILE), lambda i: (0, i + skip)),
         ],
         out_specs=(
@@ -366,7 +387,7 @@
             pl.BlockSpec((2 * width, width), fixed),
             pl.BlockSpec((TILE, width), lambda i: (i, 0)),
         ),
-        compiler_params=params(24),
+        compiler_params=params(60),
         cost_estimate=cost(6_000_000_000, 8 * 2**20),
         name="node_grads",
     )(back, want_row, features, aggregate, w_neigh, degt, adj)
@@ -392,7 +413,7 @@
             pl.BlockSpec((node_rows, TILE), lambda i: (0, i)),
         ],
         out_specs=pl.BlockSpec((TILE, width), lambda i: (i, 0)),
-        compiler_params=params(24),
+        compiler_params=params(60),
         cost_estimate=cost(6_000_000_000, 8 * 2**20),
         name="own_grads",
     )(grad_b, grad_t, w_self, adj)
@@ -438,14 +459,21 @@
     arrived = first[:, :halo_len].reshape(halo_rows, width)
     codes = first[:, halo_len, : 2 * req_len].astype(jnp.int32)
     wanted = (codes[:, :req_len] * 64 + codes[:, req_len:]).reshape(recv_rows)
-    want_col = wanted.reshape(recv_rows, 1)
     want_row = wanted.reshape(1, recv_rows)
-    aggregate, served = encode(adj, features, arrived, deg, w_self, w_neigh, want_col)
+    aggregate, served = encode(adj, features, arrived, deg, w_self, w_neigh, want_row)
     received = exchange(served.reshape(peers, req_len, width)).reshape(recv_rows, width)
 
-    wl_cols = jnp.stack([pair_weight, labels.astype(jnp.float32)], axis=1)
+    pair_rows = jnp.concatenate(
+        [
+            pair_ends.T.astype(jnp.float32),
+            pair_weight[None],
+            labels.astype(jnp.float32)[None],
+            jnp.zeros((4, pair_weight.shape[0]), jnp.float32),
+        ],
+        axis=0,
+    )
     logits, received_grad, grad_hidden, small = decode(
-        received, pair_ends, pair_ends.T, wl_cols, w_hidden, b_hidden[None], w_out[None]
+        received, pair_rows, w_hidden, b_hidden[None], w_out[None]
     )
     small = small[:2]
     small_hi = small.astype(jnp.bfloat16)

time: 242 us -> 209 us (0.86)
  local copies, waits for them, and re-layouts: 41.9 us -> 12.2 us
  blocking collectives: 0 us -> 28.9 us
  waiting for transfers between devices: 53.6 us -> 33.5 us
  starting transfers between devices: 41.6 us -> 29.3 us
    unnamed x67 -> x18, local copies, waits for them, and re-layouts: 32.7 us -> 2.89 us
    all_to_all x0 -> x1, blocking collectives: none -> 28.9 us  [exchange(): return lax.all_to_all(x, AXES, split_axis=0, concat_axis=0, tiled=True)]
    all_to_all x5 -> x4, waiting for transfers between devices: 53.6 us -> 33.5 us  [exchange(): return lax.all_to_all(x, AXES, split_axis=0, concat_axis=0, tiled=True)]
    pallas_call x1, Pallas kernels: 43.8 us -> 30.1 us  [adjacency(): pl.pallas_call(lambda *refs: counts_kernel(half, panels, *refs), grid=(ha...]
    all_to_all x5 -> x4, starting transfers between devices: 41.6 us -> 29.3 us  [exchange(): return lax.all_to_all(x, AXES, split_axis=0, concat_axis=0, tiled=True)]
    pallas_call x1, Pallas kernels: 11.5 us -> 15.7 us  [encode(): pl.pallas_call(encode_kernel, grid=(node_rows // TILE,), out_shape=(jax.S...]
    pallas_call x1, Pallas kernels: 5.87 us -> 9.66 us  [own_grads(): pl.pallas_call(own_grads_kernel, grid=(node_rows // TILE,), out_shape=jax...]
    pallas_call x1, Pallas kernels: 7.2 us -> 10 us  [node_grads(): pl.pallas_call(node_grads_kernel, grid=(halo_rows // TILE,), out_shape=(j...]
  transfers between devices with their start and end apart: 5 -> 4, of which waited for: 4 -> 3; matrix products, arithmetic and copies ran while one was open for 4% -> 3% of each run, Pallas kernels for 21% -> 20%
where the time goes in v3:
time: 209 us; the launch traced here: 208 us
  Pallas kernels  86.4 us (41%)
  waiting for transfers between devices  33.5 us (16%)
  starting transfers between devices  29.3 us (14%)
  blocking collectives  28.9 us (14%)
  local copies, waits for them, and re-layouts  12.2 us (6%)
  matrix products  8.51 us (4%)
  other arithmetic  7.57 us (4%)
    all_to_all x4, waiting for transfers between devices, exchange(): return lax.all_to_all(x, AXES, split_axis=0, concat_axis=0, tiled=True)  33.5 us
    pallas_call x1, Pallas kernels, adjacency(): pl.pallas_call(lambda *refs: counts_kernel(half, panels, *refs), grid=(ha...  30.1 us
    all_to_all x4, starting transfers between devices, exchange(): return lax.all_to_all(x, AXES, split_axis=0, concat_axis=0, tiled=True)  29.3 us
    all_to_all x1, blocking collectives, exchange(): return lax.all_to_all(x, AXES, split_axis=0, concat_axis=0, tiled=True)  28.9 us
    pallas_call x1, Pallas kernels, decode(): pl.pallas_call(decode_kernel, out_shape=(jax.ShapeDtypeStruct((pairs, 1),...  19.2 us
    pallas_call x1, Pallas kernels, encode(): pl.pallas_call(encode_kernel, grid=(node_rows // TILE,), out_shape=(jax.S...  15.7 us
    pallas_call x1, Pallas kernels, node_grads(): pl.pallas_call(node_grads_kernel, grid=(halo_rows // TILE,), out_shape=(j...  10 us
    pallas_call x1, Pallas kernels, own_grads(): pl.pallas_call(own_grads_kernel, grid=(node_rows // TILE,), out_shape=jax...  9.66 us
  transfers between devices with their start and end apart: 4, of which 3 were waited for; matrix products, arithmetic and copies ran while one was open for 3% of the time, Pallas kernels for 20%

profile of v3, /device:TPU:1, one launch (start us, length us, event | category | flops | bytes accessed | tf_op | source)
XLA Modules:
  0.0 207.8 jit_solution(15223218252020206665)
XLA Ops:
  0.6 0.9 copy.36
  1.5 0.8 copy.41
  2.3 0.1 eq.32
  2.4 0.1 fusion.7
  2.5 0.1 copy.38
  2.6 0.1 copy.42
  2.7 0.3 pad.9.clone
  3.0 3.9 %fusion.6 = bf16[2048,256]{1,0:T(8,128)(2,1)} fusion(f32[2048,256]{1,0:T(8,128)S(1)} %bitcast.58, bf16[2048,256]{1,0:T(8,128)(2,1)S(1)} %copy-done.6, s32[2048]{0:T(1024)S(1)} %eq.32), kind=kOutput, calls=%fused_computation.8 | convolution fusion | flops 2152726528 | bytes 4202496 | tf_op jit(solution)/shard_map/dot_general | solution.py:24
  6.9 11.5 %all-to-all-start = ((bf16[128,16,256]{2,1,0:T(8,128)(2,1)}), bf16[128,16,256]{2,1,0:T(8,128)(2,1)S(1)}, u32[]{:S(2)}, u32[]{:S(2)}) async-start(bf16[128,16,256]{2,1,0:T(8,128)(2,1)} %bitcast.5), calls=%async_computation | async-start | bytes 2097152 | tf_op jit(solution)/shard_map/all_to_all | solution.py:20
  19.1 1.7 slots.1
  20.8 30.1 %counts.1 = (bf16[2,1024,3072]{2,1,0:T(8,128)(2,1)}, f32[2,1024,128]{2,1,0:T(8,128)}, f32[2,8,1024]{2,1,0:T(8,128)}) custom-call(s32[16384]{0:T(1024)} %bitcast.72, s32[128,128]{1,0:T(8,128)} %get-tuple-element.27.refs_1_), custom_call_target="tpu_custom_call" | custom-call | flops 60000000 | bytes 16777216 | tf_op jit(solution)/shard_map/counts/pallas_call | solution.py:173
  51.0 0.1 slice_add_fusion
  51.1 0.7 reshape_reshape.3.want_ref
  51.8 0.8 slice_bitcast_fusion.2.arr_ref
  52.6 15.7 %encode.1 = (bf16[2048,256]{1,0:T(8,128)(2,1)}, bf16[2048,256]{1,0:T(8,128)(2,1)}) custom-call(bf16[2048,3072]{1,0:T(8,128)(2,1)} %bitcast.75, bf16[2048,256]{1,0:T(8,128)(2,1)} %feat_ref.3, bf16[1024,256]{1,0:T(8,128)(2,1)} %slice_bitcast_fusion.2.arr_ref, f32[2048,128]{1,0:T(8,128)} %bitcast.78, bf16[256,256]{1,0:T(8,128)(2,1)} %ws_ref.3, ...), custom_call_target="tpu_custom_call" | custom-call | flops 8000000000 | bytes 16777216 | tf_op jit(solution)/shard_map/encode/pallas_call | solution.py:229
  68.3 10.1 %all-to-all-start.1 = ((bf16[128,16,256]{2,1,0:T(8,128)(2,1)}), bf16[128,16,256]{2,1,0:T(8,128)(2,1)S(1)}, u32[]{:S(2)}, u32[]{:S(2)}) async-start(bf16[128,16,256]{2,1,0:T(8,128)(2,1)} %bitcast.61), calls=%async_computation.1 | async-start | bytes 2097152 | tf_op jit(solution)/shard_map/all_to_all | solution.py:20
  78.4 0.1 pad.20.clone
  78.5 0.7 maximum_maximum_fusion.pair_ref
  79.2 18.7 %all-to-all-done.1 = bf16[128,16,256]{2,1,0:T(8,128)(2,1)S(1)} async-done(((bf16[128,16,256]{2,1,0:T(8,128)(2,1)}), bf16[128,16,256]{2,1,0:T(8,128)(2,1)S(1)}, u32[]{:S(2)}, u32[]{:S(2)}) %all-to-all-start.1) | async-done | bytes 1048608 | tf_op jit(solution)/shard_map/all_to_all | solution.py:20
  97.9 1.0 copy-done.1
  98.9 19.2 %decode.1 = (f32[2048,1]{1,0:T(8,128)}, bf16[2048,256]{1,0:T(8,128)(2,1)}, bf16[512,256]{1,0:T(8,128)(2,1)}, f32[8,256]{1,0:T(8,128)}) custom-call(bf16[2048,256]{1,0:T(8,128)(2,1)} %bitcast.60, f32[8,2048]{1,0:T(8,128)} %maximum_maximum_fusion.pair_ref, bf16[512,256]{1,0:T(8,128)(2,1)} %wh_ref.1, f32[1,256]{1,0:T(1,128)} %bitcast.73, f32[1,256]{1,0:T(1,128)} %bitcast.74), custom_call_target="tpu_custom_call" | custom-call | flops 12000000000 | bytes 4194304 | tf_op jit(solution)/shard_map/decode/pallas_call | solution.py:318
  118.1 0.8 subtract_convert_fusion
  118.9 1.0 reshape.122
  119.9 0.1 broadcast_in_dim.49
  120.0 0.1 broadcast_in_dim.48
  120.1 2.0 pad_maximum_fusion
  122.1 28.9 %all_to_all.25 = bf16[128,24,256]{2,1,0:T(8,128)(2,1)S(1)} all-to-all(bf16[128,24,256]{2,1,0:T(8,128)(2,1)S(1)} %pad_maximum_fusion), channel_id=1, replica_groups=mesh['dom'=32,'grp'=4] {'dom','grp'}, dimensions={0} | all-to-all | bytes 3145728 | tf_op jit(solution)/shard_map/all_to_all | solution.py:20
  151.0 0.1 convert_reduce_fusion
  151.1 1.1 slice.81
  152.2 10.0 %node_grads.1 = (bf16[2048,256]{1,0:T(8,128)(2,1)}, bf16[256,2048]{1,0:T(8,128)(2,1)}, bf16[512,256]{1,0:T(8,128)(2,1)}, bf16[1024,256]{1,0:T(8,128)(2,1)}) custom-call(bf16[2048,256]{1,0:T(8,128)(2,1)} %bitcast.62, s32[1,2048]{1,0:T(1,128)} %reshape_reshape.3.want_ref, bf16[2048,256]{1,0:T(8,128)(2,1)} %feat_ref.3, ...), custom_call_target="tpu_custom_call" | custom-call | flops 6000000000 | bytes 8388608 | tf_op jit(solution)/shard_map/node_grads/pallas_call | solution.py:366
  162.2 1.0 reshape.125
  163.2 0.1 broadcast_in_dim.50
  163.3 2.5 %pad_maximum_fusion.1 = bf16[128,16,256]{2,1,0:T(8,128)(2,1)} fusion(bf16[128,4,256]{2,1,0:T(4,128)(2,1)S(1)} %broadcast_in_dim.50, bf16[128,4,256]{2,1,0:T(4,128)(2,1)S(1)} %reshape.125, bf16[128,8,256]{2,1,0:T(8,128)(2,1)} %bitcast.64), kind=kLoop, calls=%fused_computation.10 | loop fusion | flops 3145728 | bytes 2097152 | tf_op jit(solution)/shard_map/concatenate | solution.py:502
  165.8 3.8 %all-to-all-start.3 = ((bf16[128,16,256]{2,1,0:T(8,128)(2,1)}), bf16[128,16,256]{2,1,0:T(8,128)(2,1)S(1)}, u32[]{:S(2)}, u32[]{:S(2)}) async-start(bf16[128,16,256]{2,1,0:T(8,128)(2,1)} %pad_maximum_fusion.1), calls=%async_computation.3 | async-start | bytes 2097152 | tf_op jit(solution)/shard_map/all_to_all | solution.py:20
  169.6 0.1 copy.40
  169.7 0.1 eq.37
  169.8 0.9 reduce.1
  170.8 0.6 fusion.13
  171.4 9.7 %own_grads.1 = f32[2048,256]{1,0:T(8,128)} custom-call(bf16[2048,256]{1,0:T(8,128)(2,1)} %get-tuple-element.37.gradb_ref, bf16[256,2048]{1,0:T(8,128)(2,1)} %get-tuple-element.38.gt_ref, bf16[256,256]{1,0:T(8,128)(2,1)} %ws_ref.3, bf16[2048,3072]{1,0:T(8,128)(2,1)} %bitcast.77), custom_call_target="tpu_custom_call" | custom-call | flops 6000000000 | bytes 8388608 | tf_op jit(solution)/shard_map/own_grads/pallas_call | solution.py:405
  181.0 8.3 %all-to-all-done.3 = bf16[128,16,256]{2,1,0:T(8,128)(2,1)S(1)} async-done(((bf16[128,16,256]{2,1,0:T(8,128)(2,1)}), bf16[128,16,256]{2,1,0:T(8,128)(2,1)S(1)}, u32[]{:S(2)}, u32[]{:S(2)}) %all-to-all-start.3) | async-done | bytes 1048608 | tf_op jit(solution)/shard_map/all_to_all | solution.py:20
  189.3 0.2 slice_convert_fusion
  189.5 1.0 reshape.128
  190.5 0.7 broadcast_in_dim.52
  191.2 3.9 %all-to-all-start.4 = ((bf16[128,8,128]{2,1,0:T(8,128)(2,1)}), bf16[128,8,128]{2,1,0:T(8,128)(2,1)S(1)}, u32[]{:S(2)}, u32[]{:S(2)}) async-start(bf16[128,8,128]{2,1,0:T(8,128)(2,1)} %broadcast_in_dim.52), calls=%async_computation.4 | async-start | bytes 524288 | tf_op jit(solution)/shard_map/all_to_all | solution.py:20
  195.1 4.6 %fusion.5 = f32[2048,256]{1,0:T(8,128)} fusion(f32[2048,256]{1,0:T(8,128)} %own_grads.1, s32[1024]{0:T(1024)S(1)} %eq.37, bf16[128,16,256]{2,1,0:T(8,128)(2,1)S(1)} %all-to-all-done.3), kind=kOutput, calls=%fused_computation.7 | convolution fusion | flops 1076363264 | bytes 4722688 | tf_op jit(solution)/shard_map/dot_general | solution.py:24
  199.7 6.5 %all-to-all-done.4 = bf16[128,8,128]{2,1,0:T(8,128)(2,1)S(1)} async-done(((bf16[128,8,128]{2,1,0:T(8,128)(2,1)}), bf16[128,8,128]{2,1,0:T(8,128)(2,1)S(1)}, u32[]{:S(2)}, u32[]{:S(2)}) %all-to-all-start.4) | async-done | bytes 262176 | tf_op jit(solution)/shard_map/all_to_all | solution.py:20
  206.3 0.8 slice.71
  207.1 0.8 slice.69
  (25 shorter events, 0.2 us)
Async XLA Ops:
  0.6 2.4 %copy-start.6 = (bf16[2048,256]{1,0:T(8,128)(2,1)S(1)}, bf16[2048,256]{1,0:T(8,128)(2,1)}, u32[]{:S(2)}) copy-start(bf16[2048,256]{1,0:T(8,128)(2,1)} %feat_ref.3) | copy-start | bytes 3145732
  6.9 44.0 %all-to-all-start = ((bf16[128,16,256]{2,1,0:T(8,128)(2,1)}), bf16[128,16,256]{2,1,0:T(8,128)(2,1)S(1)}, u32[]{:S(2)}, u32[]{:S(2)}) async-start(bf16[128,16,256]{2,1,0:T(8,128)(2,1)} %bitcast.5), calls=%async_computation | async-start | bytes 2097152 | tf_op jit(solution)/shard_map/all_to_all | solution.py:20
  68.3 10.2 %copy-start.5 = (s32[2048]{0:T(1024)S(1)}, s32[2048]{0:T(1024)}, u32[]{:S(2)}) copy-start(s32[2048]{0:T(1024)} %param.21) | copy-start | bytes 24580
  68.3 10.3 %copy-start.3 = (s32[2048,2]{0,1:T(2,128)S(1)}, s32[2048,2]{0,1:T(2,128)}, u32[]{:S(2)}) copy-start(s32[2048,2]{0,1:T(2,128)} %param.20) | copy-start | bytes 49156
  68.3 10.3 %copy-start.4 = (f32[2048]{0:T(1024)S(1)}, f32[2048]{0:T(1024)}, u32[]{:S(2)}) copy-start(f32[2048]{0:T(1024)} %param.22) | copy-start | bytes 24580
  68.3 29.7 %all-to-all-start.1 = ((bf16[128,16,256]{2,1,0:T(8,128)(2,1)}), bf16[128,16,256]{2,1,0:T(8,128)(2,1)S(1)}, u32[]{:S(2)}, u32[]{:S(2)}) async-start(bf16[128,16,256]{2,1,0:T(8,128)(2,1)} %bitcast.61), calls=%async_computation.1 | async-start | bytes 2097152 | tf_op jit(solution)/shard_map/all_to_all | solution.py:20
  97.9 1.0 copy-start.1
  163.3 6.3 %copy-start.2 = (s32[1,128,8]{1,2,0:T(8,128)S(1)}, s32[1,128,8]{1,2,0:T(8,128)}, u32[]{:S(2)}) copy-start(s32[1,128,8]{1,2,0:T(8,128)} %param.18) | copy-start | bytes 12292
  163.3 6.5 %copy-start = (f32[2048,1]{1,0:T(8,128)S(1)}, f32[2048,1]{1,0:T(8,128)}, u32[]{:S(2)}) copy-start(f32[2048,1]{1,0:T(8,128)} %get-tuple-element.31) | copy-start | bytes 24580
  165.8 23.4 %all-to-all-start.3 = ((bf16[128,16,256]{2,1,0:T(8,128)(2,1)}), bf16[128,16,256]{2,1,0:T(8,128)(2,1)S(1)}, u32[]{:S(2)}, u32[]{:S(2)}) async-start(bf16[128,16,256]{2,1,0:T(8,128)(2,1)} %pad_maximum_fusion.1), calls=%async_computation.3 | async-start | bytes 2097152 | tf_op jit(solution)/shard_map/all_to_all | solution.py:20
  191.2 15.0 %all-to-all-start.4 = ((bf16[128,8,128]{2,1,0:T(8,128)(2,1)}), bf16[128,8,128]{2,1,0:T(8,128)(2,1)S(1)}, u32[]{:S(2)}, u32[]{:S(2)}) async-start(bf16[128,8,128]{2,1,0:T(8,128)(2,1)} %broadcast_in_dim.52), calls=%async_computation.4 | async-start | bytes 524288 | tf_op jit(solution)/shard_map/all_to_all | solution.py:20

commit v4 on v3

v4 whole, which is shorter than its diff:
```python
import jax
import jax.numpy as jnp
from jax import lax
from jax.experimental import pallas as pl
from jax.experimental.pallas import tpu as pltpu
from jax.sharding import PartitionSpec as P

AXES = ("dom", "grp")
LANES = 128
GROUP = 8
STRIDE = LANES // GROUP
BATCH = 8
TILE = 256
WIDE = 512
MESH = pl.DeviceIdType.MESH
CLASH = 1 << 20
VMEM = pl.BlockSpec(memory_space=pltpu.VMEM)
SMEM = pl.BlockSpec(memory_space=pltpu.SMEM)


def exchange(x):
    return lax.all_to_all(x, AXES, split_axis=0, concat_axis=0, tiled=True)


def dot32(a, b):
    return jnp.dot(a, b, preferred_element_type=jnp.float32)


def dot_nt(a, b):
    return lax.dot_general(a, b, (((1,), (1,)), ((), ())), preferred_element_type=jnp.float32)


def dot_tn(a, b):
    return lax.dot_general(a, b, (((0,), (0,)), ((), ())), preferred_element_type=jnp.float32)


def params(mib):
    return pltpu.CompilerParams(vmem_limit_bytes=mib * 2**20)


def cost(flops, size):
    return pl.CostEstimate(flops=flops, bytes_accessed=size, transcendentals=0)


def tile_of(i):
    return pl.ds(pl.multiple_of(i * TILE, TILE), TILE)


def pick(index, first, count, axis):
    shape = (index.shape[0], count) if axis == 1 else (count, index.shape[1])
    ids = lax.broadcasted_iota(jnp.int32, shape, axis) + first
    return jnp.where(index == ids, 1.0, 0.0).astype(jnp.bfloat16)


def column(ref, i):
    rows = ref[:, tile_of(i)]
    return jnp.transpose(jnp.broadcast_to(rows, (8, TILE)) if ref.shape[0] == 1 else rows)


def slots_kernel(half, panels, count_ref, src_ref, dst_ref, row_ref, unit_ref):
    chunks = src_ref.shape[0]
    lane = lax.broadcasted_iota(jnp.int32, (chunks, LANES), 1)
    slot = lax.broadcasted_iota(jnp.int32, (chunks, LANES), 0) * LANES + lane
    live = slot < count_ref[0]
    src = src_ref[...]
    dst = dst_ref[...]
    upper = jnp.where(dst >= half, 1, 0)
    row = jnp.right_shift(src, 7) * half + dst - upper * half
    row = jnp.where(live, row, half * panels + lane // STRIDE)
    unit_ref[...] = jnp.where(live, jnp.bitwise_and(src, LANES - 1) + upper * LANES, 2 * LANES)
    clash = jnp.zeros((chunks, LANES), jnp.int32)
    for k in range(1, GROUP // 2 + 1):
        clash = clash + jnp.where(row == pltpu.roll(row, k * STRIDE, 1), 1, 0)
    any_clash = jnp.max(clash.astype(jnp.float32), axis=1, keepdims=True) > 0.0
    row_ref[...] = row + jnp.where(any_clash & (lane == 0), CLASH, 0)


def counts_kernel(half, panels, row_ref, unit_ref, adj_ref, deg_ref, degt_ref, even, odd, units):
    step = pl.program_id(0)
    chunks = unit_ref.shape[0]

    @pl.when(step == 0)
    def _():
        lane = lax.broadcasted_iota(jnp.int32, (LANES, LANES), 1)
        share = half * panels // (chunks // BATCH)

        def prepare(i, carry):
            part = pl.ds(pl.multiple_of(i * share, share), share)
            for k in range(BATCH):
                c = i * BATCH + k
                wide = jnp.transpose(
                    jnp.broadcast_to(unit_ref[pl.ds(c, 1), :], (LANES, LANES))
                )
                units[pl.ds(pl.multiple_of(c * LANES, LANES), LANES), :] = jnp.where(
                    wide == lane, 1, jnp.where(wide == lane + LANES, 65536, 0)
                )
            even[part, :] = jnp.zeros((share, LANES), jnp.int32)
            odd[part, :] = jnp.zeros((share, LANES), jnp.int32)
            return carry

        lax.fori_loop(0, chunks // BATCH, prepare, 0)

        def chunk(c, carry):
            base = pl.multiple_of(c * LANES, LANES)
            places = row_ref.at[pl.ds(base, LANES)]
            head = places[0]

            def load(s):
                words = odd if s % 2 else even
                at = [places[s + STRIDE * t] for t in range(GROUP)]
                new = [
                    words[pl.ds(a, 1), :] + units[pl.ds(base + (s + STRIDE * t), 1), :]
                    for t, a in enumerate(at)
                ]
                return words, at, new

            def store(words, at, new):
                for a, n in zip(at, new):
                    words[pl.ds(a, 1), :] = n

            @pl.when(head < CLASH)
            def _():
                held = load(0)
                for s in range(1, STRIDE):
                    following = load(s)
                    store(*held)
                    held = following
                store(*held)

            @pl.when(head >= CLASH)
            def _():
                for j in range(LANES):
                    words = odd if j % 2 else even
                    a = places[j]
                    if j == 0:
                        a = a - CLASH
                    words[pl.ds(a, 1), :] = words[pl.ds(a, 1), :] + units[pl.ds(base + j, 1), :]

            return carry

        lax.fori_loop(0, chunks, chunk, 0)

    first = step * TILE
    total = jnp.zeros((TILE, LANES), jnp.int32)
    for p in range(panels):
        part = pl.ds(pl.multiple_of(p * half + first, TILE), TILE)
        word = even[part, :] + odd[part, :]
        total = total + word
        cols = slice(p * LANES, (p + 1) * LANES)
        for h, count in enumerate((jnp.bitwise_and(word, 0xFFFF), jnp.right_shift(word, 16))):
            adj_ref[h, :, cols] = count.astype(jnp.float32).astype(jnp.bfloat16)
    for h, count in enumerate((jnp.bitwise_and(total, 0xFFFF), jnp.right_shift(total, 16))):
        degree = jnp.sum(count.astype(jnp.float32), axis=1, keepdims=True)
        wide = jnp.broadcast_to(jnp.maximum(degree, 1.0), (TILE, LANES))
        deg_ref[h] = wide
        degt_ref[h] = jnp.transpose(wide)[:8]


def adjacency(edge_src, edge_dst, edge_count, node_rows, table_rows):
    half = node_rows // 2
    panels = table_rows // LANES
    chunks = edge_src.shape[0] // LANES
    grid_shape = (chunks, LANES)
    row, unit = pl.pallas_call(
        lambda *refs: slots_kernel(half, panels, *refs),
        out_shape=(
            jax.ShapeDtypeStruct(grid_shape, jnp.int32),
            jax.ShapeDtypeStruct(grid_shape, jnp.int32),
        ),
        in_specs=[SMEM, VMEM, VMEM],
        out_specs=(VMEM, VMEM),
        compiler_params=params(60),
        name="slots",
    )(edge_count, edge_src.reshape(grid_shape), edge_dst.reshape(grid_shape))
    adj, deg, degt = pl.pallas_call(
        lambda *refs: counts_kernel(half, panels, *refs),
        grid=(half // TILE,),
        out_shape=(
            jax.ShapeDtypeStruct((2, half, table_rows), jnp.bfloat16),
            jax.ShapeDtypeStruct((2, half, LANES), jnp.float32),
            jax.ShapeDtypeStruct((2, 8, half), jnp.float32),
        ),
        in_specs=[SMEM, pl.BlockSpec(grid_shape, lambda i: (0, 0))],
        out_specs=(
            pl.BlockSpec((2, TILE, table_rows), lambda i: (0, i, 0)),
            pl.BlockSpec((2, TILE, LANES), lambda i: (0, i, 0)),
            pl.BlockSpec((2, 8, TILE), lambda i: (0, 0, i)),
        ),
        scratch_shapes=[
            pltpu.VMEM((half * panels + GROUP, LANES), jnp.int32),
            pltpu.VMEM((half * panels + GROUP, LANES), jnp.int32),
            pltpu.VMEM((edge_src.shape[0], LANES), jnp.int32),
        ],
        compiler_params=params(60),
        cost_estimate=cost(60_000_000, 16 * 2**20),
        name="counts",
    )(row.reshape(-1), unit)
    return adj.reshape(node_rows, table_rows), deg.reshape(node_rows, LANES), degt


def step_kernel(
    adj_ref,
    feat_ref,
    arr_ref,
    deg_ref,
    degt_ref,
    want_ref,
    pair_ref,
    halo_ref,
    ws_ref,
    wn_ref,
    wh_ref,
    bias_ref,
    wo_ref,
    logit_ref,
    gfeat_ref,
    wts_ref,
    sums_ref,
    adj_s,
    emb_s,
    agg_s,
    served_s,
    recv_s,
    left_s,
    right_s,
    delta_s,
    pgl_s,
    pgr_s,
    rgrad_s,
    back_s,
    gradb_s,
    gt_s,
    gw_s,
    small_s,
    last_s,
    lrecv_s,
    share_s,
    srecv_s,
    adj_sem,
    send_sem,
    recv_sem,
):
    node_rows, width = feat_ref.shape
    recv_rows = want_ref.shape[1]
    pairs = pair_ref.shape[1]
    peers, block = last_s.shape[:2]
    grp = lax.axis_size("grp")
    me = lax.axis_index("dom") * grp + lax.axis_index("grp")
    burst = WIDE // block
    bursts = peers // burst
    tiles = node_rows // TILE
    barrier = pltpu.get_barrier_semaphore()

    def device(p):
        return (p // grp, lax.rem(p, grp))

    def load_adj(i):
        return pltpu.make_async_copy(
            adj_ref.at[tile_of(i), :], adj_s.at[tile_of(i), :], adj_sem.at[i]
        )

    def fetch(i, carry):
        load_adj(i).start()
        return carry

    lax.fori_loop(0, tiles, fetch, 0)

    def greet(i, carry):
        pl.semaphore_signal(
            barrier, inc=1, device_id=device(lax.rem(me + i, peers)), device_id_type=MESH
        )
        return carry

    lax.fori_loop(1, peers, greet, 0)

    def rows_of(p):
        return pl.ds(pl.multiple_of(p * block, block), block)

    def burst_at(k):
        return lax.rem(me // burst + k, bursts)

    def ship(k, source, target, which):
        def one(i, carry):
            p = burst_at(k) * burst + lax.rem(lax.rem(me, burst) + i, burst)

            @pl.when(p != me)
            def _():
                pltpu.make_async_remote_copy(
                    src_ref=source(p),
                    dst_ref=target,
                    send_sem=send_sem.at[which],
                    recv_sem=recv_sem.at[which],
                    device_id=device(p),
                    device_id_type=MESH,
                ).start()

            return carry

        lax.fori_loop(0, burst, one, 0)

    def settle(part, which):
        pltpu.make_async_copy(part, part, send_sem.at[which]).wait()
        pltpu.make_async_copy(part, part, recv_sem.at[which]).wait()

    def wide_at(k):
        return pl.ds(pl.multiple_of(burst_at(k) * WIDE, WIDE), WIDE)

    def produce(fill, source, target, which):
        fill(0)

        def middle(k, carry):
            fill(k)
            ship(k - 1, source, target, which)
            return carry

        lax.fori_loop(1, bursts, middle, 0)

    def encode(i, carry):
        load_adj(i).wait()
        at = tile_of(i)
        sums = dot32(adj_s[at, :node_rows], feat_ref[...]) + dot32(
            adj_s[at, node_rows:], arr_ref[...]
        )
        mean = (sums / deg_ref[at, :1]).astype(jnp.bfloat16)
        agg_s[at, :] = mean
        emb_s[at, :] = (dot32(feat_ref[at, :], ws_ref[...]) + dot32(mean, wn_ref[...])).astype(
            jnp.bfloat16
        )
        return carry

    lax.fori_loop(0, tiles, encode, 0)
    pl.semaphore_wait(barrier, peers - 1)

    def serve(k):
        at = wide_at(k)
        asked = jnp.transpose(jnp.broadcast_to(want_ref[:, at], (8, WIDE)))[:, :1]
        served_s[at, :] = dot32(pick(asked, 0, node_rows, 1), emb_s[...]).astype(jnp.bfloat16)

    served_of = lambda p: served_s.at[rows_of(p), :]
    produce(serve, served_of, recv_s.at[rows_of(me), :], 0)
    recv_s[rows_of(me), :] = served_s[rows_of(me), :]
    small_s[...] = jnp.zeros(small_s.shape, jnp.float32)
    ship(bursts - 1, served_of, recv_s.at[rows_of(me), :], 0)
    settle(recv_s.at[pl.ds(block, recv_rows - block), :], 0)

    def forward(i, carry):
        at = pl.ds(pl.multiple_of(i * WIDE, WIDE), WIDE)
        cols = jnp.transpose(pair_ref[:, at])
        ends = cols[:, 0:2].astype(jnp.int32)
        left = dot32(pick(ends[:, 0:1], 0, recv_rows, 1), recv_s[...]).astype(jnp.bfloat16)
        right = dot32(pick(ends[:, 1:2], 0, recv_rows, 1), recv_s[...]).astype(jnp.bfloat16)
        pre = dot32(left, wh_ref[:width, :]) + dot32(right, wh_ref[width:, :]) + bias_ref[...]
        hidden = jnp.maximum(pre, 0.0)
        logit = jnp.sum(hidden * wo_ref[...], axis=1, keepdims=True)
        logit_ref[:, at] = jnp.transpose(jnp.broadcast_to(logit, (WIDE, LANES)))[:8]
        slope = cols[:, 2:3] * (jax.nn.sigmoid(logit) - cols[:, 3:4])
        delta = jnp.where(pre > 0, slope * wo_ref[...], 0.0)
        small_s[0:1, :] += jnp.sum(delta, axis=0, keepdims=True)
        small_s[1:2, :] += jnp.sum(slope * hidden, axis=0, keepdims=True)
        delta_b = delta.astype(jnp.bfloat16)
        left_s[at, :] = left
        right_s[at, :] = right
        delta_s[at, :] = delta_b
        pgl_s[at, :] = dot_nt(delta_b, wh_ref[:width, :]).astype(jnp.bfloat16)
        pgr_s[at, :] = dot_nt(delta_b, wh_ref[width:, :]).astype(jnp.bfloat16)
        return carry

    lax.fori_loop(0, pairs // WIDE, forward, 0)
    ends_row = pair_ref[0:2, :].astype(jnp.int32)

    def collect(k):
        first = burst_at(k) * WIDE
        total = dot32(pick(ends_row[0:1, :], first, WIDE, 0), pgl_s[...]) + dot32(
            pick(ends_row[1:2, :], first, WIDE, 0), pgr_s[...]
        )
        rgrad_s[wide_at(k), :] = total.astype(jnp.bfloat16)

    rgrad_of = lambda p: rgrad_s.at[rows_of(p), :]
    produce(collect, rgrad_of, back_s.at[rows_of(me), :], 1)
    back_s[rows_of(me), :] = rgrad_s[rows_of(me), :]
    ship(bursts - 1, rgrad_of, back_s.at[rows_of(me), :], 1)
    gw_s[2 * width : 3 * width, :] = dot_tn(left_s[...], delta_s[...])
    gw_s[3 * width :, :] = dot_tn(right_s[...], delta_s[...])
    settle(back_s.at[pl.ds(block, recv_rows - block), :], 1)

    def put(i, carry):
        at = pl.ds(pl.multiple_of(i * WIDE, WIDE), WIDE)
        hot = pick(want_ref[...], i * WIDE, WIDE, 0)
        gradb_s[at, :] = dot32(hot, back_s[...]).astype(jnp.bfloat16)
        return carry

    lax.fori_loop(0, node_rows // WIDE, put, 0)
    gw_s[:width, :] = dot_tn(feat_ref[...], gradb_s[...])
    gw_s[width : 2 * width, :] = dot_tn(agg_s[...], gradb_s[...])
    degree = jnp.concatenate([degt_ref[0, 0:1, :], degt_ref[1, 0:1, :]], axis=1)
    gt_s[...] = (dot_nt(wn_ref[...], gradb_s[...]) / degree).astype(jnp.bfloat16)

    def table_grad(first):
        cols = pl.ds(pl.multiple_of(first, TILE), TILE)
        return jnp.transpose(dot32(gt_s[...], adj_s[:, cols]))

    half = block // 2

    def return_halo(k):
        t = burst_at(k)
        both = jnp.concatenate(
            [
                table_grad(node_rows + t * TILE).reshape(burst, half, width),
                gw_s[tile_of(t), :].reshape(burst, half, width),
            ],
            axis=1,
        )
        last_s[pl.ds(t * burst, burst)] = both.astype(jnp.bfloat16)

    last_of = lambda p: last_s.at[p]
    produce(return_halo, last_of, lrecv_s.at[me], 2)
    lrecv_s[me] = last_s[me]
    ship(bursts - 1, last_of, lrecv_s.at[me], 2)

    def direct(i, carry):
        at = tile_of(i)
        gfeat_ref[at, :] = dot_nt(gradb_s[at, :], ws_ref[...]) + table_grad(i * TILE)
        return carry

    lax.fori_loop(0, tiles, direct, 0)
    settle(lrecv_s.at[pl.ds(1, peers - 1)], 2)

    own = jnp.sum(lrecv_s[...].astype(jnp.float32), axis=0)[half:]
    small = small_s[...]
    small_hi = small.astype(jnp.bfloat16).astype(jnp.float32)
    small_lo = small - small_hi
    lines = [
        part[r : r + 1, c : c + LANES]
        for part in (small_hi, small_lo)
        for r in range(2)
        for c in (0, LANES)
    ]
    share_s[...] = jnp.concatenate([own[:, :LANES], own[:, LANES:]] + lines, axis=0).astype(
        jnp.bfloat16
    )

    def place(i, carry):
        at = pl.ds(pl.multiple_of(i * WIDE, WIDE), WIDE)
        hot = pick(halo_ref[...], i * WIDE, WIDE, 0)
        gfeat_ref[at, :] += dot32(hot, lrecv_s[...].reshape(recv_rows, width))
        return carry

    place(0, 0)

    def share(i, carry):
        p = lax.rem(me + i * 51, peers)
        pltpu.make_async_remote_copy(
            src_ref=share_s,
            dst_ref=srecv_s.at[me],
            send_sem=send_sem.at[3],
            recv_sem=recv_sem.at[3],
            device_id=device(p),
            device_id_type=MESH,
        ).start()
        return carry

    lax.fori_loop(1, peers, share, 0)
    srecv_s[me] = share_s[...]
    lax.fori_loop(1, node_rows // WIDE, place, 0)
    settle(srecv_s.at[pl.ds(1, peers - 1)], 3)
    everyone = srecv_s[...].astype(jnp.float32)
    wts_ref[:, :LANES] = everyone[:, :8].reshape(4 * width, LANES)
    wts_ref[:, LANES:] = everyone[:, 8:16].reshape(4 * width, LANES)
    sums_ref[...] = jnp.sum(everyone[:, 16:], axis=0)


def train_step(
    adj, features, arrived, deg, degt, want_row, pair_rows, halo_pad, w_self, w_neigh, w_hidden,
    bias, w_out, peers
):
    node_rows, width = features.shape
    table_rows = adj.shape[1]
    recv_rows = want_row.shape[1]
    pairs = pair_rows.shape[1]
    block = recv_rows // peers
    lines = width * 4 * width // peers // LANES + 8
    bf16 = lambda *shape: pltpu.VMEM(shape, jnp.bfloat16)
    return pl.pallas_call(
        step_kernel,
        out_shape=(
            jax.ShapeDtypeStruct((8, pairs), jnp.float32),
            jax.ShapeDtypeStruct((node_rows, width), jnp.float32),
            jax.ShapeDtypeStruct((4 * width, width), jnp.float32),
            jax.ShapeDtypeStruct((8, LANES), jnp.float32),
        ),
        in_specs=[pl.BlockSpec(memory_space=pl.ANY)] + [VMEM] * 12,
        out_specs=(VMEM,) * 4,
        scratch_shapes=[
            bf16(node_rows, table_rows),
            bf16(node_rows, width),
            bf16(node_rows, width),
            bf16(recv_rows, width),
            bf16(recv_rows, width),
            bf16(pairs, width),
            bf16(pairs, width),
            bf16(pairs, width),
            bf16(pairs, width),
            bf16(pairs, width),
            bf16(recv_rows, width),
            bf16(recv_rows, width),
            bf16(node_rows, width),
            bf16(width, node_rows),
            pltpu.VMEM((4 * width, width), jnp.float32),
            pltpu.VMEM((8, width), jnp.float32),
            bf16(peers, block, width),
            bf16(peers, block, width),
            bf16(lines, LANES),
            bf16(peers, lines, LANES),
            pltpu.SemaphoreType.DMA((node_rows // TILE,)),
            pltpu.SemaphoreType.DMA((4,)),
            pltpu.SemaphoreType.DMA((4,)),
        ],
        compiler_params=pltpu.CompilerParams(
            vmem_limit_bytes=62 * 2**20, collective_id=0, has_side_effects=True
        ),
        cost_estimate=cost(30_000_000_000, 24 * 2**20),
        name="train_step",
    )(
        adj, features, arrived, deg, degt, want_row, pair_rows, halo_pad, w_self, w_neigh,
        w_hidden, bias, w_out,
    )


def per_device(
    features,
    edge_src,
    edge_dst,
    edge_count,
    halo_index,
    request_rows,
    pair_ends,
    labels,
    pair_weight,
    w_self,
    w_neigh,
    w_hidden,
    b_hidden,
    w_out,
):
    node_rows, width = features.shape
    peers = lax.axis_size(AXES)
    halo_len = halo_index.shape[2]
    halo_rows = peers * halo_len
    req_len = request_rows.shape[2]
    recv_rows = peers * req_len
    nodes = lax.iota(jnp.int32, node_rows)

    halo_pad = jnp.pad(halo_index[0], ((0, 0), (0, req_len - halo_len)), constant_values=-1)
    halo_pick = (halo_pad.reshape(-1)[:, None] == nodes[None, :]).astype(jnp.bfloat16)
    asked = jnp.concatenate([request_rows[0] // 64, request_rows[0] % 64], axis=1)
    asked = jnp.pad(
        asked.astype(jnp.float32)[:, None, :],
        ((0, 0), (halo_len, req_len - halo_len - 1), (0, width - 2 * req_len)),
    ).reshape(peers * req_len, width)
    outgoing = (dot32(halo_pick, features) + asked).astype(jnp.bfloat16)
    outgoing = outgoing.reshape(peers, req_len, width)
    first = exchange(outgoing)
    edge_src, edge_dst, _ = lax.optimization_barrier((edge_src, edge_dst, outgoing))

    adj, deg, degt = adjacency(edge_src, edge_dst, edge_count, node_rows, node_rows + halo_rows)
    arrived = first[:, :halo_len].reshape(halo_rows, width)
    codes = first[:, halo_len, : 2 * req_len].astype(jnp.int32)
    wanted = (codes[:, :req_len] * 64 + codes[:, req_len:]).reshape(recv_rows)
    want_row = wanted.reshape(1, recv_rows)
    pair_rows = jnp.concatenate(
        [
            pair_ends.T.astype(jnp.float32),
            pair_weight[None],
            labels.astype(jnp.float32)[None],
            jnp.zeros((4, pair_weight.shape[0]), jnp.float32),
        ],
        axis=0,
    )
    logits, grad_features, weights, small = train_step(
        adj, features, arrived, deg, degt, want_row, pair_rows, halo_pad.reshape(1, -1), w_self,
        w_neigh, w_hidden, b_hidden[None], w_out[None], peers
    )
    small = (small[:4] + small[4:]).reshape(2, width)
    return (
        logits[0],
        grad_features,
        weights[:width],
        weights[width : 2 * width],
        weights[2 * width :],
        small[0],
        small[1],
    )


def solution(mesh):
    split = P(AXES)
    in_specs = (
        P(AXES, None),
        split,
        split,
        split,
        P(AXES, None, None),
        P(AXES, None, None),
        P(AXES, None),
        split,
        split,
        P(),
        P(),
        P(),
        P(),
        P(),
    )
    out_specs = (split, P(AXES, None), P(), P(), P(), P(), P())
    return jax.shard_map(
        per_device, mesh=mesh, in_specs=in_specs, out_specs=out_specs, check_vma=False
    )
```

time: 209 us -> 169 us (0.81)
  Pallas kernels: 86.4 us -> 139 us
  waiting for transfers between devices: 33.5 us -> 0.01 us
  blocking collectives: 28.9 us -> 0 us
  starting transfers between devices: 29.3 us -> 11.5 us
  other arithmetic: 7.57 us -> 0.92 us
  matrix products: 8.51 us -> 3.95 us
    pallas_call x4 -> x1, Pallas kernels: 54.6 us -> 107 us  [train_step(): pl.pallas_call(step_kernel, out_shape=(jax.ShapeDtypeStruct((8, pairs), j...]
    all_to_all x4 -> x1, waiting for transfers between devices: 33.5 us -> 0.01 us  [exchange(): return lax.all_to_all(x, AXES, split_axis=0, concat_axis=0, tiled=True)]
    all_to_all x1 -> x0, blocking collectives: 28.9 us -> none  [exchange(): return lax.all_to_all(x, AXES, split_axis=0, concat_axis=0, tiled=True)]
    all_to_all x4 -> x1, starting transfers between devices: 29.3 us -> 11.5 us  [exchange(): return lax.all_to_all(x, AXES, split_axis=0, concat_axis=0, tiled=True)]
    concatenate x2 -> x0, other arithmetic: 4.57 us -> none  [the longest x1 2.54 us: per_device(): jnp.concatenate([halo_grad.reshape(peers, halo_len, width), weight_terms....]
    dot_general x2 -> x1, matrix products: 8.51 us -> 3.95 us  [dot32(): return jnp.dot(a, b, preferred_element_type=jnp.float32)]
    slice x6 -> x3, local copies, waits for them, and re-layouts: 3.22 us -> 5.31 us  [the longest x1 2.02 us: per_device(): weights[2 * width:]]
  transfers between devices with their start and end apart: 4 -> 1, of which waited for: 3 -> 0; matrix products, arithmetic and copies ran while one was open for 3% -> 1% of each run, Pallas kernels for 20% -> 19%
where the time goes in v4:
time: 169 us; the launch traced here: 168 us
  Pallas kernels  139 us (82%)
  local copies, waits for them, and re-layouts  11.8 us (7%)
  starting transfers between devices  11.5 us (7%)
  matrix products  3.95 us (2%)
    pallas_call x1, Pallas kernels, train_step(): pl.pallas_call(step_kernel, out_shape=(jax.ShapeDtypeStruct((8, pairs), j...  107 us
    pallas_call x1, Pallas kernels, adjacency(): pl.pallas_call(lambda *refs: counts_kernel(half, panels, *refs), grid=(ha...  29.9 us
    all_to_all x1, starting transfers between devices, exchange(): return lax.all_to_all(x, AXES, split_axis=0, concat_axis=0, tiled=True)  11.5 us
    dot_general x1, matrix products, dot32(): return jnp.dot(a, b, preferred_element_type=jnp.float32)  3.95 us
  transfers between devices with their start and end apart: 1, of which 0 were waited for; matrix products, arithmetic and copies ran while one was open for 1% of the time, Pallas kernels for 19%

profile of v4, /device:TPU:1, one launch (start us, length us, event | category | flops | bytes accessed | tf_op | source)
XLA Modules:
  0.0 168.5 jit_solution(13160475135090219818)
XLA Ops:
  0.6 0.0 copy-start.5
  0.6 0.9 copy.42
  1.5 0.1 eq.17
  1.6 0.8 copy.37
  2.4 0.1 fusion.4
  2.5 0.1 copy.38
  2.5 0.1 copy.39
  2.6 0.1 copy.43
  2.7 0.3 pad.9.clone
  3.0 0.0 copy-done.5
  3.0 3.9 %fusion.3 = bf16[2048,256]{1,0:T(8,128)(2,1)} fusion(f32[2048,256]{1,0:T(8,128)S(1)} %bitcast.53, bf16[2048,256]{1,0:T(8,128)(2,1)S(1)} %copy-done.5, s32[2048]{0:T(1024)S(1)} %eq.17), kind=kOutput, calls=%fused_computation.4 | convolution fusion | flops 2152726528 | bytes 4202496 | tf_op jit(solution)/shard_map/dot_general | solution.py:26
  6.9 0.0 copy-start.3
  7.0 0.0 copy-start.1
  7.0 0.0 copy-start.2
  7.0 11.5 %all-to-all-start = ((bf16[128,16,256]{2,1,0:T(8,128)(2,1)}), bf16[128,16,256]{2,1,0:T(8,128)(2,1)S(1)}, u32[]{:S(2)}, u32[]{:S(2)}) async-start(bf16[128,16,256]{2,1,0:T(8,128)(2,1)} %bitcast.5), calls=%async_computation | async-start | bytes 2097152 | tf_op jit(solution)/shard_map/all_to_all | solution.py:22
  18.5 0.7 reshape.86.halo_ref
  19.8 0.0 copy-done.3
  19.8 0.1 pad.13.clone
  19.9 1.7 %slots.1 = (s32[128,128]{1,0:T(8,128)}, s32[128,128]{1,0:T(8,128)}) custom-call(s32[1]{0:T(128)S(6)} %copy.45.refs_0_, s32[128,128]{1,0:T(8,128)} %bitcast.55, s32[128,128]{1,0:T(8,128)} %bitcast.56), custom_call_target="tpu_custom_call" | custom-call | tf_op jit(solution)/shard_map/slots/pallas_call | solution.py:164
  21.6 29.9 %counts.1 = (bf16[2,1024,3072]{2,1,0:T(8,128)(2,1)}, f32[2,1024,128]{2,1,0:T(8,128)}, f32[2,8,1024]{2,1,0:T(8,128)}) custom-call(s32[16384]{0:T(1024)} %bitcast.61, s32[128,128]{1,0:T(8,128)} %get-tuple-element.21.refs_1_), custom_call_target="tpu_custom_call" | custom-call | flops 60000000 | bytes 16777216 | tf_op jit(solution)/shard_map/counts/pallas_call | solution.py:175
  51.5 0.0 copy-done.1
  51.5 0.0 copy-done.2
  51.5 0.7 maximum_maximum_fusion.pair_ref
  52.2 0.0 all-to-all-done
  52.2 0.1 slice_convert_fusion
  52.3 0.1 slice_add_fusion
  52.4 0.7 reshape_reshape.3.want_ref
  53.1 0.8 slice_bitcast_fusion.arr_ref
  53.9 107.3 %train_step.1 = (f32[8,2048]{1,0:T(8,128)}, f32[2048,256]{1,0:T(8,128)}, f32[1024,256]{1,0:T(8,128)}, f32[8,128]{1,0:T(8,128)}) custom-call(bf16[2048,3072]{1,0:T(8,128)(2,1)} %bitcast.64, bf16[2048,256]{1,0:T(8,128)(2,1)} %feat_ref.1, bf16[1024,256]{1,0:T(8,128)(2,1)} %slice_bitcast_fusion.arr_ref, f32[2048,128]{1,0:T(8,128)} %bitcast.65, ...), custom_call_target="tpu_custom_call" | custom-call | flops 30000001024 | bytes 25165824 | tf_op jit(solution)/shard_map/train_step/pallas_call | solution.py:483
  161.2 0.0 copy-start.4
  161.2 0.0 copy-start
  161.3 2.0 %slice.45 = f32[512,256]{1,0:T(8,128)} slice(f32[1024,256]{1,0:T(8,128)} %get-tuple-element.27), slice={[512:1024], [0:256]} | slice | bytes 1048576 | tf_op jit(solution)/shard_map/slice | solution.py:589
  163.3 1.9 %fusion.9 = (f32[256,256]{1,0:T(8,128)}, f32[256,256]{1,0:T(8,128)}) fusion(f32[1024,256]{1,0:T(8,128)} %get-tuple-element.27), kind=kLoop, calls=%fused_computation.27 | loop fusion | bytes 1048576 | tf_op jit(solution)/shard_map/slice | solution.py:588
  165.1 1.4 slice.42
  166.6 0.0 copy-done.4
  166.6 0.6 slice_bitcast_fusion.1
  167.2 0.0 copy-done
  167.2 1.3 copy.46
  (6 shorter events, 0.0 us)
Async XLA Ops:
  0.6 2.4 %copy-start.5 = (bf16[2048,256]{1,0:T(8,128)(2,1)S(1)}, bf16[2048,256]{1,0:T(8,128)(2,1)}, u32[]{:S(2)}) copy-start(bf16[2048,256]{1,0:T(8,128)(2,1)} %feat_ref.1) | copy-start | bytes 3145732
  6.9 12.9 %copy-start.3 = (s32[2048]{0:T(1024)S(1)}, s32[2048]{0:T(1024)}, u32[]{:S(2)}) copy-start(s32[2048]{0:T(1024)} %param.21) | copy-start | bytes 24580
  7.0 44.6 %copy-start.1 = (s32[2048,2]{0,1:T(2,128)S(1)}, s32[2048,2]{0,1:T(2,128)}, u32[]{:S(2)}) copy-start(s32[2048,2]{0,1:T(2,128)} %param.20) | copy-start | bytes 49156
  7.0 44.6 %copy-start.2 = (f32[2048]{0:T(1024)S(1)}, f32[2048]{0:T(1024)}, u32[]{:S(2)}) copy-start(f32[2048]{0:T(1024)} %param.22) | copy-start | bytes 24580
  7.0 45.3 %all-to-all-start = ((bf16[128,16,256]{2,1,0:T(8,128)(2,1)}), bf16[128,16,256]{2,1,0:T(8,128)(2,1)S(1)}, u32[]{:S(2)}, u32[]{:S(2)}) async-start(bf16[128,16,256]{2,1,0:T(8,128)(2,1)} %bitcast.5), calls=%async_computation | async-start | bytes 2097152 | tf_op jit(solution)/shard_map/all_to_all | solution.py:22
  161.2 5.3 %copy-start.4 = (f32[8,128]{1,0:T(8,128)S(1)}, f32[8,128]{1,0:T(8,128)}, u32[]{:S(2)}) copy-start(f32[8,128]{1,0:T(8,128)} %get-tuple-element.28) | copy-start | bytes 12292
  161.2 5.9 %copy-start = (f32[2048,256]{1,0:T(8,128)S(1)}, f32[2048,256]{1,0:T(8,128)}, u32[]{:S(2)}) copy-start(f32[2048,256]{1,0:T(8,128)} %get-tuple-element.43) | copy-start | bytes 6291460

commit v5 on v4

--- a/solution.py
+++ b/solution.py
@@ -12,6 +12,7 @@
 BATCH = 8
 TILE = 256
 WIDE = 512
+TALL = 1024
 MESH = pl.DeviceIdType.MESH
 CLASH = 1 << 20
 VMEM = pl.BlockSpec(memory_space=pltpu.VMEM)
@@ -214,8 +215,11 @@
     wo_ref,
     logit_ref,
     gfeat_ref,
-    wts_ref,
-    sums_ref,
+    gself_ref,
+    gneigh_ref,
+    ghid_ref,
+    gbias_ref,
+    gout_ref,
     adj_s,
     emb_s,
     agg_s,
@@ -232,8 +236,12 @@
     gt_s,
     gw_s,
     small_s,
-    last_s,
-    lrecv_s,
+    cols_s,
+    part_s,
+    precv_s,
+    halo_s,
+    hrecv_s,
+    hrows_s,
     share_s,
     srecv_s,
     adj_sem,
@@ -243,7 +251,8 @@
     node_rows, width = feat_ref.shape
     recv_rows = want_ref.shape[1]
     pairs = pair_ref.shape[1]
-    peers, block = last_s.shape[:2]
+    peers = part_s.shape[0]
+    block = recv_rows // peers
     grp = lax.axis_size("grp")
     me = lax.axis_index("dom") * grp + lax.axis_index("grp")
     burst = WIDE // block
@@ -289,7 +298,7 @@
                     src_ref=source(p),
                     dst_ref=target,
                     send_sem=send_sem.at[which],
-                    recv_sem=recv_sem.at[which],
+                    recv_sem=recv_sem.at[which, k],
                     device_id=device(p),
                     device_id_type=MESH,
                 ).start()
@@ -298,9 +307,20 @@
 
         lax.fori_loop(0, burst, one, 0)
 
-    def settle(part, which):
+    def arrived(k, ref, unit, which):
+        first = pl.ds(unit, (burst - 1) * unit) if unit else pl.ds(1, burst - 1)
+        rest = pl.ds(0, burst * unit) if unit else pl.ds(0, burst)
+        if isinstance(k, int) and k == 0:
+            part = ref.at[first]
+        else:
+            part = ref.at[rest]
+        pltpu.make_async_copy(part, part, recv_sem.at[which, k]).wait()
+
+    def sent(part, which):
         pltpu.make_async_copy(part, part, send_sem.at[which]).wait()
-        pltpu.make_async_copy(part, part, recv_sem.at[which]).wait()
+
+    def source_at(k):
+        return lax.rem(me // burst - k + bursts, bursts)
 
     def wide_at(k):
         return pl.ds(pl.multiple_of(burst_at(k) * WIDE, WIDE), WIDE)
@@ -341,25 +361,44 @@
     recv_s[rows_of(me), :] = served_s[rows_of(me), :]
     small_s[...] = jnp.zeros(small_s.shape, jnp.float32)
     ship(bursts - 1, served_of, recv_s.at[rows_of(me), :], 0)
-    settle(recv_s.at[pl.ds(block, recv_rows - block), :], 0)
+
+    def columns(i, carry):
+        at = pl.ds(pl.multiple_of(i * WIDE, WIDE), WIDE)
+        cols_s[at, :] = jnp.transpose(pair_ref[:, at])
+        return carry
+
+    lax.fori_loop(0, pairs // WIDE, columns, 0)
+    for k in range(bursts):
+        arrived(k, recv_s, block, 0)
+        b = source_at(k)
+        here = pl.ds(pl.multiple_of(b * WIDE, WIDE), WIDE)
+
+        def gather(i, carry):
+            at = pl.ds(pl.multiple_of(i * TALL, TALL), TALL)
+            for side, rows in ((0, left_s), (1, right_s)):
+                ends = cols_s[at, side : side + 1].astype(jnp.int32)
+                found = dot32(pick(ends, b * WIDE, WIDE, 1), recv_s[here, :]).astype(
+                    jnp.bfloat16
+                )
+                rows[at, :] = found if k == 0 else rows[at, :] + found
+            return carry
+
+        lax.fori_loop(0, pairs // TALL, gather, 0)
 
     def forward(i, carry):
         at = pl.ds(pl.multiple_of(i * WIDE, WIDE), WIDE)
-        cols = jnp.transpose(pair_ref[:, at])
-        ends = cols[:, 0:2].astype(jnp.int32)
-        left = dot32(pick(ends[:, 0:1], 0, recv_rows, 1), recv_s[...]).astype(jnp.bfloat16)
-        right = dot32(pick(ends[:, 1:2], 0, recv_rows, 1), recv_s[...]).astype(jnp.bfloat16)
+        cols = cols_s[at, :]
+        left = left_s[at, :]
+        right = right_s[at, :]
         pre = dot32(left, wh_ref[:width, :]) + dot32(right, wh_ref[width:, :]) + bias_ref[...]
         hidden = jnp.maximum(pre, 0.0)
         logit = jnp.sum(hidden * wo_ref[...], axis=1, keepdims=True)
-        logit_ref[:, at] = jnp.transpose(jnp.broadcast_to(logit, (WIDE, LANES)))[:8]
+        logit_ref[:, at] = jnp.transpose(jnp.broadcast_to(logit, (WIDE, LANES)))[:1]
         slope = cols[:, 2:3] * (jax.nn.sigmoid(logit) - cols[:, 3:4])
         delta = jnp.where(pre > 0, slope * wo_ref[...], 0.0)
         small_s[0:1, :] += jnp.sum(delta, axis=0, keepdims=True)
         small_s[1:2, :] += jnp.sum(slope * hidden, axis=0, keepdims=True)
         delta_b = delta.astype(jnp.bfloat16)
-        left_s[at, :] = left
-        right_s[at, :] = right
         delta_s[at, :] = delta_b
         pgl_s[at, :] = dot_nt(delta_b, wh_ref[:width, :]).astype(jnp.bfloat16)
         pgr_s[at, :] = dot_nt(delta_b, wh_ref[width:, :]).astype(jnp.bfloat16)
@@ -381,51 +420,66 @@
     ship(bursts - 1, rgrad_of, back_s.at[rows_of(me), :], 1)
     gw_s[2 * width : 3 * width, :] = dot_tn(left_s[...], delta_s[...])
     gw_s[3 * width :, :] = dot_tn(right_s[...], delta_s[...])
-    settle(back_s.at[pl.ds(block, recv_rows - block), :], 1)
-
-    def put(i, carry):
-        at = pl.ds(pl.multiple_of(i * WIDE, WIDE), WIDE)
-        hot = pick(want_ref[...], i * WIDE, WIDE, 0)
-        gradb_s[at, :] = dot32(hot, back_s[...]).astype(jnp.bfloat16)
-        return carry
-
-    lax.fori_loop(0, node_rows // WIDE, put, 0)
+    for k in range(bursts):
+        arrived(k, back_s, block, 1)
+        b = source_at(k)
+        here = pl.ds(pl.multiple_of(b * WIDE, WIDE), WIDE)
+
+        def put(i, carry):
+            at = pl.ds(pl.multiple_of(i * TALL, TALL), TALL)
+            found = dot32(pick(want_ref[:, here], i * TALL, TALL, 0), back_s[here, :])
+            gfeat_ref[at, :] = found if k == 0 else gfeat_ref[at, :] + found
+            return carry
+
+        lax.fori_loop(0, node_rows // TALL, put, 0)
+    gradb_s[...] = gfeat_ref[...].astype(jnp.bfloat16)
     gw_s[:width, :] = dot_tn(feat_ref[...], gradb_s[...])
     gw_s[width : 2 * width, :] = dot_tn(agg_s[...], gradb_s[...])
+    half = block // 2
+
+    def halves(rows):
+        wide = rows.reshape(burst, half, width)
+        return jnp.concatenate([wide[:, :, :LANES], wide[:, :, LANES:]], axis=1).astype(
+            jnp.bfloat16
+        )
+
+    def whole(blocks):
+        wide = blocks.astype(jnp.float32)
+        return jnp.concatenate([wide[:, :half], wide[:, half : 2 * half]], axis=2)
+
+    def weight_terms(k):
+        t = burst_at(k)
+        part_s[pl.ds(t * burst, burst)] = halves(gw_s[tile_of(t), :])
+
+    part_of = lambda p: part_s.at[p]
+    produce(weight_terms, part_of, precv_s.at[me], 2)
+    precv_s[me] = part_s[me]
     degree = jnp.concatenate([degt_ref[0, 0:1, :], degt_ref[1, 0:1, :]], axis=1)
     gt_s[...] = (dot_nt(wn_ref[...], gradb_s[...]) / degree).astype(jnp.bfloat16)
+    ship(bursts - 1, part_of, precv_s.at[me], 2)
 
     def table_grad(first):
         cols = pl.ds(pl.multiple_of(first, TILE), TILE)
         return jnp.transpose(dot32(gt_s[...], adj_s[:, cols]))
 
-    half = block // 2
-
     def return_halo(k):
         t = burst_at(k)
-        both = jnp.concatenate(
-            [
-                table_grad(node_rows + t * TILE).reshape(burst, half, width),
-                gw_s[tile_of(t), :].reshape(burst, half, width),
-            ],
-            axis=1,
-        )
-        last_s[pl.ds(t * burst, burst)] = both.astype(jnp.bfloat16)
-
-    last_of = lambda p: last_s.at[p]
-    produce(return_halo, last_of, lrecv_s.at[me], 2)
-    lrecv_s[me] = last_s[me]
-    ship(bursts - 1, last_of, lrecv_s.at[me], 2)
+        halo_s[pl.ds(t * burst, burst)] = halves(table_grad(node_rows + t * TILE))
+
+    halo_of = lambda p: halo_s.at[p]
+    produce(return_halo, halo_of, hrecv_s.at[me], 3)
+    hrecv_s[me] = halo_s[me]
 
     def direct(i, carry):
         at = tile_of(i)
         gfeat_ref[at, :] = dot_nt(gradb_s[at, :], ws_ref[...]) + table_grad(i * TILE)
         return carry
 
-    lax.fori_loop(0, tiles, direct, 0)
-    settle(lrecv_s.at[pl.ds(1, peers - 1)], 2)
-
-    own = jnp.sum(lrecv_s[...].astype(jnp.float32), axis=0)[half:]
+    direct(0, 0)
+    ship(bursts - 1, halo_of, hrecv_s.at[me], 3)
+    for k in range(bursts):
+        arrived(k, precv_s, 0, 2)
+    own = jnp.sum(precv_s[...].astype(jnp.float32), axis=0)
     small = small_s[...]
     small_hi = small.astype(jnp.bfloat16).astype(jnp.float32)
     small_lo = small - small_hi
@@ -435,25 +489,16 @@
         for r in range(2)
         for c in (0, LANES)
     ]
-    share_s[...] = jnp.concatenate([own[:, :LANES], own[:, LANES:]] + lines, axis=0).astype(
-        jnp.bfloat16
-    )
-
-    def place(i, carry):
-        at = pl.ds(pl.multiple_of(i * WIDE, WIDE), WIDE)
-        hot = pick(halo_ref[...], i * WIDE, WIDE, 0)
-        gfeat_ref[at, :] += dot32(hot, lrecv_s[...].reshape(recv_rows, width))
-        return carry
-
-    place(0, 0)
+    share_s[...] = jnp.concatenate([own] + lines, axis=0).astype(jnp.bfloat16)
+    direct(1, 0)
 
     def share(i, carry):
         p = lax.rem(me + i * 51, peers)
         pltpu.make_async_remote_copy(
             src_ref=share_s,
             dst_ref=srecv_s.at[me],
-            send_sem=send_sem.at[3],
-            recv_sem=recv_sem.at[3],
+            send_sem=send_sem.at[4],
+            recv_sem=recv_sem.at[4, 0],
             device_id=device(p),
             device_id_type=MESH,
         ).start()
@@ -461,12 +506,33 @@
 
     lax.fori_loop(1, peers, share, 0)
     srecv_s[me] = share_s[...]
-    lax.fori_loop(1, node_rows // WIDE, place, 0)
-    settle(srecv_s.at[pl.ds(1, peers - 1)], 3)
-    everyone = srecv_s[...].astype(jnp.float32)
-    wts_ref[:, :LANES] = everyone[:, :8].reshape(4 * width, LANES)
-    wts_ref[:, LANES:] = everyone[:, 8:16].reshape(4 * width, LANES)
-    sums_ref[...] = jnp.sum(everyone[:, 16:], axis=0)
+    lax.fori_loop(2, tiles, direct, 0)
+    for k in range(bursts):
+        arrived(k, hrecv_s, 0, 3)
+    hrows_s[...] = whole(hrecv_s[...]).reshape(peers * half, width).astype(jnp.bfloat16)
+
+    def place(i, carry):
+        at = pl.ds(pl.multiple_of(i * TALL, TALL), TALL)
+        hot = pick(halo_ref[...], i * TALL, TALL, 0)
+        gfeat_ref[at, :] += dot32(hot, hrows_s[...])
+        return carry
+
+    lax.fori_loop(0, node_rows // TALL, place, 0)
+    for which, ref in ((0, served_s), (1, rgrad_s)):
+        sent(ref.at[pl.ds(block, recv_rows - block), :], which)
+    for which, ref in ((2, part_s), (3, halo_s), (4, srecv_s)):
+        sent(ref.at[pl.ds(1, peers - 1)], which)
+    others = srecv_s.at[pl.ds(1, peers - 1)]
+    pltpu.make_async_copy(others, others, recv_sem.at[4, 0]).wait()
+    everyone = whole(srecv_s[...])
+    quarter = peers // 4
+    gself_ref[...] = everyone[:quarter].reshape(width, width)
+    gneigh_ref[...] = everyone[quarter : 2 * quarter].reshape(width, width)
+    ghid_ref[...] = everyone[2 * quarter :].reshape(2 * width, width)
+    total = jnp.sum(srecv_s[...].astype(jnp.float32)[:, block:], axis=0)
+    total = total[:4] + total[4:]
+    gbias_ref[...] = jnp.concatenate([total[0:1], total[1:2]], axis=1)
+    gout_ref[...] = jnp.concatenate([total[2:3], total[3:4]], axis=1)
 
 
 def train_step(
@@ -483,13 +549,16 @@
     return pl.pallas_call(
         step_kernel,
         out_shape=(
-            jax.ShapeDtypeStruct((8, pairs), jnp.float32),
+            jax.ShapeDtypeStruct((1, pairs), jnp.float32),
             jax.ShapeDtypeStruct((node_rows, width), jnp.float32),
-            jax.ShapeDtypeStruct((4 * width, width), jnp.float32),
-            jax.ShapeDtypeStruct((8, LANES), jnp.float32),
+            jax.ShapeDtypeStruct((width, width), jnp.float32),
+            jax.ShapeDtypeStruct((width, width), jnp.float32),
+            jax.ShapeDtypeStruct((2 * width, width), jnp.float32),
+            jax.ShapeDtypeStruct((1, width), jnp.float32),
+            jax.ShapeDtypeStruct((1, width), jnp.float32),
         ),
         in_specs=[pl.BlockSpec(memory_space=pl.ANY)] + [VMEM] * 12,
-        out_specs=(VMEM,) * 4,
+        out_specs=(VMEM,) * 7,
         scratch_shapes=[
             bf16(node_rows, table_rows),
             bf16(node_rows, width),
@@ -507,13 +576,17 @@
             bf16(width, node_rows),
             pltpu.VMEM((4 * width, width), jnp.float32),
             pltpu.VMEM((8, width), jnp.float32),
-            bf16(peers, block, width),
-            bf16(peers, block, width),
+            pltpu.VMEM((pairs, 8), jnp.float32),
+            bf16(peers, block, LANES),
+            bf16(peers, block, LANES),
+            bf16(peers, block, LANES),
+            bf16(peers, block, LANES),
+            bf16(table_rows - node_rows, width),
             bf16(lines, LANES),
             bf16(peers, lines, LANES),
             pltpu.SemaphoreType.DMA((node_rows // TILE,)),
-            pltpu.SemaphoreType.DMA((4,)),
-            pltpu.SemaphoreType.DMA((4,)),
+            pltpu.SemaphoreType.DMA((5,)),
+            pltpu.SemaphoreType.DMA((5, recv_rows // WIDE)),
         ],
         compiler_params=pltpu.CompilerParams(
             vmem_limit_bytes=62 * 2**20, collective_id=0, has_side_effects=True
@@ -576,19 +649,19 @@
         ],
         axis=0,
     )
-    logits, grad_features, weights, small = train_step(
-        adj, features, arrived, deg, degt, want_row, pair_rows, halo_pad.reshape(1, -1), w_self,
-        w_neigh, w_hidden, b_hidden[None], w_out[None], peers
+    logits, grad_features, grad_self, grad_neigh, grad_hidden, grad_bias, grad_out = train_step(
+        adj, features, arrived, deg, degt, want_row, pair_rows,
+        halo_index[0].reshape(1, halo_rows), w_self, w_neigh, w_hidden, b_hidden[None],
+        w_out[None], peers
     )
-    small = (small[:4] + small[4:]).reshape(2, width)
     return (
         logits[0],
         grad_features,
-        weights[:width],
-        weights[width : 2 * width],
-        weights[2 * width :],
-        small[0],
-        small[1],
+        grad_self,
+        grad_neigh,
+        grad_hidden,
+        grad_bias[0],
+        grad_out[0],
     )
 
 

time: 169 us -> 159 us (0.941)
  Pallas kernels: 139 us -> 129 us
    pallas_call x1, Pallas kernels: 107 us -> 96.8 us  [train_step(): pl.pallas_call(step_kernel, out_shape=(jax.ShapeDtypeStruct((1, pairs), j...]
    unnamed x16 -> x31, local copies, waits for them, and re-layouts: 3.14 us -> 9.68 us
    slice x3 -> x0, local copies, waits for them, and re-layouts: 5.31 us -> none  [the longest x1 2.02 us: per_device(): weights[2 * width:]]
  transfers between devices with their start and end apart: 1 -> 1, of which waited for: 0 -> 0; matrix products, arithmetic and copies ran while one was open for 1% -> 1% of each run, Pallas kernels for 19% -> 20%
where the time goes in v5:
time: 159 us
  Pallas kernels  129 us (81%)
  local copies, waits for them, and re-layouts  12.4 us (8%)
  starting transfers between devices  11.5 us (7%)
  matrix products  3.94 us (2%)
    pallas_call x1, Pallas kernels, train_step(): pl.pallas_call(step_kernel, out_shape=(jax.ShapeDtypeStruct((1, pairs), j...  96.8 us
    pallas_call x1, Pallas kernels, adjacency(): pl.pallas_call(lambda *refs: counts_kernel(half, panels, *refs), grid=(ha...  30.1 us
    all_to_all x1, starting transfers between devices, exchange(): return lax.all_to_all(x, AXES, split_axis=0, concat_axis=0, tiled=True)  11.5 us
    unnamed x31, local copies, waits for them, and re-layouts  9.68 us
    dot_general x1, matrix products, dot32(): return jnp.dot(a, b, preferred_element_type=jnp.float32)  3.94 us
  transfers between devices with their start and end apart: 1, of which 0 were waited for; matrix products, arithmetic and copies ran while one was open for 1% of the time, Pallas kernels for 20%

profile of v5, /device:TPU:1, one launch (start us, length us, event | category | flops | bytes accessed | tf_op | source)
XLA Modules:
  0.0 158.8 jit_solution(5167419299586767464)
XLA Ops:
  0.6 0.0 copy-start.9
  0.6 0.9 copy.37
  1.5 0.8 copy.42
  2.3 0.1 eq.17
  2.4 0.1 fusion.4
  2.5 0.1 copy.38
  2.5 0.1 copy.39
  2.6 0.1 copy.43
  2.7 0.3 pad.9.clone
  3.0 0.0 copy-done.9
  3.0 3.9 %fusion.3 = bf16[2048,256]{1,0:T(8,128)(2,1)} fusion(f32[2048,256]{1,0:T(8,128)S(1)} %bitcast.51, bf16[2048,256]{1,0:T(8,128)(2,1)S(1)} %copy-done.9, s32[2048]{0:T(1024)S(1)} %eq.17), kind=kOutput, calls=%fused_computation.4 | convolution fusion | flops 2152726528 | bytes 4202496 | tf_op jit(solution)/shard_map/dot_general | solution.py:27
  6.9 0.0 copy-start.3
  6.9 0.0 copy-start.6
  6.9 0.0 copy-start.4
  6.9 0.0 copy-start.5
  7.0 11.5 %all-to-all-start = ((bf16[128,16,256]{2,1,0:T(8,128)(2,1)}), bf16[128,16,256]{2,1,0:T(8,128)(2,1)S(1)}, u32[]{:S(2)}, u32[]{:S(2)}) async-start(bf16[128,16,256]{2,1,0:T(8,128)(2,1)} %bitcast.5), calls=%async_computation | async-start | bytes 2097152 | tf_op jit(solution)/shard_map/all_to_all | solution.py:23
  18.5 0.0 copy-done.3
  18.5 0.1 copy.41
  19.2 0.0 copy-done.6
  19.2 0.7 reshape_squeeze.3.halo_ref
  19.9 0.1 pad.13.clone
  20.0 1.7 %slots.1 = (s32[128,128]{1,0:T(8,128)}, s32[128,128]{1,0:T(8,128)}) custom-call(s32[1]{0:T(128)S(6)} %copy.51.refs_0_, s32[128,128]{1,0:T(8,128)} %bitcast.53, s32[128,128]{1,0:T(8,128)} %bitcast.54), custom_call_target="tpu_custom_call" | custom-call | tf_op jit(solution)/shard_map/slots/pallas_call | solution.py:165
  21.8 30.1 %counts.1 = (bf16[2,1024,3072]{2,1,0:T(8,128)(2,1)}, f32[2,1024,128]{2,1,0:T(8,128)}, f32[2,8,1024]{2,1,0:T(8,128)}) custom-call(s32[16384]{0:T(1024)} %bitcast.61, s32[128,128]{1,0:T(8,128)} %get-tuple-element.24.refs_1_), custom_call_target="tpu_custom_call" | custom-call | flops 60000000 | bytes 16777216 | tf_op jit(solution)/shard_map/counts/pallas_call | solution.py:176
  51.8 0.0 copy-done.4
  51.9 0.0 copy-done.5
  51.9 0.7 maximum_maximum_fusion.pair_ref
  52.6 0.0 all-to-all-done
  52.6 0.1 slice_convert_fusion
  52.6 0.1 slice_add_fusion
  52.7 0.7 reshape_reshape.3.want_ref
  53.4 0.8 slice_bitcast_fusion.arr_ref
  54.2 96.8 %train_step.1 = (f32[1,2048]{1,0:T(1,128)}, f32[2048,256]{1,0:T(8,128)}, f32[256,256]{1,0:T(8,128)}, f32[256,256]{1,0:T(8,128)}, f32[512,256]{1,0:T(8,128)}, /*index=5*/f32[1,256]{1,0:T(1,128)}, f32[1,256]{1,0:T(1,128)}) custom-call(bf16[2048,3072]{1,0:T(8,128)(2,1)} %bitcast.64, bf16[2048,256]{1,0:T(8,128)(2,1)} %feat_ref.1, ...), custom_call_target="tpu_custom_call" | custom-call | flops 30000001024 | bytes 25165824 | tf_op jit(solution)/shard_map/train_step/pallas_call | solution.py:549
  151.0 1.3 copy.52
  152.3 0.0 copy-start.2
  152.3 0.0 copy-start.1
  152.3 0.0 copy-start
  152.3 3.1 %copy.53 = f32[2048,256]{1,0:T(8,128)} copy(f32[2048,256]{1,0:T(8,128)} %get-tuple-element.45) | data formatting | bytes 4194304
  155.5 0.0 copy-done.2
  155.5 0.0 copy-start.8
  155.5 0.7 copy.54
  156.2 0.0 copy-done.1
  156.2 0.7 copy.55
  156.9 0.0 copy-done
  156.9 0.8 copy.56
  157.7 0.0 copy-done.8
  157.7 0.6 copy.57
  158.2 0.0 copy-done.7
  158.2 0.6 copy.58
  (6 shorter events, 0.0 us)
Async XLA Ops:
  0.6 2.4 %copy-start.9 = (bf16[2048,256]{1,0:T(8,128)(2,1)S(1)}, bf16[2048,256]{1,0:T(8,128)(2,1)}, u32[]{:S(2)}) copy-start(bf16[2048,256]{1,0:T(8,128)(2,1)} %feat_ref.1) | copy-start | bytes 3145732
  6.9 11.5 %copy-start.3 = (s32[1,128,8]{1,2,0:T(8,128)S(1)}, s32[1,128,8]{1,2,0:T(8,128)}, u32[]{:S(2)}) copy-start(s32[1,128,8]{1,2,0:T(8,128)} %param.18) | copy-start | bytes 12292
  6.9 12.3 %copy-start.6 = (s32[2048]{0:T(1024)S(1)}, s32[2048]{0:T(1024)}, u32[]{:S(2)}) copy-start(s32[2048]{0:T(1024)} %param.21) | copy-start | bytes 24580
  6.9 44.9 %copy-start.4 = (s32[2048,2]{0,1:T(2,128)S(1)}, s32[2048,2]{0,1:T(2,128)}, u32[]{:S(2)}) copy-start(s32[2048,2]{0,1:T(2,128)} %param.20) | copy-start | bytes 49156
  6.9 44.9 %copy-start.5 = (f32[2048]{0:T(1024)S(1)}, f32[2048]{0:T(1024)}, u32[]{:S(2)}) copy-start(f32[2048]{0:T(1024)} %param.22) | copy-start | bytes 24580
  7.0 45.6 %all-to-all-start = ((bf16[128,16,256]{2,1,0:T(8,128)(2,1)}), bf16[128,16,256]{2,1,0:T(8,128)(2,1)S(1)}, u32[]{:S(2)}, u32[]{:S(2)}) async-start(bf16[128,16,256]{2,1,0:T(8,128)(2,1)} %bitcast.5), calls=%async_computation | async-start | bytes 2097152 | tf_op jit(solution)/shard_map/all_to_all | solution.py:23
  152.3 3.1 %copy-start.2 = (f32[256,256]{1,0:T(8,128)S(1)}, f32[256,256]{1,0:T(8,128)}, u32[]{:S(2)}) copy-start(f32[256,256]{1,0:T(8,128)} %get-tuple-element.46) | copy-start | bytes 786436
  152.3 3.8 %copy-start.1 = (f32[256,256]{1,0:T(8,128)S(1)}, f32[256,256]{1,0:T(8,128)}, u32[]{:S(2)}) copy-start(f32[256,256]{1,0:T(8,128)} %get-tuple-element.47) | copy-start | bytes 786436
  152.3 4.6 %copy-start = (f32[512,256]{1,0:T(8,128)S(1)}, f32[512,256]{1,0:T(8,128)}, u32[]{:S(2)}) copy-start(f32[512,256]{1,0:T(8,128)} %get-tuple-element.48) | copy-start | bytes 1572868
  155.5 2.2 %copy-start.8 = (f32[1,256]{1,0:T(1,128)S(1)}, f32[1,256]{1,0:T(1,128)}, u32[]{:S(2)}) copy-start(f32[1,256]{1,0:T(1,128)} %get-tuple-element.33) | copy-start | bytes 3076
  155.5 2.8 %copy-start.7 = (f32[1,256]{1,0:T(1,128)S(1)}, f32[1,256]{1,0:T(1,128)}, u32[]{:S(2)}) copy-start(f32[1,256]{1,0:T(1,128)} %get-tuple-element.34) | copy-start | bytes 3076

commit v6 on v5

--- a/solution.py
+++ b/solution.py
@@ -13,14 +13,11 @@
 TILE = 256
 WIDE = 512
 TALL = 1024
-MESH = pl.DeviceIdType.MESH
+LOGICAL = pl.DeviceIdType.LOGICAL
 CLASH = 1 << 20
 VMEM = pl.BlockSpec(memory_space=pltpu.VMEM)
 SMEM = pl.BlockSpec(memory_space=pltpu.SMEM)
-
-
-def exchange(x):
-    return lax.all_to_all(x, AXES, split_axis=0, concat_axis=0, tiled=True)
+ANY = pl.BlockSpec(memory_space=pl.ANY)
 
 
 def dot32(a, b):
@@ -51,11 +48,6 @@
     shape = (index.shape[0], count) if axis == 1 else (count, index.shape[1])
     ids = lax.broadcasted_iota(jnp.int32, shape, axis) + first
     return jnp.where(index == ids, 1.0, 0.0).astype(jnp.bfloat16)
-
-
-def column(ref, i):
-    rows = ref[:, tile_of(i)]
-    return jnp.transpose(jnp.broadcast_to(rows, (8, TILE)) if ref.shape[0] == 1 else rows)
 
 
 def slots_kernel(half, panels, count_ref, src_ref, dst_ref, row_ref, unit_ref):
@@ -202,12 +194,13 @@
 def step_kernel(
     adj_ref,
     feat_ref,
-    arr_ref,
     deg_ref,
     degt_ref,
-    want_ref,
-    pair_ref,
+    ask_ref,
     halo_ref,
+    ends_ref,
+    weight_ref,
+    label_ref,
     ws_ref,
     wn_ref,
     wh_ref,
@@ -221,6 +214,15 @@
     gbias_ref,
     gout_ref,
     adj_s,
+    gfeat_s,
+    pair_s,
+    hcol_s,
+    hrow_s,
+    wcol_s,
+    wrow_s,
+    first_s,
+    frecv_s,
+    arr_s,
     emb_s,
     agg_s,
     served_s,
@@ -249,10 +251,10 @@
     recv_sem,
 ):
     node_rows, width = feat_ref.shape
-    recv_rows = want_ref.shape[1]
-    pairs = pair_ref.shape[1]
-    peers = part_s.shape[0]
-    block = recv_rows // peers
+    block, peers = ask_ref.shape
+    half = halo_ref.shape[0]
+    recv_rows = peers * block
+    pairs = ends_ref.shape[1]
     grp = lax.axis_size("grp")
     me = lax.axis_index("dom") * grp + lax.axis_index("grp")
     burst = WIDE // block
@@ -260,9 +262,6 @@
     tiles = node_rows // TILE
     barrier = pltpu.get_barrier_semaphore()
 
-    def device(p):
-        return (p // grp, lax.rem(p, grp))
-
     def load_adj(i):
         return pltpu.make_async_copy(
             adj_ref.at[tile_of(i), :], adj_s.at[tile_of(i), :], adj_sem.at[i]
@@ -276,7 +275,7 @@
 
     def greet(i, carry):
         pl.semaphore_signal(
-            barrier, inc=1, device_id=device(lax.rem(me + i, peers)), device_id_type=MESH
+            barrier, inc=1, device_id=lax.rem(me + i, peers), device_id_type=LOGICAL
         )
         return carry
 
@@ -299,8 +298,8 @@
                     dst_ref=target,
                     send_sem=send_sem.at[which],
                     recv_sem=recv_sem.at[which, k],
-                    device_id=device(p),
-                    device_id_type=MESH,
+                    device_id=p,
+                    device_id_type=LOGICAL,
                 ).start()
 
             return carry
@@ -335,12 +334,89 @@
 
         lax.fori_loop(1, bursts, middle, 0)
 
-    def encode(i, carry):
+    def halves(rows):
+        wide = rows.reshape(burst, half, width)
+        return jnp.concatenate([wide[:, :, :LANES], wide[:, :, LANES:]], axis=1)
+
+    def whole(blocks):
+        wide = blocks.astype(jnp.float32)
+        return jnp.concatenate([wide[:, :half], wide[:, half : 2 * half]], axis=2)
+
+    def spread(table, depth):
+        shape = (table.shape[0], depth, table.shape[1])
+        keep = lax.broadcasted_iota(jnp.int32, shape, 1) == lax.broadcasted_iota(
+            jnp.int32, shape, 2
+        )
+        wide = jnp.broadcast_to(table[:, None, :], shape)
+        one = jnp.sum(jnp.where(keep, wide, 0.0), axis=2, keepdims=True)
+        return one.reshape(shape[0] * depth, 1)
+
+    def as_row(col):
+        return jnp.transpose(jnp.broadcast_to(col, (col.shape[0], LANES)))[:8]
+
+    hcol_s[...] = spread(jnp.transpose(halo_ref[...].astype(jnp.float32)), half)
+    asks = ask_ref[...]
+    ask_table = jnp.transpose(
+        jnp.concatenate(
+            [
+                jnp.right_shift(asks, 6).astype(jnp.float32),
+                jnp.bitwise_and(asks, 63).astype(jnp.float32),
+                jnp.zeros((LANES - 2 * block, peers), jnp.float32),
+            ],
+            axis=0,
+        )
+    )
+    wcol_s[0:peers, :] = ask_table
+
+    def outgoing(t, carry):
+        hot = pick(hcol_s[tile_of(t), :].astype(jnp.int32), 0, node_rows, 1)
+        part = pl.ds(pl.multiple_of(t * burst, burst), burst)
+        asked = jnp.broadcast_to(wcol_s[part, :][:, None, :], (burst, 8, LANES))
+        first_s[part] = jnp.concatenate(
+            [halves(dot32(hot, feat_ref[...])), asked], axis=1
+        ).astype(jnp.bfloat16)
+        return carry
+
+    lax.fori_loop(0, bursts, outgoing, 0)
+
+    def local_sums(i, carry):
         load_adj(i).wait()
         at = tile_of(i)
-        sums = dot32(adj_s[at, :node_rows], feat_ref[...]) + dot32(
-            adj_s[at, node_rows:], arr_ref[...]
-        )
+        gfeat_s[at, :] = dot32(adj_s[at, :node_rows], feat_ref[...])
+        return carry
+
+    lax.fori_loop(0, tiles, local_sums, 0)
+    pl.semaphore_wait(barrier, peers - 1)
+    first_of = lambda p: first_s.at[p]
+    for k in range(bursts):
+        ship(k, first_of, frecv_s.at[me], 0)
+    frecv_s[me] = first_s[me]
+    pair_s[...] = jnp.concatenate(
+        [
+            ends_ref[...].astype(jnp.float32),
+            weight_ref[...],
+            label_ref[...].astype(jnp.float32),
+            jnp.zeros((4, pairs), jnp.float32),
+        ],
+        axis=0,
+    )
+
+    def columns(i, carry):
+        at = pl.ds(pl.multiple_of(i * WIDE, WIDE), WIDE)
+        cols_s[at, :] = jnp.transpose(pair_s[:, at])
+        return carry
+
+    lax.fori_loop(0, pairs // WIDE, columns, 0)
+    hrow_s[...] = as_row(hcol_s[...])
+    for k in range(bursts):
+        arrived(k, frecv_s, 0, 0)
+    arr_s[...] = whole(frecv_s[...]).reshape(peers * half, width).astype(jnp.bfloat16)
+    codes = jnp.max(frecv_s[...].astype(jnp.float32)[:, 2 * half :], axis=1)
+    wcol_s[0:peers, :] = codes * 64.0 + pltpu.roll(codes, LANES - block, 1)
+
+    def encode(i, carry):
+        at = tile_of(i)
+        sums = gfeat_s[at, :] + dot32(adj_s[at, node_rows:], arr_s[...])
         mean = (sums / deg_ref[at, :1]).astype(jnp.bfloat16)
         agg_s[at, :] = mean
         emb_s[at, :] = (dot32(feat_ref[at, :], ws_ref[...]) + dot32(mean, wn_ref[...])).astype(
@@ -349,27 +425,23 @@
         return carry
 
     lax.fori_loop(0, tiles, encode, 0)
-    pl.semaphore_wait(barrier, peers - 1)
 
     def serve(k):
         at = wide_at(k)
-        asked = jnp.transpose(jnp.broadcast_to(want_ref[:, at], (8, WIDE)))[:, :1]
-        served_s[at, :] = dot32(pick(asked, 0, node_rows, 1), emb_s[...]).astype(jnp.bfloat16)
+        part = pl.ds(pl.multiple_of(burst_at(k) * burst, burst), burst)
+        asked = spread(wcol_s[part, :], block)
+        wrow_s[:, at] = as_row(asked)
+        hot = pick(asked.astype(jnp.int32), 0, node_rows, 1)
+        served_s[at, :] = dot32(hot, emb_s[...]).astype(jnp.bfloat16)
 
     served_of = lambda p: served_s.at[rows_of(p), :]
-    produce(serve, served_of, recv_s.at[rows_of(me), :], 0)
+    produce(serve, served_of, recv_s.at[rows_of(me), :], 1)
     recv_s[rows_of(me), :] = served_s[rows_of(me), :]
     small_s[...] = jnp.zeros(small_s.shape, jnp.float32)
-    ship(bursts - 1, served_of, recv_s.at[rows_of(me), :], 0)
-
-    def columns(i, carry):
-        at = pl.ds(pl.multiple_of(i * WIDE, WIDE), WIDE)
-        cols_s[at, :] = jnp.transpose(pair_ref[:, at])
-        return carry
-
-    lax.fori_loop(0, pairs // WIDE, columns, 0)
+    ship(bursts - 1, served_of, recv_s.at[rows_of(me), :], 1)
+
     for k in range(bursts):
-        arrived(k, recv_s, block, 0)
+        arrived(k, recv_s, block, 1)
         b = source_at(k)
         here = pl.ds(pl.multiple_of(b * WIDE, WIDE), WIDE)
 
@@ -405,7 +477,7 @@
         return carry
 
     lax.fori_loop(0, pairs // WIDE, forward, 0)
-    ends_row = pair_ref[0:2, :].astype(jnp.int32)
+    ends_row = ends_ref[...]
 
     def collect(k):
         first = burst_at(k) * WIDE
@@ -415,48 +487,36 @@
         rgrad_s[wide_at(k), :] = total.astype(jnp.bfloat16)
 
     rgrad_of = lambda p: rgrad_s.at[rows_of(p), :]
-    produce(collect, rgrad_of, back_s.at[rows_of(me), :], 1)
+    produce(collect, rgrad_of, back_s.at[rows_of(me), :], 2)
     back_s[rows_of(me), :] = rgrad_s[rows_of(me), :]
-    ship(bursts - 1, rgrad_of, back_s.at[rows_of(me), :], 1)
+    ship(bursts - 1, rgrad_of, back_s.at[rows_of(me), :], 2)
     gw_s[2 * width : 3 * width, :] = dot_tn(left_s[...], delta_s[...])
     gw_s[3 * width :, :] = dot_tn(right_s[...], delta_s[...])
     for k in range(bursts):
-        arrived(k, back_s, block, 1)
+        arrived(k, back_s, block, 2)
         b = source_at(k)
         here = pl.ds(pl.multiple_of(b * WIDE, WIDE), WIDE)
 
         def put(i, carry):
             at = pl.ds(pl.multiple_of(i * TALL, TALL), TALL)
-            found = dot32(pick(want_ref[:, here], i * TALL, TALL, 0), back_s[here, :])
-            gfeat_ref[at, :] = found if k == 0 else gfeat_ref[at, :] + found
+            found = dot32(pick(wrow_s[0:1, here].astype(jnp.int32), i * TALL, TALL, 0), back_s[here, :])
+            gfeat_s[at, :] = found if k == 0 else gfeat_s[at, :] + found
             return carry
 
         lax.fori_loop(0, node_rows // TALL, put, 0)
-    gradb_s[...] = gfeat_ref[...].astype(jnp.bfloat16)
+    gradb_s[...] = gfeat_s[...].astype(jnp.bfloat16)
     gw_s[:width, :] = dot_tn(feat_ref[...], gradb_s[...])
     gw_s[width : 2 * width, :] = dot_tn(agg_s[...], gradb_s[...])
-    half = block // 2
-
-    def halves(rows):
-        wide = rows.reshape(burst, half, width)
-        return jnp.concatenate([wide[:, :, :LANES], wide[:, :, LANES:]], axis=1).astype(
-            jnp.bfloat16
-        )
-
-    def whole(blocks):
-        wide = blocks.astype(jnp.float32)
-        return jnp.concatenate([wide[:, :half], wide[:, half : 2 * half]], axis=2)
-
     def weight_terms(k):
         t = burst_at(k)
-        part_s[pl.ds(t * burst, burst)] = halves(gw_s[tile_of(t), :])
+        part_s[pl.ds(t * burst, burst)] = halves(gw_s[tile_of(t), :]).astype(jnp.bfloat16)
 
     part_of = lambda p: part_s.at[p]
-    produce(weight_terms, part_of, precv_s.at[me], 2)
+    produce(weight_terms, part_of, precv_s.at[me], 3)
     precv_s[me] = part_s[me]
     degree = jnp.concatenate([degt_ref[0, 0:1, :], degt_ref[1, 0:1, :]], axis=1)
     gt_s[...] = (dot_nt(wn_ref[...], gradb_s[...]) / degree).astype(jnp.bfloat16)
-    ship(bursts - 1, part_of, precv_s.at[me], 2)
+    ship(bursts - 1, part_of, precv_s.at[me], 3)
 
     def table_grad(first):
         cols = pl.ds(pl.multiple_of(first, TILE), TILE)
@@ -464,21 +524,23 @@
 
     def return_halo(k):
         t = burst_at(k)
-        halo_s[pl.ds(t * burst, burst)] = halves(table_grad(node_rows + t * TILE))
+        halo_s[pl.ds(t * burst, burst)] = halves(
+            table_grad(node_rows + t * TILE)
+        ).astype(jnp.bfloat16)
 
     halo_of = lambda p: halo_s.at[p]
-    produce(return_halo, halo_of, hrecv_s.at[me], 3)
+    produce(return_halo, halo_of, hrecv_s.at[me], 4)
     hrecv_s[me] = halo_s[me]
 
     def direct(i, carry):
         at = tile_of(i)
-        gfeat_ref[at, :] = dot_nt(gradb_s[at, :], ws_ref[...]) + table_grad(i * TILE)
+        gfeat_s[at, :] = dot_nt(gradb_s[at, :], ws_ref[...]) + table_grad(i * TILE)
         return carry
 
     direct(0, 0)
-    ship(bursts - 1, halo_of, hrecv_s.at[me], 3)
+    ship(bursts - 1, halo_of, hrecv_s.at[me], 4)
     for k in range(bursts):
-        arrived(k, precv_s, 0, 2)
+        arrived(k, precv_s, 0, 3)
     own = jnp.sum(precv_s[...].astype(jnp.float32), axis=0)
     small = small_s[...]
     small_hi = small.astype(jnp.bfloat16).astype(jnp.float32)
@@ -497,10 +559,10 @@
         pltpu.make_async_remote_copy(
             src_ref=share_s,
             dst_ref=srecv_s.at[me],
-            send_sem=send_sem.at[4],
-            recv_sem=recv_sem.at[4, 0],
-            device_id=device(p),
-            device_id_type=MESH,
+            send_sem=send_sem.at[5],
+            recv_sem=recv_sem.at[5, 0],
+            device_id=p,
+            device_id_type=LOGICAL,
         ).start()
         return carry
 
@@ -508,22 +570,24 @@
     srecv_s[me] = share_s[...]
     lax.fori_loop(2, tiles, direct, 0)
     for k in range(bursts):
-        arrived(k, hrecv_s, 0, 3)
+        arrived(k, hrecv_s, 0, 4)
     hrows_s[...] = whole(hrecv_s[...]).reshape(peers * half, width).astype(jnp.bfloat16)
 
     def place(i, carry):
         at = pl.ds(pl.multiple_of(i * TALL, TALL), TALL)
-        hot = pick(halo_ref[...], i * TALL, TALL, 0)
-        gfeat_ref[at, :] += dot32(hot, hrows_s[...])
+        hot = pick(hrow_s[0:1, :].astype(jnp.int32), i * TALL, TALL, 0)
+        gfeat_s[at, :] += dot32(hot, hrows_s[...])
         return carry
 
     lax.fori_loop(0, node_rows // TALL, place, 0)
-    for which, ref in ((0, served_s), (1, rgrad_s)):
+    result = pltpu.make_async_copy(gfeat_s, gfeat_ref, adj_sem.at[0])
+    result.start()
+    for which, ref in ((1, served_s), (2, rgrad_s)):
         sent(ref.at[pl.ds(block, recv_rows - block), :], which)
-    for which, ref in ((2, part_s), (3, halo_s), (4, srecv_s)):
+    for which, ref in ((0, frecv_s), (3, part_s), (4, halo_s), (5, srecv_s)):
         sent(ref.at[pl.ds(1, peers - 1)], which)
     others = srecv_s.at[pl.ds(1, peers - 1)]
-    pltpu.make_async_copy(others, others, recv_sem.at[4, 0]).wait()
+    pltpu.make_async_copy(others, others, recv_sem.at[5, 0]).wait()
     everyone = whole(srecv_s[...])
     quarter = peers // 4
     gself_ref[...] = everyone[:quarter].reshape(width, width)
@@ -533,18 +597,46 @@
     total = total[:4] + total[4:]
     gbias_ref[...] = jnp.concatenate([total[0:1], total[1:2]], axis=1)
     gout_ref[...] = jnp.concatenate([total[2:3], total[3:4]], axis=1)
+    result.wait()
+
+
+def finish_kernel(*refs):
+    count = len(refs) // 2
+    refs[count][...] = refs[0][...]
+
+    @pl.when(pl.program_id(0) == 0)
+    def _():
+        for i in range(1, count):
+            refs[count + i][...] = refs[i][...]
+
+
+def finish(arrays):
+    rows, width = arrays[0].shape
+    specs = [pl.BlockSpec((TILE, width), lambda i: (i, 0))] + [
+        pl.BlockSpec(a.shape, lambda i: (0, 0)) for a in arrays[1:]
+    ]
+    return pl.pallas_call(
+        finish_kernel,
+        grid=(rows // TILE,),
+        out_shape=tuple(jax.ShapeDtypeStruct(a.shape, a.dtype) for a in arrays),
+        in_specs=specs,
+        out_specs=tuple(specs),
+        compiler_params=params(60),
+        name="finish",
+    )(*arrays)
 
 
 def train_step(
-    adj, features, arrived, deg, degt, want_row, pair_rows, halo_pad, w_self, w_neigh, w_hidden,
-    bias, w_out, peers
+    adj, features, deg, degt, ask, halo, ends, pair_weight, labels, w_self, w_neigh, w_hidden,
+    bias, w_out
 ):
     node_rows, width = features.shape
     table_rows = adj.shape[1]
-    recv_rows = want_row.shape[1]
-    pairs = pair_rows.shape[1]
-    block = recv_rows // peers
-    lines = width * 4 * width // peers // LANES + 8
+    block, peers = ask.shape
+    half = halo.shape[0]
+    recv_rows = peers * block
+    pairs = ends.shape[1]
+    lines = 2 * half + 8
     bf16 = lambda *shape: pltpu.VMEM(shape, jnp.bfloat16)
     return pl.pallas_call(
         step_kernel,
@@ -557,10 +649,19 @@
             jax.ShapeDtypeStruct((1, width), jnp.float32),
             jax.ShapeDtypeStruct((1, width), jnp.float32),
         ),
-        in_specs=[pl.BlockSpec(memory_space=pl.ANY)] + [VMEM] * 12,
-        out_specs=(VMEM,) * 7,
+        in_specs=[ANY] + [VMEM] * 13,
+        out_specs=(VMEM, ANY) + (VMEM,) * 5,
         scratch_shapes=[
             bf16(node_rows, table_rows),
+            pltpu.VMEM((node_rows, width), jnp.float32),
+            pltpu.VMEM((8, pairs), jnp.float32),
+            pltpu.VMEM((peers * half, 1), jnp.float32),
+            pltpu.VMEM((8, peers * half), jnp.float32),
+            pltpu.VMEM((peers, LANES), jnp.float32),
+            pltpu.VMEM((8, recv_rows), jnp.float32),
+            bf16(peers, lines, LANES),
+            bf16(peers, lines, LANES),
+            bf16(peers * half, width),
             bf16(node_rows, width),
             bf16(node_rows, width),
             bf16(recv_rows, width),
@@ -581,12 +682,12 @@
             bf16(peers, block, LANES),
             bf16(peers, block, LANES),
             bf16(peers, block, LANES),
-            bf16(table_rows - node_rows, width),
+            bf16(peers * half, width),
             bf16(lines, LANES),
             bf16(peers, lines, LANES),
             pltpu.SemaphoreType.DMA((node_rows // TILE,)),
-            pltpu.SemaphoreType.DMA((5,)),
-            pltpu.SemaphoreType.DMA((5, recv_rows // WIDE)),
+            pltpu.SemaphoreType.DMA((6,)),
+            pltpu.SemaphoreType.DMA((6, recv_rows // WIDE)),
         ],
         compiler_params=pltpu.CompilerParams(
             vmem_limit_bytes=62 * 2**20, collective_id=0, has_side_effects=True
@@ -594,7 +695,7 @@
         cost_estimate=cost(30_000_000_000, 24 * 2**20),
         name="train_step",
     )(
-        adj, features, arrived, deg, degt, want_row, pair_rows, halo_pad, w_self, w_neigh,
+        adj, features, deg, degt, ask, halo, ends, pair_weight, labels, w_self, w_neigh,
         w_hidden, bias, w_out,
     )
 
@@ -615,44 +716,15 @@
     b_hidden,
     w_out,
 ):
-    node_rows, width = features.shape
-    peers = lax.axis_size(AXES)
-    halo_len = halo_index.shape[2]
-    halo_rows = peers * halo_len
-    req_len = request_rows.shape[2]
-    recv_rows = peers * req_len
-    nodes = lax.iota(jnp.int32, node_rows)
-
-    halo_pad = jnp.pad(halo_index[0], ((0, 0), (0, req_len - halo_len)), constant_values=-1)
-    halo_pick = (halo_pad.reshape(-1)[:, None] == nodes[None, :]).astype(jnp.bfloat16)
-    asked = jnp.concatenate([request_rows[0] // 64, request_rows[0] % 64], axis=1)
-    asked = jnp.pad(
-        asked.astype(jnp.float32)[:, None, :],
-        ((0, 0), (halo_len, req_len - halo_len - 1), (0, width - 2 * req_len)),
-    ).reshape(peers * req_len, width)
-    outgoing = (dot32(halo_pick, features) + asked).astype(jnp.bfloat16)
-    outgoing = outgoing.reshape(peers, req_len, width)
-    first = exchange(outgoing)
-    edge_src, edge_dst, _ = lax.optimization_barrier((edge_src, edge_dst, outgoing))
-
-    adj, deg, degt = adjacency(edge_src, edge_dst, edge_count, node_rows, node_rows + halo_rows)
-    arrived = first[:, :halo_len].reshape(halo_rows, width)
-    codes = first[:, halo_len, : 2 * req_len].astype(jnp.int32)
-    wanted = (codes[:, :req_len] * 64 + codes[:, req_len:]).reshape(recv_rows)
-    want_row = wanted.reshape(1, recv_rows)
-    pair_rows = jnp.concatenate(
-        [
-            pair_ends.T.astype(jnp.float32),
-            pair_weight[None],
-            labels.astype(jnp.float32)[None],
-            jnp.zeros((4, pair_weight.shape[0]), jnp.float32),
-        ],
-        axis=0,
+    node_rows = features.shape[0]
+    halo = halo_index[0].T
+    adj, deg, degt = adjacency(edge_src, edge_dst, edge_count, node_rows, node_rows + halo.size)
+    logits, grad_features, grad_self, grad_neigh, grad_hidden, grad_bias, grad_out = train_step(
+        adj, features, deg, degt, request_rows[0].T, halo, pair_ends.T, pair_weight[None],
+        labels[None], w_self, w_neigh, w_hidden, b_hidden[None], w_out[None]
     )
-    logits, grad_features, grad_self, grad_neigh, grad_hidden, grad_bias, grad_out = train_step(
-        adj, features, arrived, deg, degt, want_row, pair_rows,
-        halo_index[0].reshape(1, halo_rows), w_self, w_neigh, w_hidden, b_hidden[None],
-        w_out[None], peers
+    grad_features, grad_self, grad_neigh, grad_hidden, grad_bias, grad_out, logits = finish(
+        (grad_features, grad_self, grad_neigh, grad_hidden, grad_bias, grad_out, logits)
     )
     return (
         logits[0],

time: 159 us -> 153 us (0.962)
  Pallas kernels: 129 us -> 151 us
  local copies, waits for them, and re-layouts: 12.4 us -> 0 us
  starting transfers between devices: 11.5 us -> 0 us
  matrix products: 3.94 us -> 0 us
    pallas_call x1, Pallas kernels: 96.8 us -> 113 us  [train_step(): pl.pallas_call(step_kernel, out_shape=(jax.ShapeDtypeStruct((1, pairs), j...]
    all_to_all x1 -> x0, starting transfers between devices: 11.5 us -> none  [exchange(): return lax.all_to_all(x, AXES, split_axis=0, concat_axis=0, tiled=True)]
    unnamed x31 -> x0, local copies, waits for them, and re-layouts: 9.68 us -> none
    pallas_call x0 -> x1, Pallas kernels: none -> 6.44 us  [finish(): pl.pallas_call(finish_kernel, grid=(rows // TILE,), out_shape=tuple((jax....]
    dot_general x1 -> x0, matrix products: 3.94 us -> none  [dot32(): return jnp.dot(a, b, preferred_element_type=jnp.float32)]
  transfers between devices with their start and end apart: 1 -> 0, of which waited for: 0 -> 0; matrix products, arithmetic and copies ran while one was open for 1% -> 0% of each run, Pallas kernels for 20% -> 0%
where the time goes in v6:
time: 153 us
  Pallas kernels  151 us (99%)
    pallas_call x1, Pallas kernels, train_step(): pl.pallas_call(step_kernel, out_shape=(jax.ShapeDtypeStruct((1, pairs), j...  113 us
    pallas_call x1, Pallas kernels, adjacency(): pl.pallas_call(lambda *refs: counts_kernel(half, panels, *refs), grid=(ha...  30.1 us
    pallas_call x1, Pallas kernels, finish(): pl.pallas_call(finish_kernel, grid=(rows // TILE,), out_shape=tuple((jax....  6.44 us

profile of v6, /device:TPU:1, one launch (start us, length us, event | category | flops | bytes accessed | tf_op | source)
XLA Modules:
  0.0 152.6 jit_solution(9852629706480649307)
XLA Ops:
  1.3 1.7 %slots.1 = (s32[128,128]{1,0:T(8,128)}, s32[128,128]{1,0:T(8,128)}) custom-call(s32[1]{0:T(128)S(6)} %copy.21.refs_0_, s32[128,128]{1,0:T(8,128)} %bitcast.19, s32[128,128]{1,0:T(8,128)} %bitcast.20), custom_call_target="tpu_custom_call" | custom-call | tf_op jit(solution)/shard_map/slots/pallas_call | solution.py:157
  3.0 30.1 %counts.1 = (bf16[2,1024,3072]{2,1,0:T(8,128)(2,1)}, f32[2,1024,128]{2,1,0:T(8,128)}, f32[2,8,1024]{2,1,0:T(8,128)}) custom-call(s32[16384]{0:T(1024)} %bitcast.21, s32[128,128]{1,0:T(8,128)} %get-tuple-element.27.refs_1_), custom_call_target="tpu_custom_call" | custom-call | flops 60000000 | bytes 16777216 | tf_op jit(solution)/shard_map/counts/pallas_call | solution.py:168
  33.1 113.0 %train_step.1 = (f32[1,2048]{1,0:T(1,128)}, f32[2048,256]{1,0:T(8,128)}, f32[256,256]{1,0:T(8,128)}, f32[256,256]{1,0:T(8,128)}, f32[512,256]{1,0:T(8,128)}, /*index=5*/f32[1,256]{1,0:T(1,128)}, f32[1,256]{1,0:T(1,128)}) custom-call(bf16[2048,3072]{1,0:T(8,128)(2,1)} %bitcast.32, bf16[2048,256]{1,0:T(8,128)(2,1)} %feat_ref.1, f32[2048,128]{1,0:T(8,128)} %bitcast.33, ...), custom_call_target="tpu_custom_call" | custom-call | flops 30000001024 | bytes 25165824 | tf_op jit(solution)/shard_map/train_step/pallas_call | solution.py:641
  146.1 6.4 %finish.1 = (f32[2048,256]{1,0:T(8,128)}, f32[256,256]{1,0:T(8,128)}, f32[256,256]{1,0:T(8,128)}, f32[512,256]{1,0:T(8,128)}, f32[1,256]{1,0:T(1,128)}, /*index=5*/f32[1,256]{1,0:T(1,128)}, f32[1,2048]{1,0:T(1,128)}) custom-call(f32[2048,256]{1,0:T(8,128)} %get-tuple-element.31.refs_0_, f32[256,256]{1,0:T(8,128)} %get-tuple-element.32.refs_1_, ...), custom_call_target="tpu_custom_call" | custom-call | tf_op jit(solution)/shard_map/finish/pallas_call | solution.py:618

commit v7 on v6

--- a/solution.py
+++ b/solution.py
@@ -9,7 +9,6 @@
 LANES = 128
 GROUP = 8
 STRIDE = LANES // GROUP
-BATCH = 8
 TILE = 256
 WIDE = 512
 TALL = 1024
@@ -68,32 +67,29 @@
     row_ref[...] = row + jnp.where(any_clash & (lane == 0), CLASH, 0)
 
 
-def counts_kernel(half, panels, row_ref, unit_ref, adj_ref, deg_ref, degt_ref, even, odd, units):
+def counts_kernel(half, panels, row_ref, unit_ref, adj_ref, deg_ref, degt_ref, even, odd, unit_a, unit_b):
     step = pl.program_id(0)
     chunks = unit_ref.shape[0]
 
     @pl.when(step == 0)
     def _():
         lane = lax.broadcasted_iota(jnp.int32, (LANES, LANES), 1)
-        share = half * panels // (chunks // BATCH)
-
-        def prepare(i, carry):
-            part = pl.ds(pl.multiple_of(i * share, share), share)
-            for k in range(BATCH):
-                c = i * BATCH + k
-                wide = jnp.transpose(
-                    jnp.broadcast_to(unit_ref[pl.ds(c, 1), :], (LANES, LANES))
-                )
-                units[pl.ds(pl.multiple_of(c * LANES, LANES), LANES), :] = jnp.where(
-                    wide == lane, 1, jnp.where(wide == lane + LANES, 65536, 0)
-                )
-            even[part, :] = jnp.zeros((share, LANES), jnp.int32)
-            odd[part, :] = jnp.zeros((share, LANES), jnp.int32)
+
+        def clear(i, carry):
+            even[tile_of(i), :] = jnp.zeros((TILE, LANES), jnp.int32)
+            odd[tile_of(i), :] = jnp.zeros((TILE, LANES), jnp.int32)
             return carry
 
-        lax.fori_loop(0, chunks // BATCH, prepare, 0)
-
-        def chunk(c, carry):
+        lax.fori_loop(0, half * panels // TILE, clear, 0)
+
+        def units_of(c):
+            c = jnp.minimum(c, chunks - 1)
+            wide = jnp.transpose(jnp.broadcast_to(unit_ref[pl.ds(c, 1), :], (LANES, LANES)))
+            return jnp.where(wide == lane, 1, jnp.where(wide == lane + LANES, 65536, 0))
+
+        unit_a[...] = units_of(0)
+
+        def chunk(c, units, later):
             base = pl.multiple_of(c * LANES, LANES)
             places = row_ref.at[pl.ds(base, LANES)]
             head = places[0]
@@ -102,7 +98,7 @@
                 words = odd if s % 2 else even
                 at = [places[s + STRIDE * t] for t in range(GROUP)]
                 new = [
-                    words[pl.ds(a, 1), :] + units[pl.ds(base + (s + STRIDE * t), 1), :]
+                    words[pl.ds(a, 1), :] + units[pl.ds(s + STRIDE * t, 1), :]
                     for t, a in enumerate(at)
                 ]
                 return words, at, new
@@ -113,25 +109,31 @@
 
             @pl.when(head < CLASH)
             def _():
+                coming = units_of(c + 1)
                 held = load(0)
                 for s in range(1, STRIDE):
                     following = load(s)
                     store(*held)
                     held = following
                 store(*held)
+                later[...] = coming
 
             @pl.when(head >= CLASH)
             def _():
+                later[...] = units_of(c + 1)
                 for j in range(LANES):
                     words = odd if j % 2 else even
                     a = places[j]
                     if j == 0:
                         a = a - CLASH
-                    words[pl.ds(a, 1), :] = words[pl.ds(a, 1), :] + units[pl.ds(base + j, 1), :]
-
+                    words[pl.ds(a, 1), :] = words[pl.ds(a, 1), :] + units[pl.ds(j, 1), :]
+
+        def two(i, carry):
+            chunk(2 * i, unit_a, unit_b)
+            chunk(2 * i + 1, unit_b, unit_a)
             return carry
 
-        lax.fori_loop(0, chunks, chunk, 0)
+        lax.fori_loop(0, chunks // 2, two, 0)
 
     first = step * TILE
     total = jnp.zeros((TILE, LANES), jnp.int32)
@@ -182,7 +184,8 @@
         scratch_shapes=[
             pltpu.VMEM((half * panels + GROUP, LANES), jnp.int32),
             pltpu.VMEM((half * panels + GROUP, LANES), jnp.int32),
-            pltpu.VMEM((edge_src.shape[0], LANES), jnp.int32),
+            pltpu.VMEM((LANES, LANES), jnp.int32),
+            pltpu.VMEM((LANES, LANES), jnp.int32),
         ],
         compiler_params=params(60),
         cost_estimate=cost(60_000_000, 16 * 2**20),
@@ -554,8 +557,13 @@
     share_s[...] = jnp.concatenate([own] + lines, axis=0).astype(jnp.bfloat16)
     direct(1, 0)
 
+    core = lax.rem(me // grp, 2)
+    partner = me + (1 - 2 * core) * grp
+    groups = peers // (2 * grp)
+
     def share(i, carry):
-        p = lax.rem(me + i * 51, peers)
+        q = lax.rem((me // (2 * grp)) * grp + lax.rem(me, grp) + i * 27, peers // 2)
+        p = (q // grp) * (2 * grp) + core * grp + lax.rem(q, grp)
         pltpu.make_async_remote_copy(
             src_ref=share_s,
             dst_ref=srecv_s.at[me],
@@ -566,7 +574,7 @@
         ).start()
         return carry
 
-    lax.fori_loop(1, peers, share, 0)
+    lax.fori_loop(1, peers // 2, share, 0)
     srecv_s[me] = share_s[...]
     lax.fori_loop(2, tiles, direct, 0)
     for k in range(bursts):
@@ -582,12 +590,30 @@
     lax.fori_loop(0, node_rows // TALL, place, 0)
     result = pltpu.make_async_copy(gfeat_s, gfeat_ref, adj_sem.at[0])
     result.start()
+    others = srecv_s.at[pl.ds(1, peers // 2 - 1)]
+    pltpu.make_async_copy(others, others, recv_sem.at[5, 0]).wait()
+
+    def across(i, carry):
+        part = srecv_s.at[pl.ds(i * (2 * grp) + core * grp, grp)]
+        pltpu.make_async_remote_copy(
+            src_ref=part,
+            dst_ref=part,
+            send_sem=send_sem.at[6],
+            recv_sem=recv_sem.at[5, 1],
+            device_id=partner,
+            device_id_type=LOGICAL,
+        ).start()
+        return carry
+
+    lax.fori_loop(0, groups, across, 0)
+    sent(others, 5)
+    sent(srecv_s.at[pl.ds(0, peers // 2)], 6)
     for which, ref in ((1, served_s), (2, rgrad_s)):
         sent(ref.at[pl.ds(block, recv_rows - block), :], which)
-    for which, ref in ((0, frecv_s), (3, part_s), (4, halo_s), (5, srecv_s)):
+    for which, ref in ((0, frecv_s), (3, part_s), (4, halo_s)):
         sent(ref.at[pl.ds(1, peers - 1)], which)
-    others = srecv_s.at[pl.ds(1, peers - 1)]
-    pltpu.make_async_copy(others, others, recv_sem.at[5, 0]).wait()
+    mates = srecv_s.at[pl.ds(0, peers // 2)]
+    pltpu.make_async_copy(mates, mates, recv_sem.at[5, 1]).wait()
     everyone = whole(srecv_s[...])
     quarter = peers // 4
     gself_ref[...] = everyone[:quarter].reshape(width, width)
@@ -600,27 +626,40 @@
     result.wait()
 
 
-def finish_kernel(*refs):
-    count = len(refs) // 2
-    refs[count][...] = refs[0][...]
-
-    @pl.when(pl.program_id(0) == 0)
-    def _():
-        for i in range(1, count):
-            refs[count + i][...] = refs[i][...]
+def finish_kernel(count, *refs):
+    taken, given, held = refs[:count], refs[count : 2 * count], refs[2 * count : 3 * count]
+    in_sem, out_sem = refs[3 * count :]
+    parts = []
+    for a, h, b in zip(taken, held, given):
+        rows = a.shape[0]
+        step = TILE if rows > TILE else rows
+        parts += [(a, h, b, pl.ds(r, step)) for r in range(0, rows, step)]
+    moves = [
+        (
+            pltpu.make_async_copy(a.at[at, :], h.at[at, :], in_sem.at[n]),
+            pltpu.make_async_copy(h.at[at, :], b.at[at, :], out_sem.at[n]),
+        )
+        for n, (a, h, b, at) in enumerate(parts)
+    ]
+    for fetch, _ in moves:
+        fetch.start()
+    for fetch, put in moves:
+        fetch.wait()
+        put.start()
+    for _, put in moves:
+        put.wait()
 
 
 def finish(arrays):
-    rows, width = arrays[0].shape
-    specs = [pl.BlockSpec((TILE, width), lambda i: (i, 0))] + [
-        pl.BlockSpec(a.shape, lambda i: (0, 0)) for a in arrays[1:]
-    ]
+    count = len(arrays)
+    moves = sum(max(a.shape[0] // TILE, 1) for a in arrays)
     return pl.pallas_call(
-        finish_kernel,
-        grid=(rows // TILE,),
+        lambda *refs: finish_kernel(count, *refs),
         out_shape=tuple(jax.ShapeDtypeStruct(a.shape, a.dtype) for a in arrays),
-        in_specs=specs,
-        out_specs=tuple(specs),
+        in_specs=[ANY] * count,
+        out_specs=(ANY,) * count,
+        scratch_shapes=[pltpu.VMEM(a.shape, a.dtype) for a in arrays]
+        + [pltpu.SemaphoreType.DMA((moves,)), pltpu.SemaphoreType.DMA((moves,))],
         compiler_params=params(60),
         name="finish",
     )(*arrays)
@@ -686,7 +725,7 @@
             bf16(lines, LANES),
             bf16(peers, lines, LANES),
             pltpu.SemaphoreType.DMA((node_rows // TILE,)),
-            pltpu.SemaphoreType.DMA((6,)),
+            pltpu.SemaphoreType.DMA((7,)),
             pltpu.SemaphoreType.DMA((6, recv_rows // WIDE)),
         ],
         compiler_params=pltpu.CompilerParams(

time: 153 us -> 146 us (0.954)
  Pallas kernels: 151 us -> 144 us
    pallas_call x1, Pallas kernels: 6.44 us -> 2.87 us  [finish(): pl.pallas_call(lambda *refs: finish_kernel(count, *refs), out_shape=tuple...]
    pallas_call x1, Pallas kernels: 113 us -> 111 us  [train_step(): pl.pallas_call(step_kernel, out_shape=(jax.ShapeDtypeStruct((1, pairs), j...]
where the time goes in v7:
time: 146 us
  Pallas kernels  144 us (99%)
    pallas_call x1, Pallas kernels, train_step(): pl.pallas_call(step_kernel, out_shape=(jax.ShapeDtypeStruct((1, pairs), j...  111 us
    pallas_call x1, Pallas kernels, adjacency(): pl.pallas_call(lambda *refs: counts_kernel(half, panels, *refs), grid=(ha...  28.6 us

profile of v7, /device:TPU:1, one launch (start us, length us, event | category | flops | bytes accessed | tf_op | source)
XLA Modules:
  0.0 145.8 jit_solution(1344229470312570238)
XLA Ops:
  1.3 1.7 %slots.1 = (s32[128,128]{1,0:T(8,128)}, s32[128,128]{1,0:T(8,128)}) custom-call(s32[1]{0:T(128)S(6)} %copy.21.refs_0_, s32[128,128]{1,0:T(8,128)} %bitcast.19, s32[128,128]{1,0:T(8,128)} %bitcast.20), custom_call_target="tpu_custom_call" | custom-call | tf_op jit(solution)/shard_map/slots/pallas_call | solution.py:159
  3.0 28.6 %counts.1 = (bf16[2,1024,3072]{2,1,0:T(8,128)(2,1)}, f32[2,1024,128]{2,1,0:T(8,128)}, f32[2,8,1024]{2,1,0:T(8,128)}) custom-call(s32[16384]{0:T(1024)} %bitcast.21, s32[128,128]{1,0:T(8,128)} %get-tuple-element.27.refs_1_), custom_call_target="tpu_custom_call" | custom-call | flops 60000000 | bytes 16777216 | tf_op jit(solution)/shard_map/counts/pallas_call | solution.py:170
  31.6 111.1 %train_step.1 = (f32[1,2048]{1,0:T(1,128)}, f32[2048,256]{1,0:T(8,128)}, f32[256,256]{1,0:T(8,128)}, f32[256,256]{1,0:T(8,128)}, f32[512,256]{1,0:T(8,128)}, /*index=5*/f32[1,256]{1,0:T(1,128)}, f32[1,256]{1,0:T(1,128)}) custom-call(bf16[2048,3072]{1,0:T(8,128)(2,1)} %bitcast.32, bf16[2048,256]{1,0:T(8,128)(2,1)} %feat_ref.1, f32[2048,128]{1,0:T(8,128)} %bitcast.33, ...), custom_call_target="tpu_custom_call" | custom-call | flops 30000001024 | bytes 25165824 | tf_op jit(solution)/shard_map/train_step/pallas_call | solution.py:680
  142.8 2.9 %finish.1 = (f32[2048,256]{1,0:T(8,128)}, f32[256,256]{1,0:T(8,128)}, f32[256,256]{1,0:T(8,128)}, f32[512,256]{1,0:T(8,128)}, f32[1,256]{1,0:T(1,128)}, /*index=5*/f32[1,256]{1,0:T(1,128)}, f32[1,2048]{1,0:T(1,128)}) custom-call(f32[2048,256]{1,0:T(8,128)} %get-tuple-element.31.refs_0_, f32[256,256]{1,0:T(8,128)} %get-tuple-element.32.refs_1_, ...), custom_call_target="tpu_custom_call" | custom-call | tf_op jit(solution)/shard_map/finish/pallas_call | solution.py:656

commit v8 on v7

--- a/solution.py
+++ b/solution.py
@@ -49,30 +49,35 @@
     return jnp.where(index == ids, 1.0, 0.0).astype(jnp.bfloat16)
 
 
-def slots_kernel(half, panels, count_ref, src_ref, dst_ref, row_ref, unit_ref):
-    chunks = src_ref.shape[0]
-    lane = lax.broadcasted_iota(jnp.int32, (chunks, LANES), 1)
-    slot = lax.broadcasted_iota(jnp.int32, (chunks, LANES), 0) * LANES + lane
-    live = slot < count_ref[0]
-    src = src_ref[...]
-    dst = dst_ref[...]
+def edge_words(half, panels, count, src, dst):
+    shape = src.shape
+    lane = lax.broadcasted_iota(jnp.int32, shape, 1)
+    live = lax.broadcasted_iota(jnp.int32, shape, 0) * LANES + lane < count
     upper = jnp.where(dst >= half, 1, 0)
     row = jnp.right_shift(src, 7) * half + dst - upper * half
     row = jnp.where(live, row, half * panels + lane // STRIDE)
-    unit_ref[...] = jnp.where(live, jnp.bitwise_and(src, LANES - 1) + upper * LANES, 2 * LANES)
-    clash = jnp.zeros((chunks, LANES), jnp.int32)
+    unit = jnp.where(live, jnp.bitwise_and(src, LANES - 1) + upper * LANES, 2 * LANES)
+    clash = jnp.zeros(shape, jnp.int32)
     for k in range(1, GROUP // 2 + 1):
         clash = clash + jnp.where(row == pltpu.roll(row, k * STRIDE, 1), 1, 0)
     any_clash = jnp.max(clash.astype(jnp.float32), axis=1, keepdims=True) > 0.0
-    row_ref[...] = row + jnp.where(any_clash & (lane == 0), CLASH, 0)
-
-
-def counts_kernel(half, panels, row_ref, unit_ref, adj_ref, deg_ref, degt_ref, even, odd, unit_a, unit_b):
+    return row + jnp.where(any_clash & (lane == 0), CLASH, 0), unit
+
+
+def counts_kernel(
+    half, panels, count_ref, src_ref, dst_ref, adj_ref, degt_ref, even, odd, unit_a, unit_b,
+    row_v, row_ref, unit_ref, row_sem
+):
     step = pl.program_id(0)
     chunks = unit_ref.shape[0]
 
     @pl.when(step == 0)
     def _():
+        row_v[...], unit_ref[...] = edge_words(
+            half, panels, count_ref[0], src_ref[...], dst_ref[...]
+        )
+        words = pltpu.make_async_copy(row_v, row_ref, row_sem)
+        words.start()
         lane = lax.broadcasted_iota(jnp.int32, (LANES, LANES), 1)
 
         def clear(i, carry):
@@ -81,6 +86,7 @@
             return carry
 
         lax.fori_loop(0, half * panels // TILE, clear, 0)
+        words.wait()
 
         def units_of(c):
             c = jnp.minimum(c, chunks - 1)
@@ -90,8 +96,7 @@
         unit_a[...] = units_of(0)
 
         def chunk(c, units, later):
-            base = pl.multiple_of(c * LANES, LANES)
-            places = row_ref.at[pl.ds(base, LANES)]
+            places = row_ref.at[c]
             head = places[0]
 
             def load(s):
@@ -147,7 +152,6 @@
     for h, count in enumerate((jnp.bitwise_and(total, 0xFFFF), jnp.right_shift(total, 16))):
         degree = jnp.sum(count.astype(jnp.float32), axis=1, keepdims=True)
         wide = jnp.broadcast_to(jnp.maximum(degree, 1.0), (TILE, LANES))
-        deg_ref[h] = wide
         degt_ref[h] = jnp.transpose(wide)[:8]
 
 
@@ -156,29 +160,16 @@
     panels = table_rows // LANES
     chunks = edge_src.shape[0] // LANES
     grid_shape = (chunks, LANES)
-    row, unit = pl.pallas_call(
-        lambda *refs: slots_kernel(half, panels, *refs),
-        out_shape=(
-            jax.ShapeDtypeStruct(grid_shape, jnp.int32),
-            jax.ShapeDtypeStruct(grid_shape, jnp.int32),
-        ),
-        in_specs=[SMEM, VMEM, VMEM],
-        out_specs=(VMEM, VMEM),
-        compiler_params=params(60),
-        name="slots",
-    )(edge_count, edge_src.reshape(grid_shape), edge_dst.reshape(grid_shape))
-    adj, deg, degt = pl.pallas_call(
+    adj, degt = pl.pallas_call(
         lambda *refs: counts_kernel(half, panels, *refs),
         grid=(half // TILE,),
         out_shape=(
             jax.ShapeDtypeStruct((2, half, table_rows), jnp.bfloat16),
-            jax.ShapeDtypeStruct((2, half, LANES), jnp.float32),
             jax.ShapeDtypeStruct((2, 8, half), jnp.float32),
         ),
-        in_specs=[SMEM, pl.BlockSpec(grid_shape, lambda i: (0, 0))],
+        in_specs=[SMEM] + [pl.BlockSpec(grid_shape, lambda i: (0, 0))] * 2,
         out_specs=(
             pl.BlockSpec((2, TILE, table_rows), lambda i: (0, i, 0)),
-            pl.BlockSpec((2, TILE, LANES), lambda i: (0, i, 0)),
             pl.BlockSpec((2, 8, TILE), lambda i: (0, 0, i)),
         ),
         scratch_shapes=[
@@ -186,18 +177,21 @@
             pltpu.VMEM((half * panels + GROUP, LANES), jnp.int32),
             pltpu.VMEM((LANES, LANES), jnp.int32),
             pltpu.VMEM((LANES, LANES), jnp.int32),
+            pltpu.VMEM(grid_shape, jnp.int32),
+            pltpu.SMEM(grid_shape, jnp.int32),
+            pltpu.VMEM(grid_shape, jnp.int32),
+            pltpu.SemaphoreType.DMA,
         ],
         compiler_params=params(60),
         cost_estimate=cost(60_000_000, 16 * 2**20),
         name="counts",
-    )(row.reshape(-1), unit)
-    return adj.reshape(node_rows, table_rows), deg.reshape(node_rows, LANES), degt
+    )(edge_count, edge_src.reshape(grid_shape), edge_dst.reshape(grid_shape))
+    return adj.reshape(node_rows, table_rows), degt
 
 
 def step_kernel(
     adj_ref,
     feat_ref,
-    deg_ref,
     degt_ref,
     ask_ref,
     halo_ref,
@@ -219,6 +213,7 @@
     adj_s,
     gfeat_s,
     pair_s,
+    deg_s,
     hcol_s,
     hrow_s,
     wcol_s,
@@ -244,6 +239,8 @@
     cols_s,
     part_s,
     precv_s,
+    hpart_s,
+    hprecv_s,
     halo_s,
     hrecv_s,
     hrows_s,
@@ -277,12 +274,22 @@
     lax.fori_loop(0, tiles, fetch, 0)
 
     def greet(i, carry):
-        pl.semaphore_signal(
-            barrier, inc=1, device_id=lax.rem(me + i, peers), device_id_type=LOGICAL
-        )
-        return carry
-
-    lax.fori_loop(1, peers, greet, 0)
+        for u in range(7):
+            pl.semaphore_signal(
+                barrier,
+                inc=1,
+                device_id=jnp.bitwise_and(me + (i * 7 + u + 1), peers - 1),
+                device_id_type=LOGICAL,
+            )
+        return carry
+
+    pl.semaphore_signal(
+        barrier,
+        inc=1,
+        device_id=jnp.bitwise_and(me + (peers - 1), peers - 1),
+        device_id_type=LOGICAL,
+    )
+    lax.fori_loop(0, (peers - 2) // 7, greet, 0)
 
     def rows_of(p):
         return pl.ds(pl.multiple_of(p * block, block), block)
@@ -291,23 +298,26 @@
         return lax.rem(me // burst + k, bursts)
 
     def ship(k, source, target, which):
-        def one(i, carry):
-            p = burst_at(k) * burst + lax.rem(lax.rem(me, burst) + i, burst)
-
-            @pl.when(p != me)
-            def _():
-                pltpu.make_async_remote_copy(
-                    src_ref=source(p),
-                    dst_ref=target,
-                    send_sem=send_sem.at[which],
-                    recv_sem=recv_sem.at[which, k],
-                    device_id=p,
-                    device_id_type=LOGICAL,
-                ).start()
-
-            return carry
-
-        lax.fori_loop(0, burst, one, 0)
+        low = jnp.bitwise_and(me, burst - 1)
+        first = burst_at(k) * burst
+
+        def one(i):
+            p = first + jnp.bitwise_and(low + i, burst - 1)
+            pltpu.make_async_remote_copy(
+                src_ref=source(p),
+                dst_ref=target,
+                send_sem=send_sem.at[which],
+                recv_sem=recv_sem.at[which, k],
+                device_id=p,
+                device_id_type=LOGICAL,
+            ).start()
+
+        @pl.when(k > 0)
+        def _():
+            one(0)
+
+        for i in range(1, burst):
+            one(i)
 
     def arrived(k, ref, unit, which):
         first = pl.ds(unit, (burst - 1) * unit) if unit else pl.ds(1, burst - 1)
@@ -357,6 +367,7 @@
     def as_row(col):
         return jnp.transpose(jnp.broadcast_to(col, (col.shape[0], LANES)))[:8]
 
+    deg_s[...] = jnp.concatenate([degt_ref[0], degt_ref[1]], axis=1)
     hcol_s[...] = spread(jnp.transpose(halo_ref[...].astype(jnp.float32)), half)
     asks = ask_ref[...]
     ask_table = jnp.transpose(
@@ -420,7 +431,8 @@
     def encode(i, carry):
         at = tile_of(i)
         sums = gfeat_s[at, :] + dot32(adj_s[at, node_rows:], arr_s[...])
-        mean = (sums / deg_ref[at, :1]).astype(jnp.bfloat16)
+        degree = jnp.transpose(deg_s[:, at])[:, :1]
+        mean = (sums / degree).astype(jnp.bfloat16)
         agg_s[at, :] = mean
         emb_s[at, :] = (dot32(feat_ref[at, :], ws_ref[...]) + dot32(mean, wn_ref[...])).astype(
             jnp.bfloat16
@@ -495,6 +507,26 @@
     ship(bursts - 1, rgrad_of, back_s.at[rows_of(me), :], 2)
     gw_s[2 * width : 3 * width, :] = dot_tn(left_s[...], delta_s[...])
     gw_s[3 * width :, :] = dot_tn(right_s[...], delta_s[...])
+
+    def eighths(rows):
+        wide = rows.reshape(burst // 2, 8, width)
+        both = jnp.concatenate([wide[:, None, :, :LANES], wide[:, None, :, LANES:]], axis=1)
+        return both.reshape(burst, 8, LANES).astype(jnp.bfloat16)
+
+    def joined(blocks):
+        wide = blocks.reshape(peers // 2, 2, 8, LANES)
+        return jnp.concatenate([wide[:, 0], wide[:, 1]], axis=2).reshape(2 * width, width)
+
+    def eighth_of(t):
+        return pl.ds(pl.multiple_of(t * LANES, LANES), LANES)
+
+    for k in range(bursts):
+        t = burst_at(k)
+        hpart_s[pl.ds(t * burst, burst)] = eighths(gw_s[eighth_of(t + bursts), :])
+    hpart_of = lambda p: hpart_s.at[p]
+    hprecv_s[me] = hpart_s[me]
+    for k in range(bursts):
+        ship(k, hpart_of, hprecv_s.at[me], 7)
     for k in range(bursts):
         arrived(k, back_s, block, 2)
         b = source_at(k)
@@ -512,13 +544,12 @@
     gw_s[width : 2 * width, :] = dot_tn(agg_s[...], gradb_s[...])
     def weight_terms(k):
         t = burst_at(k)
-        part_s[pl.ds(t * burst, burst)] = halves(gw_s[tile_of(t), :]).astype(jnp.bfloat16)
+        part_s[pl.ds(t * burst, burst)] = eighths(gw_s[eighth_of(t), :])
 
     part_of = lambda p: part_s.at[p]
     produce(weight_terms, part_of, precv_s.at[me], 3)
     precv_s[me] = part_s[me]
-    degree = jnp.concatenate([degt_ref[0, 0:1, :], degt_ref[1, 0:1, :]], axis=1)
-    gt_s[...] = (dot_nt(wn_ref[...], gradb_s[...]) / degree).astype(jnp.bfloat16)
+    gt_s[...] = (dot_nt(wn_ref[...], gradb_s[...]) / deg_s[0:1, :]).astype(jnp.bfloat16)
     ship(bursts - 1, part_of, precv_s.at[me], 3)
 
     def table_grad(first):
@@ -544,7 +575,14 @@
     ship(bursts - 1, halo_of, hrecv_s.at[me], 4)
     for k in range(bursts):
         arrived(k, precv_s, 0, 3)
-    own = jnp.sum(precv_s[...].astype(jnp.float32), axis=0)
+        arrived(k, hprecv_s, 0, 7)
+    own = jnp.concatenate(
+        [
+            jnp.sum(precv_s[...].astype(jnp.float32), axis=0),
+            jnp.sum(hprecv_s[...].astype(jnp.float32), axis=0),
+        ],
+        axis=0,
+    )
     small = small_s[...]
     small_hi = small.astype(jnp.bfloat16).astype(jnp.float32)
     small_lo = small - small_hi
@@ -562,19 +600,20 @@
     groups = peers // (2 * grp)
 
     def share(i, carry):
-        q = lax.rem((me // (2 * grp)) * grp + lax.rem(me, grp) + i * 27, peers // 2)
-        p = (q // grp) * (2 * grp) + core * grp + lax.rem(q, grp)
-        pltpu.make_async_remote_copy(
-            src_ref=share_s,
-            dst_ref=srecv_s.at[me],
-            send_sem=send_sem.at[5],
-            recv_sem=recv_sem.at[5, 0],
-            device_id=p,
-            device_id_type=LOGICAL,
-        ).start()
-        return carry
-
-    lax.fori_loop(1, peers // 2, share, 0)
+        own_q = (me // (2 * grp)) * grp + lax.rem(me, grp)
+        for u in range(7):
+            q = jnp.bitwise_and(own_q + (i * 7 + u + 1) * 27, peers // 2 - 1)
+            pltpu.make_async_remote_copy(
+                src_ref=share_s,
+                dst_ref=srecv_s.at[me],
+                send_sem=send_sem.at[5],
+                recv_sem=recv_sem.at[5, 0],
+                device_id=q + (q // grp) * grp + core * grp,
+                device_id_type=LOGICAL,
+            ).start()
+        return carry
+
+    lax.fori_loop(0, (peers // 2 - 1) // 7, share, 0)
     srecv_s[me] = share_s[...]
     lax.fori_loop(2, tiles, direct, 0)
     for k in range(bursts):
@@ -610,16 +649,16 @@
     sent(srecv_s.at[pl.ds(0, peers // 2)], 6)
     for which, ref in ((1, served_s), (2, rgrad_s)):
         sent(ref.at[pl.ds(block, recv_rows - block), :], which)
-    for which, ref in ((0, frecv_s), (3, part_s), (4, halo_s)):
+    for which, ref in ((0, frecv_s), (3, part_s), (4, halo_s), (7, hpart_s)):
         sent(ref.at[pl.ds(1, peers - 1)], which)
     mates = srecv_s.at[pl.ds(0, peers // 2)]
     pltpu.make_async_copy(mates, mates, recv_sem.at[5, 1]).wait()
-    everyone = whole(srecv_s[...])
-    quarter = peers // 4
-    gself_ref[...] = everyone[:quarter].reshape(width, width)
-    gneigh_ref[...] = everyone[quarter : 2 * quarter].reshape(width, width)
-    ghid_ref[...] = everyone[2 * quarter :].reshape(2 * width, width)
-    total = jnp.sum(srecv_s[...].astype(jnp.float32)[:, block:], axis=0)
+    everyone = srecv_s[...].astype(jnp.float32)
+    node_terms = joined(everyone[:, :8])
+    gself_ref[...] = node_terms[:width]
+    gneigh_ref[...] = node_terms[width:]
+    ghid_ref[...] = joined(everyone[:, 8:16])
+    total = jnp.sum(everyone[:, block:], axis=0)
     total = total[:4] + total[4:]
     gbias_ref[...] = jnp.concatenate([total[0:1], total[1:2]], axis=1)
     gout_ref[...] = jnp.concatenate([total[2:3], total[3:4]], axis=1)
@@ -666,7 +705,7 @@
 
 
 def train_step(
-    adj, features, deg, degt, ask, halo, ends, pair_weight, labels, w_self, w_neigh, w_hidden,
+    adj, features, degt, ask, halo, ends, pair_weight, labels, w_self, w_neigh, w_hidden,
     bias, w_out
 ):
     node_rows, width = features.shape
@@ -688,12 +727,13 @@
             jax.ShapeDtypeStruct((1, width), jnp.float32),
             jax.ShapeDtypeStruct((1, width), jnp.float32),
         ),
-        in_specs=[ANY] + [VMEM] * 13,
+        in_specs=[ANY] + [VMEM] * 12,
         out_specs=(VMEM, ANY) + (VMEM,) * 5,
         scratch_shapes=[
             bf16(node_rows, table_rows),
             pltpu.VMEM((node_rows, width), jnp.float32),
             pltpu.VMEM((8, pairs), jnp.float32),
+            pltpu.VMEM((8, node_rows), jnp.float32),
             pltpu.VMEM((peers * half, 1), jnp.float32),
             pltpu.VMEM((8, peers * half), jnp.float32),
             pltpu.VMEM((peers, LANES), jnp.float32),
@@ -717,16 +757,18 @@
             pltpu.VMEM((4 * width, width), jnp.float32),
             pltpu.VMEM((8, width), jnp.float32),
             pltpu.VMEM((pairs, 8), jnp.float32),
-            bf16(peers, block, LANES),
-            bf16(peers, block, LANES),
+            bf16(peers, half, LANES),
+            bf16(peers, half, LANES),
+            bf16(peers, half, LANES),
+            bf16(peers, half, LANES),
             bf16(peers, block, LANES),
             bf16(peers, block, LANES),
             bf16(peers * half, width),
             bf16(lines, LANES),
             bf16(peers, lines, LANES),
             pltpu.SemaphoreType.DMA((node_rows // TILE,)),
-            pltpu.SemaphoreType.DMA((7,)),
-            pltpu.SemaphoreType.DMA((6, recv_rows // WIDE)),
+            pltpu.SemaphoreType.DMA((8,)),
+            pltpu.SemaphoreType.DMA((8, recv_rows // WIDE)),
         ],
         compiler_params=pltpu.CompilerParams(
             vmem_limit_bytes=62 * 2**20, collective_id=0, has_side_effects=True
@@ -734,7 +776,7 @@
         cost_estimate=cost(30_000_000_000, 24 * 2**20),
         name="train_step",
     )(
-        adj, features, deg, degt, ask, halo, ends, pair_weight, labels, w_self, w_neigh,
+        adj, features, degt, ask, halo, ends, pair_weight, labels, w_self, w_neigh,
         w_hidden, bias, w_out,
     )
 
@@ -757,9 +799,9 @@
 ):
     node_rows = features.shape[0]
     halo = halo_index[0].T
-    adj, deg, degt = adjacency(edge_src, edge_dst, edge_count, node_rows, node_rows + halo.size)
+    adj, degt = adjacency(edge_src, edge_dst, edge_count, node_rows, node_rows + halo.size)
     logits, grad_features, grad_self, grad_neigh, grad_hidden, grad_bias, grad_out = train_step(
-        adj, features, deg, degt, request_rows[0].T, halo, pair_ends.T, pair_weight[None],
+        adj, features, degt, request_rows[0].T, halo, pair_ends.T, pair_weight[None],
         labels[None], w_self, w_neigh, w_hidden, b_hidden[None], w_out[None]
     )
     grad_features, grad_self, grad_neigh, grad_hidden, grad_bias, grad_out, logits = finish(

time: 146 us -> 139 us (0.952)
  Pallas kernels: 144 us -> 137 us
    pallas_call x1, Pallas kernels: 111 us -> 106 us  [train_step(): pl.pallas_call(step_kernel, out_shape=(jax.ShapeDtypeStruct((1, pairs), j...]
    pallas_call x1 -> x0, Pallas kernels: 1.74 us -> none  [adjacency(): pl.pallas_call(lambda *refs: slots_kernel(half, panels, *refs), out_shape...]
where the time goes in v8:
time: 139 us; the launch traced here: 138 us
  Pallas kernels  137 us (99%)
  between operations  1.46 us (1%)
    pallas_call x1, Pallas kernels, train_step(): pl.pallas_call(step_kernel, out_shape=(jax.ShapeDtypeStruct((1, pairs), j...  106 us
    pallas_call x1, Pallas kernels, adjacency(): pl.pallas_call(lambda *refs: counts_kernel(half, panels, *refs), grid=(ha...  28 us
    pallas_call x1, Pallas kernels, finish(): pl.pallas_call(lambda *refs: finish_kernel(count, *refs), out_shape=tuple...  2.87 us

profile of v8, /device:TPU:1, one launch (start us, length us, event | category | flops | bytes accessed | tf_op | source)
XLA Modules:
  0.0 138.0 jit_solution(17515035017432281757)
XLA Ops:
  1.3 28.0 %counts.1 = (bf16[2,1024,3072]{2,1,0:T(8,128)(2,1)}, f32[2,8,1024]{2,1,0:T(8,128)}) custom-call(s32[1]{0:T(128)S(6)} %copy.21.refs_0_, s32[128,128]{1,0:T(8,128)} %bitcast.17, s32[128,128]{1,0:T(8,128)} %bitcast.18), custom_call_target="tpu_custom_call" | custom-call | flops 60000000 | bytes 16777216 | tf_op jit(solution)/shard_map/counts/pallas_call | solution.py:163
  29.3 105.7 %train_step.1 = (f32[1,2048]{1,0:T(1,128)}, f32[2048,256]{1,0:T(8,128)}, f32[256,256]{1,0:T(8,128)}, f32[256,256]{1,0:T(8,128)}, f32[512,256]{1,0:T(8,128)}, /*index=5*/f32[1,256]{1,0:T(1,128)}, f32[1,256]{1,0:T(1,128)}) custom-call(bf16[2048,3072]{1,0:T(8,128)(2,1)} %bitcast.29, bf16[2048,256]{1,0:T(8,128)(2,1)} %feat_ref.1, ...), custom_call_target="tpu_custom_call" | custom-call | flops 30000001024 | bytes 25165824 | tf_op jit(solution)/shard_map/train_step/pallas_call | solution.py:719
  135.0 2.9 %finish.1 = (f32[2048,256]{1,0:T(8,128)}, f32[256,256]{1,0:T(8,128)}, f32[256,256]{1,0:T(8,128)}, f32[512,256]{1,0:T(8,128)}, f32[1,256]{1,0:T(1,128)}, /*index=5*/f32[1,256]{1,0:T(1,128)}, f32[1,2048]{1,0:T(1,128)}) custom-call(f32[2048,256]{1,0:T(8,128)} %get-tuple-element.25.refs_0_, f32[256,256]{1,0:T(8,128)} %get-tuple-element.26.refs_1_, ...), custom_call_target="tpu_custom_call" | custom-call | tf_op jit(solution)/shard_map/finish/pallas_call | solution.py:695

commit v9 on v8

--- a/solution.py
+++ b/solution.py
@@ -217,6 +217,9 @@
     hcol_s,
     hrow_s,
     wcol_s,
+    wfull_s,
+    feat_t,
+    agg_t,
     wrow_s,
     first_s,
     frecv_s,
@@ -259,6 +262,7 @@
     me = lax.axis_index("dom") * grp + lax.axis_index("grp")
     burst = WIDE // block
     bursts = peers // burst
+    hburst = burst // 2
     tiles = node_rows // TILE
     barrier = pltpu.get_barrier_semaphore()
 
@@ -333,9 +337,6 @@
 
     def source_at(k):
         return lax.rem(me // burst - k + bursts, bursts)
-
-    def wide_at(k):
-        return pl.ds(pl.multiple_of(burst_at(k) * WIDE, WIDE), WIDE)
 
     def produce(fill, source, target, which):
         fill(0)
@@ -428,8 +429,41 @@
     codes = jnp.max(frecv_s[...].astype(jnp.float32)[:, 2 * half :], axis=1)
     wcol_s[0:peers, :] = codes * 64.0 + pltpu.roll(codes, LANES - block, 1)
 
+    def ship_half(n, source, target, which):
+        k = n // 2
+        low = jnp.bitwise_and(me, hburst - 1)
+        first = half_at(n)
+
+        def one(i):
+            p = first + jnp.bitwise_and(low + i, hburst - 1)
+            pltpu.make_async_remote_copy(
+                src_ref=source(p),
+                dst_ref=target,
+                send_sem=send_sem.at[which],
+                recv_sem=recv_sem.at[which, k],
+                device_id=p,
+                device_id_type=LOGICAL,
+            ).start()
+
+        @pl.when(n > 0)
+        def _():
+            one(0)
+
+        for i in range(1, hburst):
+            one(i)
+
+    def produce_halves(fill, source, target, which):
+        fill(0)
+
+        def middle(n, carry):
+            fill(n)
+            ship_half(n - 1, source, target, which)
+            return carry
+
+        lax.fori_loop(1, 2 * bursts, middle, 0)
+
     def encode(i, carry):
-        at = tile_of(i)
+        at = pl.ds(pl.multiple_of(i * TALL, TALL), TALL)
         sums = gfeat_s[at, :] + dot32(adj_s[at, node_rows:], arr_s[...])
         degree = jnp.transpose(deg_s[:, at])[:, :1]
         mean = (sums / degree).astype(jnp.bfloat16)
@@ -439,21 +473,35 @@
         )
         return carry
 
-    lax.fori_loop(0, tiles, encode, 0)
-
-    def serve(k):
-        at = wide_at(k)
-        part = pl.ds(pl.multiple_of(burst_at(k) * burst, burst), burst)
-        asked = spread(wcol_s[part, :], block)
-        wrow_s[:, at] = as_row(asked)
+    lax.fori_loop(0, node_rows // TALL, encode, 0)
+
+    def half_at(n):
+        k, sub = n // 2, lax.rem(n, 2)
+        low = jnp.bitwise_and(me, burst - 1) // hburst
+        return burst_at(k) * burst + jnp.bitwise_and(low + sub, 1) * hburst
+
+    def serve(n):
+        p = half_at(n)
+        at = pl.ds(pl.multiple_of(p * block, TILE), TILE)
+        asked = spread(wcol_s[pl.ds(pl.multiple_of(p, hburst), hburst), :], block)
+        wfull_s[at, :] = asked
         hot = pick(asked.astype(jnp.int32), 0, node_rows, 1)
         served_s[at, :] = dot32(hot, emb_s[...]).astype(jnp.bfloat16)
 
     served_of = lambda p: served_s.at[rows_of(p), :]
-    produce(serve, served_of, recv_s.at[rows_of(me), :], 1)
+    produce_halves(serve, served_of, recv_s.at[rows_of(me), :], 1)
     recv_s[rows_of(me), :] = served_s[rows_of(me), :]
     small_s[...] = jnp.zeros(small_s.shape, jnp.float32)
-    ship(bursts - 1, served_of, recv_s.at[rows_of(me), :], 1)
+    ship_half(2 * bursts - 1, served_of, recv_s.at[rows_of(me), :], 1)
+    feat_t[...] = jnp.transpose(feat_ref[...])
+    agg_t[...] = jnp.transpose(agg_s[...])
+
+    def ask_rows(i, carry):
+        at = pl.ds(pl.multiple_of(i * WIDE, WIDE), WIDE)
+        wrow_s[:, at] = as_row(wfull_s[at, :])
+        return carry
+
+    lax.fori_loop(0, recv_rows // WIDE, ask_rows, 0)
 
     for k in range(bursts):
         arrived(k, recv_s, block, 1)
@@ -473,14 +521,14 @@
         lax.fori_loop(0, pairs // TALL, gather, 0)
 
     def forward(i, carry):
-        at = pl.ds(pl.multiple_of(i * WIDE, WIDE), WIDE)
+        at = pl.ds(pl.multiple_of(i * TALL, TALL), TALL)
         cols = cols_s[at, :]
         left = left_s[at, :]
         right = right_s[at, :]
         pre = dot32(left, wh_ref[:width, :]) + dot32(right, wh_ref[width:, :]) + bias_ref[...]
         hidden = jnp.maximum(pre, 0.0)
         logit = jnp.sum(hidden * wo_ref[...], axis=1, keepdims=True)
-        logit_ref[:, at] = jnp.transpose(jnp.broadcast_to(logit, (WIDE, LANES)))[:1]
+        logit_ref[:, at] = jnp.transpose(jnp.broadcast_to(logit, (TALL, LANES)))[:1]
         slope = cols[:, 2:3] * (jax.nn.sigmoid(logit) - cols[:, 3:4])
         delta = jnp.where(pre > 0, slope * wo_ref[...], 0.0)
         small_s[0:1, :] += jnp.sum(delta, axis=0, keepdims=True)
@@ -491,20 +539,20 @@
         pgr_s[at, :] = dot_nt(delta_b, wh_ref[width:, :]).astype(jnp.bfloat16)
         return carry
 
-    lax.fori_loop(0, pairs // WIDE, forward, 0)
+    lax.fori_loop(0, pairs // TALL, forward, 0)
     ends_row = ends_ref[...]
 
-    def collect(k):
-        first = burst_at(k) * WIDE
-        total = dot32(pick(ends_row[0:1, :], first, WIDE, 0), pgl_s[...]) + dot32(
-            pick(ends_row[1:2, :], first, WIDE, 0), pgr_s[...]
+    def collect(n):
+        first = half_at(n) * block
+        total = dot32(pick(ends_row[0:1, :], first, TILE, 0), pgl_s[...]) + dot32(
+            pick(ends_row[1:2, :], first, TILE, 0), pgr_s[...]
         )
-        rgrad_s[wide_at(k), :] = total.astype(jnp.bfloat16)
+        rgrad_s[pl.ds(pl.multiple_of(first, TILE), TILE), :] = total.astype(jnp.bfloat16)
 
     rgrad_of = lambda p: rgrad_s.at[rows_of(p), :]
-    produce(collect, rgrad_of, back_s.at[rows_of(me), :], 2)
+    produce_halves(collect, rgrad_of, back_s.at[rows_of(me), :], 2)
     back_s[rows_of(me), :] = rgrad_s[rows_of(me), :]
-    ship(bursts - 1, rgrad_of, back_s.at[rows_of(me), :], 2)
+    ship_half(2 * bursts - 1, rgrad_of, back_s.at[rows_of(me), :], 2)
     gw_s[2 * width : 3 * width, :] = dot_tn(left_s[...], delta_s[...])
     gw_s[3 * width :, :] = dot_tn(right_s[...], delta_s[...])
 
@@ -540,8 +588,8 @@
 
         lax.fori_loop(0, node_rows // TALL, put, 0)
     gradb_s[...] = gfeat_s[...].astype(jnp.bfloat16)
-    gw_s[:width, :] = dot_tn(feat_ref[...], gradb_s[...])
-    gw_s[width : 2 * width, :] = dot_tn(agg_s[...], gradb_s[...])
+    gw_s[:width, :] = dot32(feat_t[...], gradb_s[...])
+    gw_s[width : 2 * width, :] = dot32(agg_t[...], gradb_s[...])
     def weight_terms(k):
         t = burst_at(k)
         part_s[pl.ds(t * burst, burst)] = eighths(gw_s[eighth_of(t), :])
@@ -737,6 +785,9 @@
             pltpu.VMEM((peers * half, 1), jnp.float32),
             pltpu.VMEM((8, peers * half), jnp.float32),
             pltpu.VMEM((peers, LANES), jnp.float32),
+            pltpu.VMEM((recv_rows, 1), jnp.float32),
+            bf16(width, node_rows),
+            bf16(width, node_rows),
             pltpu.VMEM((8, recv_rows), jnp.float32),
             bf16(peers, lines, LANES),
             bf16(peers, lines, LANES),

time: 139 us -> 136 us (0.978)
  Pallas kernels: 137 us -> 135 us
    pallas_call x1, Pallas kernels: 106 us -> 104 us  [train_step(): pl.pallas_call(step_kernel, out_shape=(jax.ShapeDtypeStruct((1, pairs), j...]
where the time goes in v9:
time: 136 us
  Pallas kernels  135 us (99%)
  between operations  1.46 us (1%)
    pallas_call x1, Pallas kernels, train_step(): pl.pallas_call(step_kernel, out_shape=(jax.ShapeDtypeStruct((1, pairs), j...  104 us
    pallas_call x1, Pallas kernels, adjacency(): pl.pallas_call(lambda *refs: counts_kernel(half, panels, *refs), grid=(ha...  27.9 us
    pallas_call x1, Pallas kernels, finish(): pl.pallas_call(lambda *refs: finish_kernel(count, *refs), out_shape=tuple...  2.87 us

profile of v9, /device:TPU:1, one launch (start us, length us, event | category | flops | bytes accessed | tf_op | source)
XLA Modules:
  0.0 136.2 jit_solution(9460123534038854866)
XLA Ops:
  1.3 27.9 %counts.1 = (bf16[2,1024,3072]{2,1,0:T(8,128)(2,1)}, f32[2,8,1024]{2,1,0:T(8,128)}) custom-call(s32[1]{0:T(128)S(6)} %copy.21.refs_0_, s32[128,128]{1,0:T(8,128)} %bitcast.17, s32[128,128]{1,0:T(8,128)} %bitcast.18), custom_call_target="tpu_custom_call" | custom-call | flops 60000000 | bytes 16777216 | tf_op jit(solution)/shard_map/counts/pallas_call | solution.py:163
  29.2 104.0 %train_step.1 = (f32[1,2048]{1,0:T(1,128)}, f32[2048,256]{1,0:T(8,128)}, f32[256,256]{1,0:T(8,128)}, f32[256,256]{1,0:T(8,128)}, f32[512,256]{1,0:T(8,128)}, /*index=5*/f32[1,256]{1,0:T(1,128)}, f32[1,256]{1,0:T(1,128)}) custom-call(bf16[2048,3072]{1,0:T(8,128)(2,1)} %bitcast.29, bf16[2048,256]{1,0:T(8,128)(2,1)} %feat_ref.1, ...), custom_call_target="tpu_custom_call" | custom-call | flops 30000001024 | bytes 25165824 | tf_op jit(solution)/shard_map/train_step/pallas_call | solution.py:767
  133.1 2.9 %finish.1 = (f32[2048,256]{1,0:T(8,128)}, f32[256,256]{1,0:T(8,128)}, f32[256,256]{1,0:T(8,128)}, f32[512,256]{1,0:T(8,128)}, f32[1,256]{1,0:T(1,128)}, /*index=5*/f32[1,256]{1,0:T(1,128)}, f32[1,2048]{1,0:T(1,128)}) custom-call(f32[2048,256]{1,0:T(8,128)} %get-tuple-element.25.refs_0_, f32[256,256]{1,0:T(8,128)} %get-tuple-element.26.refs_1_, ...), custom_call_target="tpu_custom_call" | custom-call | tf_op jit(solution)/shard_map/finish/pallas_call | solution.py:743

commit v10 on v9

--- a/solution.py
+++ b/solution.py
@@ -191,16 +191,16 @@
 
 def step_kernel(
     adj_ref,
-    feat_ref,
+    feat_in,
     degt_ref,
     ask_ref,
     halo_ref,
     ends_ref,
     weight_ref,
     label_ref,
-    ws_ref,
-    wn_ref,
-    wh_ref,
+    ws_in,
+    wn_in,
+    wh_in,
     bias_ref,
     wo_ref,
     logit_ref,
@@ -211,6 +211,10 @@
     gbias_ref,
     gout_ref,
     adj_s,
+    feat_ref,
+    ws_ref,
+    wn_ref,
+    wh_ref,
     gfeat_s,
     pair_s,
     deg_s,
@@ -221,6 +225,8 @@
     feat_t,
     agg_t,
     wrow_s,
+    ask_s,
+    arecv_s,
     first_s,
     frecv_s,
     arr_s,
@@ -249,6 +255,7 @@
     hrows_s,
     share_s,
     srecv_s,
+    in_sem,
     adj_sem,
     send_sem,
     recv_sem,
@@ -271,11 +278,19 @@
             adj_ref.at[tile_of(i), :], adj_s.at[tile_of(i), :], adj_sem.at[i]
         )
 
+    loads = [
+        pltpu.make_async_copy(a, b, in_sem.at[n])
+        for n, (a, b) in enumerate(
+            ((feat_in, feat_ref), (ws_in, ws_ref), (wn_in, wn_ref), (wh_in, wh_ref))
+        )
+    ]
+    for load in loads:
+        load.start()
+
     def fetch(i, carry):
         load_adj(i).start()
         return carry
 
-    lax.fori_loop(0, tiles, fetch, 0)
 
     def greet(i, carry):
         for u in range(7):
@@ -294,6 +309,9 @@
         device_id_type=LOGICAL,
     )
     lax.fori_loop(0, (peers - 2) // 7, greet, 0)
+    lax.fori_loop(0, tiles, fetch, 0)
+    for load in loads:
+        load.wait()
 
     def rows_of(p):
         return pl.ds(pl.multiple_of(p * block, block), block)
@@ -370,26 +388,18 @@
 
     deg_s[...] = jnp.concatenate([degt_ref[0], degt_ref[1]], axis=1)
     hcol_s[...] = spread(jnp.transpose(halo_ref[...].astype(jnp.float32)), half)
-    asks = ask_ref[...]
     ask_table = jnp.transpose(
         jnp.concatenate(
-            [
-                jnp.right_shift(asks, 6).astype(jnp.float32),
-                jnp.bitwise_and(asks, 63).astype(jnp.float32),
-                jnp.zeros((LANES - 2 * block, peers), jnp.float32),
-            ],
+            [ask_ref[...].astype(jnp.float32), jnp.zeros((LANES - block, peers), jnp.float32)],
             axis=0,
         )
     )
-    wcol_s[0:peers, :] = ask_table
+    ask_s[...] = ask_table.astype(jnp.int32).reshape(peers, 1, LANES)
 
     def outgoing(t, carry):
         hot = pick(hcol_s[tile_of(t), :].astype(jnp.int32), 0, node_rows, 1)
         part = pl.ds(pl.multiple_of(t * burst, burst), burst)
-        asked = jnp.broadcast_to(wcol_s[part, :][:, None, :], (burst, 8, LANES))
-        first_s[part] = jnp.concatenate(
-            [halves(dot32(hot, feat_ref[...])), asked], axis=1
-        ).astype(jnp.bfloat16)
+        first_s[part] = halves(dot32(hot, feat_ref[...])).astype(jnp.bfloat16)
         return carry
 
     lax.fori_loop(0, bursts, outgoing, 0)
@@ -405,7 +415,11 @@
     first_of = lambda p: first_s.at[p]
     for k in range(bursts):
         ship(k, first_of, frecv_s.at[me], 0)
+    ask_of = lambda p: ask_s.at[p]
+    for k in range(bursts):
+        ship(k, ask_of, arecv_s.at[me], 8)
     frecv_s[me] = first_s[me]
+    arecv_s[me] = ask_s[me]
     pair_s[...] = jnp.concatenate(
         [
             ends_ref[...].astype(jnp.float32),
@@ -425,9 +439,9 @@
     hrow_s[...] = as_row(hcol_s[...])
     for k in range(bursts):
         arrived(k, frecv_s, 0, 0)
+        arrived(k, arecv_s, 0, 8)
     arr_s[...] = whole(frecv_s[...]).reshape(peers * half, width).astype(jnp.bfloat16)
-    codes = jnp.max(frecv_s[...].astype(jnp.float32)[:, 2 * half :], axis=1)
-    wcol_s[0:peers, :] = codes * 64.0 + pltpu.roll(codes, LANES - block, 1)
+    wcol_s[0:peers, :] = jnp.max(arecv_s[...], axis=1).astype(jnp.float32)
 
     def ship_half(n, source, target, which):
         k = n // 2
@@ -697,7 +711,7 @@
     sent(srecv_s.at[pl.ds(0, peers // 2)], 6)
     for which, ref in ((1, served_s), (2, rgrad_s)):
         sent(ref.at[pl.ds(block, recv_rows - block), :], which)
-    for which, ref in ((0, frecv_s), (3, part_s), (4, halo_s), (7, hpart_s)):
+    for which, ref in ((0, frecv_s), (3, part_s), (4, halo_s), (7, hpart_s), (8, arecv_s)):
         sent(ref.at[pl.ds(1, peers - 1)], which)
     mates = srecv_s.at[pl.ds(0, peers // 2)]
     pltpu.make_async_copy(mates, mates, recv_sem.at[5, 1]).wait()
@@ -775,10 +789,14 @@
             jax.ShapeDtypeStruct((1, width), jnp.float32),
             jax.ShapeDtypeStruct((1, width), jnp.float32),
         ),
-        in_specs=[ANY] + [VMEM] * 12,
+        in_specs=[ANY, ANY] + [VMEM] * 6 + [ANY] * 3 + [VMEM] * 2,
         out_specs=(VMEM, ANY) + (VMEM,) * 5,
         scratch_shapes=[
             bf16(node_rows, table_rows),
+            bf16(node_rows, width),
+            bf16(width, width),
+            bf16(width, width),
+            bf16(2 * width, width),
             pltpu.VMEM((node_rows, width), jnp.float32),
             pltpu.VMEM((8, pairs), jnp.float32),
             pltpu.VMEM((8, node_rows), jnp.float32),
@@ -789,8 +807,10 @@
             bf16(width, node_rows),
             bf16(width, node_rows),
             pltpu.VMEM((8, recv_rows), jnp.float32),
-            bf16(peers, lines, LANES),
-            bf16(peers, lines, LANES),
+            pltpu.VMEM((peers, 1, LANES), jnp.int32),
+            pltpu.VMEM((peers, 1, LANES), jnp.int32),
+            bf16(peers, block, LANES),
+            bf16(peers, block, LANES),
             bf16(peers * half, width),
             bf16(node_rows, width),
             bf16(node_rows, width),
@@ -817,9 +837,10 @@
             bf16(peers * half, width),
             bf16(lines, LANES),
             bf16(peers, lines, LANES),
+            pltpu.SemaphoreType.DMA((4,)),
             pltpu.SemaphoreType.DMA((node_rows // TILE,)),
-            pltpu.SemaphoreType.DMA((8,)),
-            pltpu.SemaphoreType.DMA((8, recv_rows // WIDE)),
+            pltpu.SemaphoreType.DMA((9,)),
+            pltpu.SemaphoreType.DMA((9, recv_rows // WIDE)),
         ],
         compiler_params=pltpu.CompilerParams(
             vmem_limit_bytes=62 * 2**20, collective_id=0, has_side_effects=True

time: 136 us -> 135 us (level)
  Pallas kernels: 135 us -> 133 us
    pallas_call x1, Pallas kernels: 104 us -> 101 us  [train_step(): pl.pallas_call(step_kernel, out_shape=(jax.ShapeDtypeStruct((1, pairs), j...]
where the time goes in v10:
time: 135 us; the launch traced here: 134 us
  Pallas kernels  133 us (99%)
  between operations  1.46 us (1%)
    pallas_call x1, Pallas kernels, train_step(): pl.pallas_call(step_kernel, out_shape=(jax.ShapeDtypeStruct((1, pairs), j...  101 us
    pallas_call x1, Pallas kernels, adjacency(): pl.pallas_call(lambda *refs: counts_kernel(half, panels, *refs), grid=(ha...  28.5 us
    pallas_call x1, Pallas kernels, finish(): pl.pallas_call(lambda *refs: finish_kernel(count, *refs), out_shape=tuple...  2.87 us

profile of v10, /device:TPU:1, one launch (start us, length us, event | category | flops | bytes accessed | tf_op | source)
XLA Modules:
  0.0 134.3 jit_solution(9840651477144939890)
XLA Ops:
  1.3 28.5 %counts.1 = (bf16[2,1024,3072]{2,1,0:T(8,128)(2,1)}, f32[2,8,1024]{2,1,0:T(8,128)}) custom-call(s32[1]{0:T(128)S(6)} %copy.21.refs_0_, s32[128,128]{1,0:T(8,128)} %bitcast.17, s32[128,128]{1,0:T(8,128)} %bitcast.18), custom_call_target="tpu_custom_call" | custom-call | flops 60000000 | bytes 16777216 | tf_op jit(solution)/shard_map/counts/pallas_call | solution.py:163
  29.8 101.4 %train_step.1 = (f32[1,2048]{1,0:T(1,128)}, f32[2048,256]{1,0:T(8,128)}, f32[256,256]{1,0:T(8,128)}, f32[256,256]{1,0:T(8,128)}, f32[512,256]{1,0:T(8,128)}, /*index=5*/f32[1,256]{1,0:T(1,128)}, f32[1,256]{1,0:T(1,128)}) custom-call(bf16[2048,3072]{1,0:T(8,128)(2,1)} %bitcast.29, bf16[2048,256]{1,0:T(8,128)(2,1)} %feat_in.1, ...), custom_call_target="tpu_custom_call" | custom-call | flops 30000001024 | bytes 25165824 | tf_op jit(solution)/shard_map/train_step/pallas_call | solution.py:781
  131.3 2.9 %finish.1 = (f32[2048,256]{1,0:T(8,128)}, f32[256,256]{1,0:T(8,128)}, f32[256,256]{1,0:T(8,128)}, f32[512,256]{1,0:T(8,128)}, f32[1,256]{1,0:T(1,128)}, /*index=5*/f32[1,256]{1,0:T(1,128)}, f32[1,2048]{1,0:T(1,128)}) custom-call(f32[2048,256]{1,0:T(8,128)} %get-tuple-element.25.refs_0_, f32[256,256]{1,0:T(8,128)} %get-tuple-element.26.refs_1_, ...), custom_call_target="tpu_custom_call" | custom-call | tf_op jit(solution)/shard_map/finish/pallas_call | solution.py:757

commit v11 on v10

--- a/solution.py
+++ b/solution.py
@@ -7,7 +7,7 @@
 
 AXES = ("dom", "grp")
 LANES = 128
-GROUP = 8
+GROUP = 4
 STRIDE = LANES // GROUP
 TILE = 256
 WIDE = 512

time: 135 us -> 134 us (level)
  no operation moved by 1% of the time
where the time goes in v11:
time: 134 us
  Pallas kernels  133 us (99%)
  between operations  1.46 us (1%)
    pallas_call x1, Pallas kernels, train_step(): pl.pallas_call(step_kernel, out_shape=(jax.ShapeDtypeStruct((1, pairs), j...  103 us
    pallas_call x1, Pallas kernels, adjacency(): pl.pallas_call(lambda *refs: counts_kernel(half, panels, *refs), grid=(ha...  27.4 us
    pallas_call x1, Pallas kernels, finish(): pl.pallas_call(lambda *refs: finish_kernel(count, *refs), out_shape=tuple...  2.87 us

profile of v11, /device:TPU:1, one launch (start us, length us, event | category | flops | bytes accessed | tf_op | source)
XLA Modules:
  0.0 134.4 jit_solution(4015716145537760014)
XLA Ops:
  1.3 27.4 %counts.1 = (bf16[2,1024,3072]{2,1,0:T(8,128)(2,1)}, f32[2,8,1024]{2,1,0:T(8,128)}) custom-call(s32[1]{0:T(128)S(6)} %copy.21.refs_0_, s32[128,128]{1,0:T(8,128)} %bitcast.17, s32[128,128]{1,0:T(8,128)} %bitcast.18), custom_call_target="tpu_custom_call" | custom-call | flops 60000000 | bytes 16777216 | tf_op jit(solution)/shard_map/counts/pallas_call | solution.py:163
  28.7 102.6 %train_step.1 = (f32[1,2048]{1,0:T(1,128)}, f32[2048,256]{1,0:T(8,128)}, f32[256,256]{1,0:T(8,128)}, f32[256,256]{1,0:T(8,128)}, f32[512,256]{1,0:T(8,128)}, /*index=5*/f32[1,256]{1,0:T(1,128)}, f32[1,256]{1,0:T(1,128)}) custom-call(bf16[2048,3072]{1,0:T(8,128)(2,1)} %bitcast.29, bf16[2048,256]{1,0:T(8,128)(2,1)} %feat_in.1, ...), custom_call_target="tpu_custom_call" | custom-call | flops 30000001024 | bytes 25165824 | tf_op jit(solution)/shard_map/train_step/pallas_call | solution.py:781
  131.3 2.9 %finish.1 = (f32[2048,256]{1,0:T(8,128)}, f32[256,256]{1,0:T(8,128)}, f32[256,256]{1,0:T(8,128)}, f32[512,256]{1,0:T(8,128)}, f32[1,256]{1,0:T(1,128)}, /*index=5*/f32[1,256]{1,0:T(1,128)}, f32[1,2048]{1,0:T(1,128)}) custom-call(f32[2048,256]{1,0:T(8,128)} %get-tuple-element.25.refs_0_, f32[256,256]{1,0:T(8,128)} %get-tuple-element.26.refs_1_, ...), custom_call_target="tpu_custom_call" | custom-call | tf_op jit(solution)/shard_map/finish/pallas_call | solution.py:757

commit v12 on v11

--- a/solution.py
+++ b/solution.py
@@ -10,6 +10,7 @@
 GROUP = 4
 STRIDE = LANES // GROUP
 TILE = 256
+STRIP = 128
 WIDE = 512
 TALL = 1024
 LOGICAL = pl.DeviceIdType.LOGICAL
@@ -140,10 +141,10 @@
 
         lax.fori_loop(0, chunks // 2, two, 0)
 
-    first = step * TILE
-    total = jnp.zeros((TILE, LANES), jnp.int32)
+    first = step * STRIP
+    total = jnp.zeros((STRIP, LANES), jnp.int32)
     for p in range(panels):
-        part = pl.ds(pl.multiple_of(p * half + first, TILE), TILE)
+        part = pl.ds(pl.multiple_of(p * half + first, STRIP), STRIP)
         word = even[part, :] + odd[part, :]
         total = total + word
         cols = slice(p * LANES, (p + 1) * LANES)
@@ -151,7 +152,7 @@
             adj_ref[h, :, cols] = count.astype(jnp.float32).astype(jnp.bfloat16)
     for h, count in enumerate((jnp.bitwise_and(total, 0xFFFF), jnp.right_shift(total, 16))):
         degree = jnp.sum(count.astype(jnp.float32), axis=1, keepdims=True)
-        wide = jnp.broadcast_to(jnp.maximum(degree, 1.0), (TILE, LANES))
+        wide = jnp.broadcast_to(jnp.maximum(degree, 1.0), (STRIP, LANES))
         degt_ref[h] = jnp.transpose(wide)[:8]
 
 
@@ -162,15 +163,15 @@
     grid_shape = (chunks, LANES)
     adj, degt = pl.pallas_call(
         lambda *refs: counts_kernel(half, panels, *refs),
-        grid=(half // TILE,),
+        grid=(half // STRIP,),
         out_shape=(
             jax.ShapeDtypeStruct((2, half, table_rows), jnp.bfloat16),
             jax.ShapeDtypeStruct((2, 8, half), jnp.float32),
         ),
         in_specs=[SMEM] + [pl.BlockSpec(grid_shape, lambda i: (0, 0))] * 2,
         out_specs=(
-            pl.BlockSpec((2, TILE, table_rows), lambda i: (0, i, 0)),
-            pl.BlockSpec((2, 8, TILE), lambda i: (0, 0, i)),
+            pl.BlockSpec((2, STRIP, table_rows), lambda i: (0, i, 0)),
+            pl.BlockSpec((2, 8, STRIP), lambda i: (0, 0, i)),
         ),
         scratch_shapes=[
             pltpu.VMEM((half * panels + GROUP, LANES), jnp.int32),

time: 134 us -> 135 us (level)
  no operation moved by 1% of the time
where the time goes in v12:
time: 135 us; the launch traced here: 134 us
  Pallas kernels  133 us (99%)
  between operations  1.46 us (1%)
    pallas_call x1, Pallas kernels, train_step(): pl.pallas_call(step_kernel, out_shape=(jax.ShapeDtypeStruct((1, pairs), j...  102 us
    pallas_call x1, Pallas kernels, adjacency(): pl.pallas_call(lambda *refs: counts_kernel(half, panels, *refs), grid=(ha...  28 us
    pallas_call x1, Pallas kernels, finish(): pl.pallas_call(lambda *refs: finish_kernel(count, *refs), out_shape=tuple...  2.87 us

profile of v12, /device:TPU:1, one launch (start us, length us, event | category | flops | bytes accessed | tf_op | source)
XLA Modules:
  0.0 134.5 jit_solution(9568521329151326438)
XLA Ops:
  1.3 28.0 %counts.1 = (bf16[2,1024,3072]{2,1,0:T(8,128)(2,1)}, f32[2,8,1024]{2,1,0:T(8,128)}) custom-call(s32[1]{0:T(128)S(6)} %copy.21.refs_0_, s32[128,128]{1,0:T(8,128)} %bitcast.17, s32[128,128]{1,0:T(8,128)} %bitcast.18), custom_call_target="tpu_custom_call" | custom-call | flops 60000000 | bytes 16777216 | tf_op jit(solution)/shard_map/counts/pallas_call | solution.py:164
  29.3 102.2 %train_step.1 = (f32[1,2048]{1,0:T(1,128)}, f32[2048,256]{1,0:T(8,128)}, f32[256,256]{1,0:T(8,128)}, f32[256,256]{1,0:T(8,128)}, f32[512,256]{1,0:T(8,128)}, /*index=5*/f32[1,256]{1,0:T(1,128)}, f32[1,256]{1,0:T(1,128)}) custom-call(bf16[2048,3072]{1,0:T(8,128)(2,1)} %bitcast.29, bf16[2048,256]{1,0:T(8,128)(2,1)} %feat_in.1, ...), custom_call_target="tpu_custom_call" | custom-call | flops 30000001024 | bytes 25165824 | tf_op jit(solution)/shard_map/train_step/pallas_call | solution.py:782
  131.4 2.9 %finish.1 = (f32[2048,256]{1,0:T(8,128)}, f32[256,256]{1,0:T(8,128)}, f32[256,256]{1,0:T(8,128)}, f32[512,256]{1,0:T(8,128)}, f32[1,256]{1,0:T(1,128)}, /*index=5*/f32[1,256]{1,0:T(1,128)}, f32[1,2048]{1,0:T(1,128)}) custom-call(f32[2048,256]{1,0:T(8,128)} %get-tuple-element.25.refs_0_, f32[256,256]{1,0:T(8,128)} %get-tuple-element.26.refs_1_, ...), custom_call_target="tpu_custom_call" | custom-call | tf_op jit(solution)/shard_map/finish/pallas_call | solution.py:758

commit v13 on v11

--- a/solution.py
+++ b/solution.py
@@ -487,7 +487,7 @@
         )
         return carry
 
-    lax.fori_loop(0, node_rows // TALL, encode, 0)
+    lax.fori_loop(0, node_rows // TALL, encode, 0, unroll=2)
 
     def half_at(n):
         k, sub = n // 2, lax.rem(n, 2)
@@ -553,7 +553,7 @@
         pgr_s[at, :] = dot_nt(delta_b, wh_ref[width:, :]).astype(jnp.bfloat16)
         return carry
 
-    lax.fori_loop(0, pairs // TALL, forward, 0)
+    lax.fori_loop(0, pairs // TALL, forward, 0, unroll=2)
     ends_row = ends_ref[...]
 
     def collect(n):

time: 134 us -> 134 us (level)
  no operation moved by 1% of the time
where the time goes in v13:
time: 134 us; the launch traced here: 133 us
  Pallas kernels  132 us (99%)
  between operations  1.46 us (1%)
    pallas_call x1, Pallas kernels, train_step(): pl.pallas_call(step_kernel, out_shape=(jax.ShapeDtypeStruct((1, pairs), j...  101 us
    pallas_call x1, Pallas kernels, adjacency(): pl.pallas_call(lambda *refs: counts_kernel(half, panels, *refs), grid=(ha...  27.4 us
    pallas_call x1, Pallas kernels, finish(): pl.pallas_call(lambda *refs: finish_kernel(count, *refs), out_shape=tuple...  2.87 us

profile of v13, /device:TPU:1, one launch (start us, length us, event | category | flops | bytes accessed | tf_op | source)
XLA Modules:
  0.0 133.3 jit_solution(6871588552454917813)
XLA Ops:
  1.3 27.4 %counts.1 = (bf16[2,1024,3072]{2,1,0:T(8,128)(2,1)}, f32[2,8,1024]{2,1,0:T(8,128)}) custom-call(s32[1]{0:T(128)S(6)} %copy.21.refs_0_, s32[128,128]{1,0:T(8,128)} %bitcast.17, s32[128,128]{1,0:T(8,128)} %bitcast.18), custom_call_target="tpu_custom_call" | custom-call | flops 60000000 | bytes 16777216 | tf_op jit(solution)/shard_map/counts/pallas_call | solution.py:163
  28.7 101.5 %train_step.1 = (f32[1,2048]{1,0:T(1,128)}, f32[2048,256]{1,0:T(8,128)}, f32[256,256]{1,0:T(8,128)}, f32[256,256]{1,0:T(8,128)}, f32[512,256]{1,0:T(8,128)}, /*index=5*/f32[1,256]{1,0:T(1,128)}, f32[1,256]{1,0:T(1,128)}) custom-call(bf16[2048,3072]{1,0:T(8,128)(2,1)} %bitcast.29, bf16[2048,256]{1,0:T(8,128)(2,1)} %feat_in.1, ...), custom_call_target="tpu_custom_call" | custom-call | flops 30000001024 | bytes 25165824 | tf_op jit(solution)/shard_map/train_step/pallas_call | solution.py:781
  130.2 2.9 %finish.1 = (f32[2048,256]{1,0:T(8,128)}, f32[256,256]{1,0:T(8,128)}, f32[256,256]{1,0:T(8,128)}, f32[512,256]{1,0:T(8,128)}, f32[1,256]{1,0:T(1,128)}, /*index=5*/f32[1,256]{1,0:T(1,128)}, f32[1,2048]{1,0:T(1,128)}) custom-call(f32[2048,256]{1,0:T(8,128)} %get-tuple-element.25.refs_0_, f32[256,256]{1,0:T(8,128)} %get-tuple-element.26.refs_1_, ...), custom_call_target="tpu_custom_call" | custom-call | tf_op jit(solution)/shard_map/finish/pallas_call | solution.py:757
